TPU v7x, 32 devices: a whole 2x2x4 slice. The times are simulated.
32 devices in a mesh: vocab: 8 (over z, y), prompt: 4 (over x, core).
Axes of the slice: x: 2, y: 2, z: 4, core: 2. Of those that a mesh axis runs over, the one named last changes fastest.
Arguments:
- latent_vectors: bfloat16 [4096, 3584], P('prompt')
- unembedding_table: bfloat16 [3584, 81920], P('prompt', 'vocab'), may hold values from -0.3125 to 0.3125
- sampled_ids: int32 [4096], P('prompt'), may hold values from 0 to 81919
- query_of_reply: int32 [1024], P('prompt'), may hold values from 0 to 63, as said below
- critic_ratings: float32 [1024], P('prompt'), may hold values from -5 to 5
- initial_heat: float32 [64], P('prompt'), may hold values from 0.3 to 3
Outputs:
- sampled_logprob: float32 [4096], P('prompt')
- estep_factors: float32 [1024], P('prompt')
- temperature_out: float32 [64], P('prompt')
- weighted_nll: float32 [], replicated
Inputs may be any that keep to these rules, and one draw needn't show every extreme that they name: Response r belongs to prompt query_of_reply[r]; every prompt has exactly 16 responses, all held by the same index of prompt as the prompt itself (the prompts of index i of prompt are i * 16 to i * 16 + 15), in any order there.
All inputs are finite; a program needn't handle non-finite values.
Results may differ from a plain program's by a relative error of at most 0.0003.
Values may be sent and summed in bfloat16 or wider, within the bound.
No kernel may reach another device: no remote copies, remote signals or barrier semaphores. Data moves between devices by JAX's collectives and lax.ppermute only.
A program may use at most 192 MiB of HBM per device.

v0:
```python
import jax
import jax.numpy as jnp
from jax import lax
from jax.sharding import PartitionSpec as P

REPLIES_EACH = 16
WIN = 4
NEWTON = 3
PROMPTS_PER_SHARD = 16


def joined(value, axis, join):
    pieces = jax.tree.map(lambda part: lax.all_gather(part, axis), value)
    head = jax.tree.map(lambda part: part[0], pieces)
    tail = jax.tree.map(lambda part: part[1:], pieces)
    subtotal, _ = lax.scan(lambda subtotal, section: (join(subtotal, section), None), head, tail)
    return subtotal


def combine_pair(first, second):
    largest = jnp.maximum(first[0], second[0])
    grand_accumulated = first[1] * jnp.exp(first[0] - largest) + second[1] * jnp.exp(
        second[0] - largest
    )
    return (largest, grand_accumulated)


def fit_lagrange_heat(critic_ratings, sampled_onehot, initial_heat):
    masked = jnp.where(sampled_onehot > 0.5, critic_ratings[:, None], jnp.float32(-1e30))
    running_maximum = jnp.max(masked, axis=0)
    top_r = jnp.sum(sampled_onehot * running_maximum[None, :], axis=1)
    lagrange_heat = initial_heat
    for step in range(NEWTON):
        heat_of_reply = jnp.sum(sampled_onehot * lagrange_heat[None, :], axis=1)
        expo = jnp.exp((critic_ratings - top_r) / heat_of_reply)
        grand_accumulated = jnp.sum(sampled_onehot * expo[:, None], axis=0)
        share = expo / jnp.sum(sampled_onehot * grand_accumulated[None, :], axis=1)
        average_value = jnp.sum(sampled_onehot * (share * critic_ratings)[:, None], axis=0)
        mean_r = jnp.sum(sampled_onehot * average_value[None, :], axis=1)
        spread_queries = jnp.sum(
            sampled_onehot * (share * (critic_ratings - mean_r) ** 2)[:, None], axis=0
        )
        spread_queries = jnp.maximum(spread_queries, 0.1)
        first_derivative = (
            0.1
            + jnp.log(grand_accumulated / REPLIES_EACH)
            + (running_maximum - average_value) / lagrange_heat
        )
        second_derivative = spread_queries / lagrange_heat**3
        lagrange_heat = jnp.clip(
            lagrange_heat - first_derivative / second_derivative,
            0.5 * lagrange_heat,
            2.0 * lagrange_heat,
        )
    heat_of_reply = jnp.sum(sampled_onehot * lagrange_heat[None, :], axis=1)
    expo = jnp.exp((critic_ratings - top_r) / heat_of_reply)
    grand_accumulated = jnp.sum(sampled_onehot * expo[:, None], axis=0)
    estep_factors = expo / jnp.sum(sampled_onehot * grand_accumulated[None, :], axis=1)
    return (lagrange_heat, estep_factors)


def shards(
    latent_vectors, unembedding_table, sampled_ids, query_of_reply, critic_ratings, initial_heat
):
    columns = unembedding_table.shape[1]
    logits = jnp.dot(
        latent_vectors,
        lax.all_gather(unembedding_table, "prompt", axis=0, tiled=True),
        preferred_element_type=jnp.float32,
    )
    largest = jnp.max(logits, axis=1)
    sum_exp = jnp.sum(jnp.exp(logits - largest[:, None]), axis=1)
    offset = lax.axis_index("vocab") * columns
    local_target = sampled_ids - offset
    positions = lax.broadcasted_iota(jnp.int32, (1, columns), 1)
    chosen_part = jnp.sum(jnp.where(positions == local_target[:, None], logits, 0.0), axis=1)
    whole_max, whole_sum = joined((largest, sum_exp), "vocab", combine_pair)
    chosen = lax.psum(chosen_part, "vocab")
    sampled_logprob = chosen - (whole_max + jnp.log(whole_sum))
    resp_logp = jnp.sum(sampled_logprob.reshape(-1, WIN), axis=1)
    local_group = query_of_reply - lax.axis_index("prompt") * PROMPTS_PER_SHARD
    sampled_onehot = (
        local_group[:, None] == jnp.arange(PROMPTS_PER_SHARD, dtype=jnp.int32)[None, :]
    ).astype(jnp.float32)
    lagrange_heat, estep_factors = fit_lagrange_heat(critic_ratings, sampled_onehot, initial_heat)
    shard_loss_part = jnp.sum(estep_factors * resp_logp)
    total_loss = lax.psum(shard_loss_part, "prompt")
    weighted_nll = -total_loss / (PROMPTS_PER_SHARD * lax.axis_size("prompt") * WIN)
    return (sampled_logprob, estep_factors, lagrange_heat, weighted_nll)


def solution(mesh):
    placed = (
        P("prompt", None),
        P("prompt", "vocab"),
        P("prompt"),
        P("prompt"),
        P("prompt"),
        P("prompt"),
    )
    return jax.shard_map(
        shards,
        mesh=mesh,
        in_specs=placed,
        out_specs=(P("prompt"), P("prompt"), P("prompt"), P()),
        check_vma=False,
    )
```

profile of v0, /device:TPU:0, one launch (start us, length us, event | category | flops | bytes accessed | tf_op | source)
XLA Modules:
  0.0 647.3 jit_solution(10593019584822207506)
XLA Ops:
  7.2 0.0 all-gather.4.cloned.1.call-start
  7.2 0.7 all-gather.4.cloned.1.call-update
  7.9 0.7 broadcast_subtract_fusion.1
  8.6 0.8 select_reduce_fusion.23
  9.4 0.7 select_reduce_fusion.21
  10.1 0.7 divide_exponential_fusion.3
  10.8 0.1 select_reduce_fusion.20
  10.9 0.1 select_reduce_fusion.19
  11.0 0.7 fusion.11
  11.7 0.1 select_reduce_fusion.18
  11.8 0.1 select_reduce_fusion.17
  11.9 0.7 multiply_multiply_fusion.2
  12.6 0.1 select_reduce_fusion.16
  12.7 0.7 maximum_minimum_fusion.2
  13.4 0.1 select_reduce_fusion.15
  13.5 0.1 select_reduce_fusion.14
  13.6 0.1 select_reduce_fusion.13
  13.7 0.7 fusion.10
  14.4 0.1 select_reduce_fusion.12
  14.5 0.1 select_reduce_fusion.11
  14.6 0.7 multiply_multiply_fusion.1
  15.3 0.1 select_reduce_fusion.10
  15.4 0.1 select_reduce_fusion.9
  15.5 0.1 select_reduce_fusion.8
  15.7 0.1 select_reduce_fusion.7
  15.8 0.7 fusion.9
  16.5 0.1 select_reduce_fusion.6
  16.6 0.1 select_reduce_fusion.5
  16.7 0.7 multiply_multiply_fusion
  17.3 0.1 select_reduce_fusion.4
  17.5 0.0 copy-start.5
  17.5 0.1 select_reduce_fusion.3
  17.6 0.0 copy-start.2
  17.6 0.1 select_reduce_fusion.2
  17.7 0.7 select_reduce_fusion.1
  18.4 0.0 copy-done.5
  18.4 0.0 copy-done.2
  18.4 1.3 broadcast_subtract_fusion
  19.7 422.6 %all-gather.4.cloned.1.call-done = bf16[3584,10240]{1,0:T(8,128)(2,1)} async-done(((bf16[896,10240]{1,0:T(8,128)(2,1)}), bf16[3584,10240]{1,0:T(8,128)(2,1)}) %all-gather.4.cloned.1.call-update) | async-done | bytes 73400336 | tf_op jit(solution)/shard_map/all_gather | solution.py:68
  442.3 0.0 copy-start
  442.3 86.5 %fusion.12 = (f32[1024]{0:T(1024)S(1)}, f32[1024,10240]{1,0:T(8,128)}) fusion(bf16[1024,3584]{1,0:T(8,128)(2,1)} %param.8, bf16[3584,10240]{1,0:T(8,128)(2,1)} %all-gather.4.cloned.1.call-done), kind=kOutput, calls=%fused_computation.60 | convolution fusion | flops 75172413440 | bytes 122687488 | tf_op jit(solution)/shard_map/dot_general | solution.py:66
  528.8 0.0 copy-start.3
  528.8 0.0 copy-start.4
  528.8 30.8 %all-gather = f32[8192]{0:T(1024)S(1)} all-gather(f32[1024]{0:T(1024)S(1)} %get-tuple-element.62), channel_id=2, replica_groups=mesh['vocab'=8,'prompt'=4] {'vocab'}, dimensions={0}, use_global_device_ids=true | all-gather | bytes 36864 | tf_op jit(solution)/shard_map/all_gather | solution.py:13
  559.6 0.0 copy-done
  559.6 18.8 %exponential_reduce_fusion = (f32[1024]{0:T(1024)S(1)}, f32[1024]{0:T(1024)S(1)}) fusion(f32[1024,10240]{1,0:T(8,128)} %get-tuple-element.63, f32[1024]{0:T(1024)S(1)} %get-tuple-element.62, s32[1024]{0:T(1024)S(1)} %copy-done), kind=kLoop, calls=%fused_computation.3 | loop fusion | flops 52426752 | bytes 41959424 | tf_op jit(solution)/shard_map/reduce_sum | solution.py:72
  578.4 30.6 %all-gather.1 = f32[8192]{0:T(1024)S(1)} all-gather(f32[1024]{0:T(1024)S(1)} %get-tuple-element.34), channel_id=3, replica_groups=mesh['vocab'=8,'prompt'=4] {'vocab'}, dimensions={0}, use_global_device_ids=true | all-gather | bytes 36864 | tf_op jit(solution)/shard_map/all_gather | solution.py:13
  609.0 21.3 %psum.14 = f32[1024]{0:T(1024)S(1)} all-reduce(f32[1024]{0:T(1024)S(1)} %get-tuple-element.35), channel_id=1, replica_groups=mesh['vocab'=8,'prompt'=4] {'vocab'}, use_global_device_ids=true, to_apply=%region_1.0 | all-reduce | flops 1024 | bytes 8192 | tf_op jit(solution)/shard_map/psum | solution.py:78
  630.3 0.4 while.12
  630.7 0.0 copy-start.1
  630.7 0.1 reshape.37
  630.8 0.1 reduce_sum.258
  631.0 0.0 copy-done.3
  631.0 0.0 copy-done.4
  631.0 1.2 multiply_reduce_fusion
  632.1 6.5 %psum.15 = f32[]{:T(128)} all-reduce(f32[]{:T(128)} %get-tuple-element.50), channel_id=1, replica_groups=mesh['vocab'=8,'prompt'=4] {'prompt'}, use_global_device_ids=true, to_apply=%region_31.32 | all-reduce | flops 1 | bytes 8 | tf_op jit(solution)/shard_map/psum | solution.py:87
  639.3 0.0 copy-done.1
  (26 shorter events, 0.3 us)
Async XLA Ops:
  7.2 435.1 %all-gather.4.cloned.1.call-start = ((), (), s32[]{:S(2)}) async-start(), calls=%async_computation | async-start | bytes 91750400 | tf_op jit(solution)/shard_map/all_gather | solution.py:68
  17.5 0.9 copy-start.5
  17.6 0.8 copy-start.2
  442.3 117.3 %copy-start = (s32[1024]{0:T(1024)S(1)}, s32[1024]{0:T(1024)}, u32[]{:S(2)}) copy-start(s32[1024]{0:T(1024)} %broadcast_subtract_fusion) | copy-start | bytes 12292
  528.8 102.1 %copy-start.3 = (f32[256]{0:T(256)S(1)}, f32[256]{0:T(256)}, u32[]{:S(2)}) copy-start(f32[256]{0:T(256)} %copy-done.2) | copy-start | bytes 3076
  528.8 102.2 %copy-start.4 = (f32[256]{0:T(256)S(1)}, f32[256]{0:T(256)}, u32[]{:S(2)}) copy-start(f32[256]{0:T(256)} %select_reduce_fusion.1) | copy-start | bytes 3076
  630.7 8.6 %copy-start.1 = (f32[1024]{0:T(1024)}, f32[1024]{0:T(1024)S(1)}, u32[]{:S(2)}) copy-start(f32[1024]{0:T(1024)S(1)} %add_subtract_fusion) | copy-start | bytes 12292
Sparse Core Ops, SparseCore 0:
  9.6 432.6 all-gather.3
where the time goes:
time: 648 us; the launch traced here: 647 us
  waiting for transfers between devices  423 us (65%)
  blocking collectives  89.2 us (14%)
  matrix products  86.5 us (13%)
  other arithmetic  31.9 us (5%)
  between operations  15.9 us (2%)
    all_gather x1, waiting for transfers between devices, shards(): lax.all_gather(unembedding_table, 'prompt', axis=0, tiled=True)  423 us
    dot_general x1, matrix products, shards(): jnp.dot(latent_vectors, lax.all_gather(unembedding_table, 'prompt', axis=...  86.5 us
    all_gather x2, blocking collectives, joined(): pieces = jax.tree.map(lambda part: lax.all_gather(part, axis), value)  61.4 us
    psum x1, blocking collectives, shards(): chosen = lax.psum(chosen_part, 'vocab')  21.3 us
    reduce_sum x1, other arithmetic, shards(): sum_exp = jnp.sum(jnp.exp(logits - largest[:, None]), axis=1)  18.8 us
  transfers between devices with their start and end apart: 1, of which 1 were waited for; matrix products, arithmetic and copies ran while one was open for 2% of the time, Pallas kernels for 0%

commit v1 on v0

v1 whole, which is shorter than its diff:
```python
import functools

import jax
import jax.numpy as jnp
from jax import lax
from jax.experimental import pallas as pl
from jax.experimental.pallas import tpu as pltpu
from jax.sharding import PartitionSpec as P


REPLIES_EACH = 16
WIN = 4
NEWTON = 3
PROMPTS_PER_SHARD = 16


LANES = 128
WIDTH = 512
ROWS = 512
CUTS = 4
EARLY = 2
VMEM_LIMIT = 60 * 1024 * 1024


def fit_lagrange_heat(critic_ratings, sampled_onehot, initial_heat):
    masked = jnp.where(sampled_onehot > 0.5, critic_ratings[:, None], jnp.float32(-1e30))
    running_maximum = jnp.max(masked, axis=0)
    top_r = jnp.sum(sampled_onehot * running_maximum[None, :], axis=1)
    lagrange_heat = initial_heat
    for _ in range(NEWTON):
        heat_of_reply = jnp.sum(sampled_onehot * lagrange_heat[None, :], axis=1)
        expo = jnp.exp((critic_ratings - top_r) / heat_of_reply)
        grand_accumulated = jnp.sum(sampled_onehot * expo[:, None], axis=0)
        share = expo / jnp.sum(sampled_onehot * grand_accumulated[None, :], axis=1)
        average_value = jnp.sum(sampled_onehot * (share * critic_ratings)[:, None], axis=0)
        mean_r = jnp.sum(sampled_onehot * average_value[None, :], axis=1)
        spread_queries = jnp.sum(
            sampled_onehot * (share * (critic_ratings - mean_r) ** 2)[:, None], axis=0
        )
        spread_queries = jnp.maximum(spread_queries, 0.1)
        first_derivative = (
            0.1
            + jnp.log(grand_accumulated / REPLIES_EACH)
            + (running_maximum - average_value) / lagrange_heat
        )
        second_derivative = spread_queries / lagrange_heat**3
        lagrange_heat = jnp.clip(
            lagrange_heat - first_derivative / second_derivative,
            0.5 * lagrange_heat,
            2.0 * lagrange_heat,
        )
    heat_of_reply = jnp.sum(sampled_onehot * lagrange_heat[None, :], axis=1)
    expo = jnp.exp((critic_ratings - top_r) / heat_of_reply)
    grand_accumulated = jnp.sum(sampled_onehot * expo[:, None], axis=0)
    estep_factors = expo / jnp.sum(sampled_onehot * grand_accumulated[None, :], axis=1)
    return (lagrange_heat, estep_factors)


def swap(value, axis, distance):
    size = lax.axis_size(axis)
    return lax.ppermute(value, axis, [(i, i ^ distance) for i in range(size)])


def shift(value, axis, distance):
    size = lax.axis_size(axis)
    return lax.ppermute(value, axis, [(i, (i + distance) % size) for i in range(size)])


def after(value, *others):
    return lax.optimization_barrier((value, *others))[0]


def cut_kernel(me_ref, *refs):
    count = len(refs) // 2
    for source, target in zip(refs[:count], refs[count:]):
        target[...] = source[...]


def cut_blocks(me, table, prompts, offset, width):
    rows = table.shape[0]
    quarter = table.shape[1] // prompts
    tall = rows // CUTS

    def piece(distance):
        return pl.BlockSpec(
            (tall, width),
            lambda i, me_ref: (i, ((me_ref[0] ^ distance) * quarter + offset) // width),
        )

    return pl.pallas_call(
        cut_kernel,
        grid_spec=pltpu.PrefetchScalarGridSpec(
            num_scalar_prefetch=1,
            grid=(CUTS,),
            in_specs=[piece(d) for d in range(1, prompts)],
            out_specs=[pl.BlockSpec((tall, width), lambda i, me_ref: (i, 0))] * (prompts - 1),
        ),
        out_shape=[jax.ShapeDtypeStruct((rows, width), table.dtype)] * (prompts - 1),
        cost_estimate=pl.CostEstimate(
            flops=rows * width, bytes_accessed=12 * rows * width, transcendentals=0
        ),
        name="cut",
    )(me, *([table] * (prompts - 1)))


def chunk_kernel(cfg, me_ref, place_ref, *refs):
    refs = list(refs)
    take = lambda count: [refs.pop(0) for _ in range(count)]
    distances, offset, quarter = cfg["distances"], cfg["offset"], cfg["quarter"]
    pieces = take(len(distances))
    tokens = take(cfg["tokens"])
    partial_ref = take(1)[0] if cfg["partial"] else None
    ids_ref = take(1)[0] if cfg["finish"] else None
    prior_ref = take(1)[0] if cfg["prior"] else None
    outs = take(cfg["outs"])
    weights, held, piece_sem, token_sem = take(4)
    first, second = take(2) if cfg["finish"] else (None, None)
    stats_ref = take(1)[0] if cfg["prior"] else (outs[0] if cfg["finish"] else None)
    before, before_sem = take(2) if cfg["partial"] else (None, None)

    step = pl.program_id(0)
    steps = cfg["steps"]
    me = me_ref[0]
    depth = pieces[-1].shape[0]
    width = weights.shape[1]
    tall = 2 * ROWS
    whole = len(distances) * depth == tokens[0].shape[1]

    strips = []
    for ref in tokens:
        high = min(ref.shape[0], tall)
        strips += [(ref, row, high) for row in range(0, ref.shape[0], high)]

    def copies(which):
        slot = which % 2
        found = []
        reached = 0
        start = which * tall
        for ref, row, high in strips:
            if start <= reached < start + tall:
                at = pl.ds(reached - start, high)
                if whole:
                    found.append((ref.at[pl.ds(row, high), :], held.at[slot, at, :]))
                else:
                    for index, distance in enumerate(distances):
                        owner = pl.multiple_of(lax.bitwise_xor(me, distance) * depth, depth)
                        found.append(
                            (
                                ref.at[pl.ds(row, high), pl.ds(owner, depth)],
                                held.at[slot, at, pl.ds(index * depth, depth)],
                            )
                        )
            reached += high
        made = [
            pltpu.make_async_copy(source, target, token_sem.at[slot, index])
            for index, (source, target) in enumerate(found)
        ]
        if partial_ref is not None:
            made.append(
                pltpu.make_async_copy(
                    partial_ref.at[pl.ds(start, tall), :], before.at[slot], before_sem.at[slot]
                )
            )
        return made

    def piece_copy(index):
        distance = distances[index]
        owner = lax.bitwise_xor(me, distance) if whole else index
        row = owner * depth
        target = weights.at[pl.ds(pl.multiple_of(row, depth) if whole else row, depth), :]
        source = pieces[index]
        if distance == 0:
            column = pl.multiple_of(me * quarter + offset, LANES)
            source = source.at[:, pl.ds(column, width)]
        return pltpu.make_async_copy(source, target, piece_sem.at[index])

    def finish(acc, tile):
        lane = lax.broadcasted_iota(jnp.int32, (LANES, LANES), 1)
        for part in range(ROWS // LANES):
            row = place_ref[tile * (ROWS // LANES) + part]
            logits = acc[part * LANES : (part + 1) * LANES, :]
            ids = ids_ref[pl.ds(pl.multiple_of(row * LANES, LANES), LANES), :]
            largest = jnp.max(logits, axis=1, keepdims=True)
            total = jnp.sum(jnp.exp(logits - largest), axis=1, keepdims=True)
            picked = jnp.zeros((LANES, LANES), jnp.float32)
            for block in range(width // LANES):
                hit = ids == lane + (offset + block * LANES)
                picked += jnp.where(hit, logits[:, block * LANES : (block + 1) * LANES], 0.0)
            chosen = jnp.sum(picked, axis=1, keepdims=True)
            packed = jnp.where(lane == 0, largest, jnp.where(lane == 1, total, chosen)).T
            for kind in range(3):
                stats_ref[kind, pl.ds(row, 1), :] = packed[kind : kind + 1, :]

    def product(slot, low):
        value = jnp.dot(
            held[slot, low : low + ROWS, :], weights[...], preferred_element_type=jnp.float32
        )
        return value if before is None else value + before[slot, low : low + ROWS, :]

    @pl.when(step == 0)
    def _():
        for copy in copies(0):
            copy.start()
        for index in range(len(distances)):
            piece_copy(index).start()
        if second is not None:
            second[...] = jnp.zeros_like(second)
        for index in range(len(distances)):
            piece_copy(index).wait()

    for which in range(steps):

        @pl.when(step == which)
        def _():
            if which + 1 < steps:
                for copy in copies(which + 1):
                    copy.start()
            for copy in copies(which):
                copy.wait()

    slot = lax.rem(step, 2)
    if not cfg["finish"]:
        outs[0][0:ROWS, :] = product(slot, 0)
        outs[0][ROWS:tall, :] = product(slot, ROWS)
        return

    first[...] = product(slot, 0)
    finish(second, jnp.maximum(2 * step - 1, 0))
    second[...] = product(slot, ROWS)
    finish(first, 2 * step)

    @pl.when(step == steps - 1)
    def _():
        finish(second, 2 * step + 1)
        if prior_ref is not None:
            each = prior_ref.shape[1] // len(outs)
            for index, out in enumerate(outs):
                rows = slice(index * each, (index + 1) * each)
                largest = jnp.maximum(stats_ref[0, rows, :], prior_ref[0, rows, :])
                out[0] = largest
                out[1] = stats_ref[1, rows, :] * jnp.exp(
                    stats_ref[0, rows, :] - largest
                ) + prior_ref[1, rows, :] * jnp.exp(prior_ref[0, rows, :] - largest)
                out[2] = stats_ref[2, rows, :] + prior_ref[2, rows, :]


def chunk_call(
    me, place, pieces, distances, tokens, quarter, offset, width, ids=None, partial=None,
    prior=None, parts=1
):
    count = sum(part.shape[0] for part in tokens)
    depth = pieces[-1].shape[0]
    inner = depth * len(distances)
    finish = ids is not None
    tall = 2 * ROWS
    steps = count // tall
    rows = count // LANES
    anywhere = pl.BlockSpec(memory_space=pl.ANY)
    whole = lambda shape: pl.BlockSpec(shape, lambda i, *_: (0,) * len(shape))
    operands = [*pieces, *tokens]
    in_specs = [anywhere] * len(operands)
    most = max(1, tall // min(part.shape[0] for part in tokens))
    scratch = [
        pltpu.VMEM((inner, width), tokens[0].dtype),
        pltpu.VMEM((2, tall, inner), tokens[0].dtype),
        pltpu.SemaphoreType.DMA((len(distances),)),
        pltpu.SemaphoreType.DMA((2, most * len(distances))),
    ]
    if partial is not None:
        operands.append(partial)
        in_specs.append(anywhere)
    if finish:
        operands.append(ids)
        in_specs.append(whole(ids.shape))
        scratch += [pltpu.VMEM((ROWS, width), jnp.float32)] * 2
    if prior is not None:
        operands.append(prior)
        in_specs.append(whole(prior.shape))
        scratch.append(pltpu.VMEM(prior.shape, jnp.float32))
        shape = (3, rows // parts, LANES)
        out_shape = [jax.ShapeDtypeStruct(shape, jnp.float32)] * parts
        out_specs = [whole(shape)] * parts
    elif finish:
        out_shape = [jax.ShapeDtypeStruct((3, rows, LANES), jnp.float32)]
        out_specs = [whole((3, rows, LANES))]
    else:
        out_shape = [jax.ShapeDtypeStruct((count, width), jnp.float32)]
        out_specs = [pl.BlockSpec((tall, width), lambda i, *_: (i, 0))]
    if partial is not None:
        scratch += [pltpu.VMEM((2, tall, width), jnp.float32), pltpu.SemaphoreType.DMA((2,))]
    cfg = dict(
        distances=distances,
        offset=offset,
        quarter=quarter,
        tokens=len(tokens),
        partial=partial is not None,
        finish=finish,
        prior=prior is not None,
        outs=len(out_shape),
        steps=steps,
    )
    return pl.pallas_call(
        functools.partial(chunk_kernel, cfg),
        grid_spec=pltpu.PrefetchScalarGridSpec(
            num_scalar_prefetch=2,
            grid=(steps,),
            in_specs=in_specs,
            out_specs=out_specs,
            scratch_shapes=scratch,
        ),
        out_shape=out_shape,
        compiler_params=pltpu.CompilerParams(
            dimension_semantics=("arbitrary",), vmem_limit_bytes=VMEM_LIMIT
        ),
        cost_estimate=pl.CostEstimate(
            flops=2 * count * inner * width,
            bytes_accessed=2 * inner * (count + width),
            transcendentals=count * width,
        ),
        name="chunk",
    )(me, place, *operands)


def tree(values):
    while len(values) > 1:
        pairs = [a + b for a, b in zip(values[::2], values[1::2])]
        values = pairs + values[2 * len(pairs) :]
    return values[0]


def merge(parts):
    largest = functools.reduce(jnp.maximum, [part[0] for part in parts])
    total = tree([part[1] * jnp.exp(part[0] - largest) for part in parts])
    chosen = tree([part[2] for part in parts])
    return jnp.stack([largest, total, chosen])


def all_pairs(value, axis):
    return [value] + [swap(value, axis, d) for d in range(1, lax.axis_size(axis))]


def exchange_stats(latent_vectors, unembedding_table, sampled_ids):
    prompts = lax.axis_size("prompt")
    vocabs = lax.axis_size("vocab")
    me = lax.axis_index("prompt").astype(jnp.int32)
    shard = lax.axis_index("vocab").astype(jnp.int32)
    each = latent_vectors.shape[0]
    columns = unembedding_table.shape[1]
    quarter = columns // prompts
    half = prompts // 2
    mine = me.reshape(1)
    chunks = quarter // WIDTH
    spans = list(range(prompts))

    strip = each // vocabs
    own = lax.dynamic_slice_in_dim(latent_vectors, shard * strip, strip, 0)
    over = swap(own, "prompt", half)
    partner = swap(latent_vectors, "prompt", 1)
    ids_all = [sampled_ids] + [swap(sampled_ids, "prompt", d) for d in range(1, prompts)]
    local = jnp.concatenate(ids_all) - (shard * columns + me * quarter)
    ids = jnp.broadcast_to(local[:, None], (each * prompts, LANES))

    cut = [
        cut_blocks(mine, unembedding_table, prompts, chunk * WIDTH, WIDTH)
        for chunk in range(chunks)
    ]
    pieces = []
    for blocks in cut:
        sent = [swap(block, "prompt", d + 1) for d, block in enumerate(blocks)]
        pieces.append([unembedding_table] + sent)

    ring = [after(over, *cut[0])]
    remote = []
    for hop in range(vocabs // 2):
        remote += [ring[-1], swap(ring[-1], "vocab", 1)]
        if hop + 1 < vocabs // 2:
            ring.append(shift(ring[-1], "vocab", 2))
    remote_pair = [swap(part, "prompt", 1) for part in remote]

    rows = strip // LANES
    order = []
    for hop in range(vocabs // 2):
        for other in (0, 1):
            origin = lax.rem((shard ^ other) - 2 * hop + vocabs, vocabs)
            order += [origin * rows + part for part in range(rows)]
    order = jnp.stack(order).astype(jnp.int32)
    near = jnp.arange(2 * each // LANES, dtype=jnp.int32)
    far = jnp.concatenate([order, order + each // LANES])
    place = jnp.concatenate([near, far + 2 * each // LANES])

    close, distant = [latent_vectors, partner], remote + remote_pair
    halves = ((near, close, ids[: 2 * each]), (far, distant, ids[2 * each :]))
    both = (place, close + distant, ids)
    early = min(EARLY, chunks - 1)
    jobs = [(chunk, half) for half in (0, 1) for chunk in range(early)]
    jobs += [(chunk, None) for chunk in range(early, chunks - 1)]
    done = {}
    gate = mine
    for chunk, half in jobs:
        where, tokens, part = both if half is None else halves[half]
        done[chunk, half] = chunk_call(
            gate, where, pieces[chunk], spans, tokens, quarter, chunk * WIDTH, WIDTH, ids=part
        )[0]
        gate = after(mine, done[chunk, half])
    prior = [jnp.concatenate([done[chunk, 0], done[chunk, 1]], axis=1) for chunk in range(early)]
    prior = merge(prior + [done[chunk, None] for chunk in range(early, chunks - 1)])
    offset = (chunks - 1) * WIDTH
    partial = chunk_call(
        gate, place, pieces[-1][: prompts - 1], spans[: prompts - 1], close + distant, quarter,
        offset, WIDTH,
    )[0]
    blocks = chunk_call(
        mine, place, pieces[-1][prompts - 1 :], spans[prompts - 1 :], close + distant, quarter,
        offset, WIDTH, ids=ids, partial=partial, prior=prior, parts=prompts,
    )
    return merge([block if d == 0 else swap(block, "prompt", d) for d, block in enumerate(blocks)])


def gather_stats(latent_vectors, unembedding_table, sampled_ids):
    columns = unembedding_table.shape[1]
    logits = jnp.dot(
        latent_vectors,
        lax.all_gather(unembedding_table, "prompt", axis=0, tiled=True),
        preferred_element_type=jnp.float32,
    )
    largest = jnp.max(logits, axis=1)
    total = jnp.sum(jnp.exp(logits - largest[:, None]), axis=1)
    local = sampled_ids - lax.axis_index("vocab") * columns
    positions = lax.broadcasted_iota(jnp.int32, (1, columns), 1)
    chosen = jnp.sum(jnp.where(positions == local[:, None], logits, 0.0), axis=1)
    return jnp.stack([largest, total, chosen]).reshape(3, -1, LANES)


def over_vocab(stats):
    size = lax.axis_size("vocab")
    if size <= 8:
        return merge(all_pairs(stats, "vocab"))
    distance = 1
    while distance < size:
        stats = merge([stats, swap(stats, "vocab", distance)])
        distance *= 2
    return stats


def shards(
    latent_vectors, unembedding_table, sampled_ids, query_of_reply, critic_ratings, initial_heat
):
    prompts = lax.axis_size("prompt")
    vocabs = lax.axis_size("vocab")
    each, columns = latent_vectors.shape[0], unembedding_table.shape[1]
    local_group = query_of_reply - lax.axis_index("prompt") * PROMPTS_PER_SHARD
    sampled_onehot = (
        local_group[:, None] == jnp.arange(PROMPTS_PER_SHARD, dtype=jnp.int32)[None, :]
    ).astype(jnp.float32)
    lagrange_heat, estep_factors = fit_lagrange_heat(critic_ratings, sampled_onehot, initial_heat)

    fits = (
        prompts == 4
        and vocabs % 2 == 0
        and columns % (prompts * WIDTH) == 0
        and columns > prompts * WIDTH
        and each % (2 * ROWS) == 0
        and each % (vocabs * LANES) == 0
    )
    partial = (exchange_stats if fits else gather_stats)(
        latent_vectors, unembedding_table, sampled_ids
    )
    whole_max, whole_sum, chosen = over_vocab(partial)
    sampled_logprob = chosen - (whole_max + jnp.log(whole_sum))
    spread_factors = jnp.repeat(estep_factors, WIN).reshape(sampled_logprob.shape)
    loss_part = jnp.sum(spread_factors * sampled_logprob)
    total_loss = tree(all_pairs(loss_part.reshape(1), "prompt"))[0]
    weighted_nll = -total_loss / (PROMPTS_PER_SHARD * prompts * WIN)
    return (sampled_logprob.reshape(-1), estep_factors, lagrange_heat, weighted_nll)


def solution(mesh):
    placed = (
        P("prompt", None),
        P("prompt", "vocab"),
        P("prompt"),
        P("prompt"),
        P("prompt"),
        P("prompt"),
    )
    return jax.shard_map(
        shards,
        mesh=mesh,
        in_specs=placed,
        out_specs=(P("prompt"), P("prompt"), P("prompt"), P()),
        check_vma=False,
    )
```

time: 648 us -> 384 us (0.59)
  waiting for transfers between devices: 423 us -> 144 us
  Pallas kernels: 0 us -> 165 us
  blocking collectives: 89.2 us -> 0 us
  matrix products: 86.5 us -> 0 us
  starting transfers between devices: 0.04 us -> 45.2 us
  other arithmetic: 31.9 us -> 12.4 us
  between operations: 15.9 us -> 4.75 us
  local copies, waits for them, and re-layouts: 0.26 us -> 11.1 us
    all_gather x1 -> x0, waiting for transfers between devices: 423 us -> none  [shards(): lax.all_gather(unembedding_table, 'prompt', axis=0, tiled=True)]
    pallas_call x0 -> x13, Pallas kernels: none -> 165 us  [the longest x8 144 us: chunk_call(): pl.pallas_call(functools.partial(chunk_kernel, cfg), grid_spec=pltpu.Pref...]
    ppermute x0 -> x48, waiting for transfers between devices: none -> 144 us  [the longest x45 142 us: swap(): return lax.ppermute(value, axis, [(i, i ^ distance) for i in range(size)])]
    dot_general x1 -> x0, matrix products: 86.5 us -> none  [shards(): jnp.dot(latent_vectors, lax.all_gather(unembedding_table, 'prompt', axis=...]
    all_gather x2 -> x0, blocking collectives: 61.4 us -> none  [joined(): pieces = jax.tree.map(lambda part: lax.all_gather(part, axis), value)]
    ppermute x0 -> x48, starting transfers between devices: none -> 45.2 us  [the longest x45 40.2 us: swap(): return lax.ppermute(value, axis, [(i, i ^ distance) for i in range(size)])]
    psum x2 -> x0, blocking collectives: 27.8 us -> none  [the longest x1 21.3 us: shards(): chosen = lax.psum(chosen_part, 'vocab')]
    reduce_sum x3 -> x1, other arithmetic: 20 us -> 0.63 us  [shards(): loss_part = jnp.sum(spread_factors * sampled_logprob)]
  transfers between devices with their start and end apart: 1 -> 48, of which waited for: 1 -> 16; matrix products, arithmetic and copies ran while one was open for 2% -> 5% of each run, Pallas kernels for 0% -> 40%
where the time goes in v1:
time: 384 us; the launch traced here: 382 us
  Pallas kernels  165 us (43%)
  waiting for transfers between devices  144 us (38%)
  starting transfers between devices  45.2 us (12%)
  other arithmetic  12.4 us (3%)
  local copies, waits for them, and re-layouts  11.1 us (3%)
  between operations  4.75 us (1%)
    pallas_call x8, Pallas kernels, chunk_call(): pl.pallas_call(functools.partial(chunk_kernel, cfg), grid_spec=pltpu.Pref...  144 us
    ppermute x45, waiting for transfers between devices, swap(): return lax.ppermute(value, axis, [(i, i ^ distance) for i in range(size)])  142 us
    ppermute x45, starting transfers between devices, swap(): return lax.ppermute(value, axis, [(i, i ^ distance) for i in range(size)])  40.2 us
    pallas_call x5, Pallas kernels, cut_blocks(): pl.pallas_call(cut_kernel, grid_spec=pltpu.PrefetchScalarGridSpec(num_sca...  20.8 us
  transfers between devices with their start and end apart: 48, of which 16 were waited for; matrix products, arithmetic and copies ran while one was open for 5% of the time, Pallas kernels for 40%

profile of v1, /device:TPU:0, one launch (start us, length us, event | category | flops | bytes accessed | tf_op | source)
XLA Modules:
  0.0 382.5 jit_solution(4749712907784806123)
XLA Ops:
  1.3 2.9 collective-permute-start.22
  4.2 1.2 constant_dynamic-slice_fusion
  5.4 1.5 collective-permute-start.2
  7.6 0.8 select_reduce_fusion.22
  8.4 0.7 select_reduce_fusion.20
  10.0 0.7 fusion.55
  10.9 0.7 multiply_multiply_fusion.2
  12.7 0.7 fusion.54
  13.4 4.1 %cut.6 = (bf16[896,512]{1,0:T(8,128)(2,1)}, bf16[896,512]{1,0:T(8,128)(2,1)}, bf16[896,512]{1,0:T(8,128)(2,1)}) custom-call(s32[1]{0:T(128)} %bitcast.me_ref, bf16[896,10240]{1,0:T(8,128)(2,1)} %refs_0_.23, bf16[896,10240]{1,0:T(8,128)(2,1)} %refs_0_.23, bf16[896,10240]{1,0:T(8,128)(2,1)} %refs_0_.23), custom_call_target="tpu_custom_call" | custom-call | flops 458752 | bytes 5505024 | tf_op jit(solution)/shard_map/cut/pallas_call | solution.py:90
  17.5 10.6 %collective-permute-done.2.refs_4_.refs_6_.refs_5_.refs_3_ = bf16[128,3584]{1,0:T(8,128)(2,1)S(1)} collective-permute-done((bf16[128,3584]{1,0:T(8,128)(2,1)S(1)}, bf16[128,3584]{1,0:T(8,128)(2,1)S(1)}, u32[]{:S(2)}, u32[]{:S(2)}) %collective-permute-start.2) | collective-permute-done | bytes 917536 | tf_op jit(solution)/shard_map/ppermute | solution.py:61
  28.1 1.8 collective-permute-start.19
  30.1 1.8 collective-permute-start.4
  32.0 4.2 %cut.7 = (bf16[896,512]{1,0:T(8,128)(2,1)}, bf16[896,512]{1,0:T(8,128)(2,1)}, bf16[896,512]{1,0:T(8,128)(2,1)}) custom-call(s32[1]{0:T(128)} %bitcast.me_ref, bf16[896,10240]{1,0:T(8,128)(2,1)} %refs_0_.23, bf16[896,10240]{1,0:T(8,128)(2,1)} %refs_0_.23, bf16[896,10240]{1,0:T(8,128)(2,1)} %refs_0_.23), custom_call_target="tpu_custom_call" | custom-call | flops 458752 | bytes 5505024 | tf_op jit(solution)/shard_map/cut/pallas_call | solution.py:90
  36.6 15.1 %collective-permute-done.19.refs_2_ = bf16[896,512]{1,0:T(8,128)(2,1)} collective-permute-done((bf16[896,512]{1,0:T(8,128)(2,1)}, bf16[896,512]{1,0:T(8,128)(2,1)}, u32[]{:S(2)}, u32[]{:S(2)}) %collective-permute-start.19) | collective-permute-done | bytes 917536 | tf_op jit(solution)/shard_map/ppermute | solution.py:61
  51.8 1.7 collective-permute-start.25
  53.5 17.2 %collective-permute-done.20.refs_3_ = bf16[896,512]{1,0:T(8,128)(2,1)} collective-permute-done((bf16[896,512]{1,0:T(8,128)(2,1)}, bf16[896,512]{1,0:T(8,128)(2,1)}, u32[]{:S(2)}, u32[]{:S(2)}) %collective-permute-start.20) | collective-permute-done | bytes 917536 | tf_op jit(solution)/shard_map/ppermute | solution.py:61
  70.7 1.9 collective-permute-start.26
  72.6 1.6 collective-permute-start.6
  74.6 1.6 collective-permute-start.3
  76.2 14.9 %collective-permute-done.25.refs_2_ = bf16[896,512]{1,0:T(8,128)(2,1)} collective-permute-done((bf16[896,512]{1,0:T(8,128)(2,1)}, bf16[896,512]{1,0:T(8,128)(2,1)}, u32[]{:S(2)}, u32[]{:S(2)}) %collective-permute-start.25) | collective-permute-done | bytes 917536 | tf_op jit(solution)/shard_map/ppermute | solution.py:61
  91.1 18.6 %collective-permute-done.26.refs_3_ = bf16[896,512]{1,0:T(8,128)(2,1)} collective-permute-done((bf16[896,512]{1,0:T(8,128)(2,1)}, bf16[896,512]{1,0:T(8,128)(2,1)}, u32[]{:S(2)}, u32[]{:S(2)}) %collective-permute-start.26) | collective-permute-done | bytes 917536 | tf_op jit(solution)/shard_map/ppermute | solution.py:61
  109.7 1.8 collective-permute-start.5
  111.5 1.6 collective-permute-start.8
  113.6 4.1 %cut.8 = (bf16[896,512]{1,0:T(8,128)(2,1)}, bf16[896,512]{1,0:T(8,128)(2,1)}, bf16[896,512]{1,0:T(8,128)(2,1)}) custom-call(s32[1]{0:T(128)} %bitcast.me_ref, bf16[896,10240]{1,0:T(8,128)(2,1)} %refs_0_.23, bf16[896,10240]{1,0:T(8,128)(2,1)} %refs_0_.23, bf16[896,10240]{1,0:T(8,128)(2,1)} %refs_0_.23), custom_call_target="tpu_custom_call" | custom-call | flops 458752 | bytes 5505024 | tf_op jit(solution)/shard_map/cut/pallas_call | solution.py:90
  117.8 4.2 %cut.9 = (bf16[896,512]{1,0:T(8,128)(2,1)}, bf16[896,512]{1,0:T(8,128)(2,1)}, bf16[896,512]{1,0:T(8,128)(2,1)}) custom-call(s32[1]{0:T(128)} %bitcast.me_ref, bf16[896,10240]{1,0:T(8,128)(2,1)} %refs_0_.23, bf16[896,10240]{1,0:T(8,128)(2,1)} %refs_0_.23, bf16[896,10240]{1,0:T(8,128)(2,1)} %refs_0_.23), custom_call_target="tpu_custom_call" | custom-call | flops 458752 | bytes 5505024 | tf_op jit(solution)/shard_map/cut/pallas_call | solution.py:90
  121.9 4.2 %cut.5 = (bf16[896,512]{1,0:T(8,128)(2,1)}, bf16[896,512]{1,0:T(8,128)(2,1)}, bf16[896,512]{1,0:T(8,128)(2,1)}) custom-call(s32[1]{0:T(128)} %bitcast.me_ref, bf16[896,10240]{1,0:T(8,128)(2,1)} %refs_0_.23, bf16[896,10240]{1,0:T(8,128)(2,1)} %refs_0_.23, bf16[896,10240]{1,0:T(8,128)(2,1)} %refs_0_.23), custom_call_target="tpu_custom_call" | custom-call | flops 458752 | bytes 5505024 | tf_op jit(solution)/shard_map/cut/pallas_call | solution.py:90
  127.1 5.3 %collective-permute-done.5.refs_7_.refs_9_.refs_8_.refs_6_ = bf16[128,3584]{1,0:T(8,128)(2,1)} collective-permute-done((bf16[128,3584]{1,0:T(8,128)(2,1)S(1)}, bf16[128,3584]{1,0:T(8,128)(2,1)}, u32[]{:S(2)}, u32[]{:S(2)}) %collective-permute-start.5) | collective-permute-done | bytes 917536 | tf_op jit(solution)/shard_map/ppermute | solution.py:61
  132.4 1.7 collective-permute-start.7
  134.2 1.6 collective-permute-done.8.refs_10_.refs_12_.refs_11_.refs_9_
  136.9 18.8 %collective-permute-done.7.refs_9_.refs_11_.refs_10_.refs_8_ = bf16[128,3584]{1,0:T(8,128)(2,1)} collective-permute-done((bf16[128,3584]{1,0:T(8,128)(2,1)S(1)}, bf16[128,3584]{1,0:T(8,128)(2,1)}, u32[]{:S(2)}, u32[]{:S(2)}) %collective-permute-start.7) | collective-permute-done | bytes 917536 | tf_op jit(solution)/shard_map/ppermute | solution.py:61
  155.8 18.2 %collective-permute-done.9.refs_11_.refs_13_.refs_12_.refs_10_ = bf16[128,3584]{1,0:T(8,128)(2,1)} collective-permute-done((bf16[128,3584]{1,0:T(8,128)(2,1)}, bf16[128,3584]{1,0:T(8,128)(2,1)}, u32[]{:S(2)}, u32[]{:S(2)}) %collective-permute-start.9) | collective-permute-done | bytes 917536 | tf_op jit(solution)/shard_map/ppermute | solution.py:61
  174.5 1.3 broadcast_in_dim.24.refs_6_
  176.3 15.4 %chunk.8 = f32[3,16,128]{2,1,0:T(8,128)} custom-call(s32[1]{0:T(128)} %bitcast.me_ref, s32[16]{0:T(128)} %iota.12.place_ref, bf16[896,10240]{1,0:T(8,128)(2,1)} %refs_0_.23, bf16[896,512]{1,0:T(8,128)(2,1)} %copy-done.6, bf16[896,512]{1,0:T(8,128)(2,1)} %collective-permute-done.19.refs_2_, bf16[896,512]{1,0:T(8,128)(2,1)} %collective-permute-done.20.refs_3_, ...), custom_call_target="tpu_custom_call" | custom-call | flops 7516192768 | bytes 18350080 | tf_op jit(solution)/shard_map/chunk/pallas_call | solution.py:302
  192.2 15.5 %chunk.9 = f32[3,16,128]{2,1,0:T(8,128)} custom-call(s32[1]{0:T(128)} %bitcast.me_ref, s32[16]{0:T(128)} %iota.13.place_ref, bf16[896,10240]{1,0:T(8,128)(2,1)} %refs_0_.23, bf16[896,512]{1,0:T(8,128)(2,1)} %collective-permute-done.24.refs_1_, bf16[896,512]{1,0:T(8,128)(2,1)} %collective-permute-done.25.refs_2_, ...), custom_call_target="tpu_custom_call" | custom-call | flops 7516192768 | bytes 18350080 | tf_op jit(solution)/shard_map/chunk/pallas_call | solution.py:302
  207.9 1.8 collective-permute-start.28
  210.1 1.7 collective-permute-start.31
  211.8 1.3 broadcast_in_dim.25.refs_20_
  213.1 16.0 %chunk.10 = f32[3,16,128]{2,1,0:T(8,128)} custom-call(s32[1]{0:T(128)} %bitcast.me_ref, s32[16]{0:T(128)} %copy-done.17, bf16[896,10240]{1,0:T(8,128)(2,1)} %refs_0_.23, bf16[896,512]{1,0:T(8,128)(2,1)} %copy-done.6, bf16[896,512]{1,0:T(8,128)(2,1)} %collective-permute-done.19.refs_2_, bf16[896,512]{1,0:T(8,128)(2,1)} %collective-permute-done.20.refs_3_, ...), custom_call_target="tpu_custom_call" | custom-call | flops 7516192768 | bytes 18350080 | tf_op jit(solution)/shard_map/chunk/pallas_call | solution.py:302
  229.1 16.2 %chunk.11 = f32[3,16,128]{2,1,0:T(8,128)} custom-call(s32[1]{0:T(128)} %bitcast.me_ref, s32[16]{0:T(128)} %copy-done.17, bf16[896,10240]{1,0:T(8,128)(2,1)} %refs_0_.23, bf16[896,512]{1,0:T(8,128)(2,1)} %collective-permute-done.24.refs_1_, bf16[896,512]{1,0:T(8,128)(2,1)} %collective-permute-done.25.refs_2_, ...), custom_call_target="tpu_custom_call" | custom-call | flops 7516192768 | bytes 18350080 | tf_op jit(solution)/shard_map/chunk/pallas_call | solution.py:302
  245.8 4.4 %collective-permute-done.29.refs_3_ = bf16[896,512]{1,0:T(8,128)(2,1)} collective-permute-done((bf16[896,512]{1,0:T(8,128)(2,1)}, bf16[896,512]{1,0:T(8,128)(2,1)}, u32[]{:S(2)}, u32[]{:S(2)}) %collective-permute-start.29) | collective-permute-done | bytes 917536 | tf_op jit(solution)/shard_map/ppermute | solution.py:61
  250.2 1.4 collective-permute-start.34
  251.5 2.9 broadcast_in_dim.26.refs_22_.refs_20_
  254.4 24.5 %chunk.12 = f32[3,32,128]{2,1,0:T(8,128)} custom-call(s32[1]{0:T(128)} %bitcast.me_ref, s32[32]{0:T(128)} %pad_add_fusion.place_ref, bf16[896,10240]{1,0:T(8,128)(2,1)} %refs_0_.23, bf16[896,512]{1,0:T(8,128)(2,1)} %copy-done.21, bf16[896,512]{1,0:T(8,128)(2,1)} %collective-permute-done.28.refs_2_, bf16[896,512]{1,0:T(8,128)(2,1)} %collective-permute-done.29.refs_3_, ...), custom_call_target="tpu_custom_call" | custom-call | flops 15032385536 | bytes 33030144 | tf_op jit(solution)/shard_map/chunk/pallas_call | solution.py:302
  279.6 9.9 %collective-permute-done.32.refs_3_ = bf16[896,512]{1,0:T(8,128)(2,1)} collective-permute-done((bf16[896,512]{1,0:T(8,128)(2,1)}, bf16[896,512]{1,0:T(8,128)(2,1)}, u32[]{:S(2)}, u32[]{:S(2)}) %collective-permute-start.32) | collective-permute-done | bytes 917536 | tf_op jit(solution)/shard_map/ppermute | solution.py:61
  289.5 24.5 %chunk.13 = f32[3,32,128]{2,1,0:T(8,128)} custom-call(s32[1]{0:T(128)} %bitcast.me_ref, s32[32]{0:T(128)} %pad_add_fusion.place_ref, bf16[896,10240]{1,0:T(8,128)(2,1)} %refs_0_.23, bf16[896,512]{1,0:T(8,128)(2,1)} %collective-permute-done.30.refs_1_, bf16[896,512]{1,0:T(8,128)(2,1)} %collective-permute-done.31.refs_2_, ...), custom_call_target="tpu_custom_call" | custom-call | flops 15032385536 | bytes 33030144 | tf_op jit(solution)/shard_map/chunk/pallas_call | solution.py:302
  314.0 0.8 fusion.3
  315.5 0.9 copy-done.7
  316.4 1.0 copy-done.8
  317.4 19.0 %chunk.14.refs_19_ = f32[4096,512]{1,0:T(8,128)} custom-call(s32[1]{0:T(128)} %bitcast.me_ref, s32[32]{0:T(128)} %pad_add_fusion.place_ref, bf16[896,10240]{1,0:T(8,128)(2,1)} %refs_0_.23, bf16[896,512]{1,0:T(8,128)(2,1)} %copy-done.7, bf16[896,512]{1,0:T(8,128)(2,1)} %copy-done.8, bf16[1024,3584]{1,0:T(8,128)(2,1)} %refs_1_.11, ...), custom_call_target="tpu_custom_call" | custom-call | flops 11274289152 | bytes 24772608 | tf_op jit(solution)/shard_map/chunk/pallas_call | solution.py:302
  336.5 0.9 copy-done.9
  337.4 13.2 %chunk.15 = (f32[3,8,128]{2,1,0:T(8,128)}, f32[3,8,128]{2,1,0:T(8,128)}, f32[3,8,128]{2,1,0:T(8,128)}, f32[3,8,128]{2,1,0:T(8,128)}) custom-call(s32[1]{0:T(128)} %bitcast.me_ref, s32[32]{0:T(128)} %pad_add_fusion.place_ref, bf16[896,512]{1,0:T(8,128)(2,1)} %copy-done.9, bf16[1024,3584]{1,0:T(8,128)(2,1)} %refs_1_.11, ...), custom_call_target="tpu_custom_call" | custom-call | flops 3758096384 | bytes 8257536 | tf_op jit(solution)/shard_map/chunk/pallas_call | solution.py:302
  351.2 1.7 collective-permute-start.36
  353.0 2.1 collective-permute-done.36
  355.1 1.3 collective-permute-done.37
  356.4 0.7 add_add_fusion
  357.1 1.6 collective-permute-start.38
  358.7 1.6 collective-permute-start.39
  360.8 2.6 collective-permute-start.41
  363.4 1.3 collective-permute-start.42
  364.7 3.6 collective-permute-start.43
  368.9 1.3 collective-permute-done.43
  370.2 4.5 %collective-permute-done.44 = f32[3,8,128]{2,1,0:T(8,128)S(1)} collective-permute-done((f32[3,8,128]{2,1,0:T(8,128)S(1)}, f32[3,8,128]{2,1,0:T(8,128)S(1)}, u32[]{:S(2)}, u32[]{:S(2)}) %collective-permute-start.44) | collective-permute-done | bytes 12320 | tf_op jit(solution)/shard_map/ppermute | solution.py:61
  375.9 1.6 collective-permute-start.45
  377.5 1.3 fusion.20
  (151 shorter events, 14.1 us)
Async XLA Ops:
  0.6 173.3 %collective-permute-start.1 = (bf16[1024,3584]{1,0:T(8,128)(2,1)}, bf16[1024,3584]{1,0:T(8,128)(2,1)}, u32[]{:S(2)}, u32[]{:S(2)}) collective-permute-start(bf16[1024,3584]{1,0:T(8,128)(2,1)} %refs_1_.11), channel_id=1, source_target_pairs={{0,1},{1,0},{2,3},{3,2},{4,5},{5,4},{6,7},{7,6},{8,9},{9,8},{10,11... | collective-permute-start | bytes 22020104 | tf_op jit(solution)/shard_map/ppermute | solution.py:61
  1.2 27.0 %collective-permute-start.21 = (s32[1024]{0:T(1024)}, s32[1024]{0:T(1024)S(1)}, u32[]{:S(2)}, u32[]{:S(2)}) collective-permute-start(s32[1024]{0:T(1024)} %param.8), channel_id=1, source_target_pairs={{0,1},{1,0},{2,3},{3,2},{4,5},{5,4},{6,7},{7,6},{8,9},{9,8},{10,11... | collective-permute-start | bytes 12296 | tf_op jit(solution)/shard_map/ppermute | solution.py:61
  1.3 28.7 %collective-permute-start.22 = (s32[1024]{0:T(1024)}, s32[1024]{0:T(1024)S(1)}, u32[]{:S(2)}, u32[]{:S(2)}) collective-permute-start(s32[1024]{0:T(1024)} %param.8), channel_id=1, source_target_pairs={{0,2},{1,3},{2,0},{3,1},{4,6},{5,7},{6,4},{7,5},{8,10},{9,11},{10,... | collective-permute-start | bytes 12296 | tf_op jit(solution)/shard_map/ppermute | solution.py:61
  4.2 25.9 %collective-permute-start.23 = (s32[1024]{0:T(1024)}, s32[1024]{0:T(1024)S(1)}, u32[]{:S(2)}, u32[]{:S(2)}) collective-permute-start(s32[1024]{0:T(1024)} %param.8), channel_id=1, source_target_pairs={{0,3},{1,2},{2,1},{3,0},{4,7},{5,6},{6,5},{7,4},{8,11},{9,10},{10,... | collective-permute-start | bytes 12296 | tf_op jit(solution)/shard_map/ppermute | solution.py:61
  5.4 22.7 %collective-permute-start.2 = (bf16[128,3584]{1,0:T(8,128)(2,1)S(1)}, bf16[128,3584]{1,0:T(8,128)(2,1)S(1)}, u32[]{:S(2)}, u32[]{:S(2)}) collective-permute-start(bf16[128,3584]{1,0:T(8,128)(2,1)S(1)} %constant_dynamic-slice_fusion), channel_id=1, source_target_pairs={{0,2},{1,3},{2,0},{3,1},{4,6},{5,7},{6,4},{7,5},{8,10},{9,11},{10,... | collective-permute-start | bytes 2752520 | tf_op jit(solution)/shard_map/ppermute | solution.py:61
  28.1 62.9 %copy-start = (bf16[128,3584]{1,0:T(8,128)(2,1)}, bf16[128,3584]{1,0:T(8,128)(2,1)S(1)}, u32[]{:S(2)}) copy-start(bf16[128,3584]{1,0:T(8,128)(2,1)S(1)} %collective-permute-done.2.refs_4_.refs_6_.refs_5_.refs_3_) | copy-start | bytes 2752516
  28.1 8.3 %collective-permute-start.18 = (bf16[896,512]{1,0:T(8,128)(2,1)}, bf16[896,512]{1,0:T(8,128)(2,1)S(1)}, u32[]{:S(2)}, u32[]{:S(2)}) collective-permute-start(bf16[896,512]{1,0:T(8,128)(2,1)} %get-tuple-element.31), channel_id=1, source_target_pairs={{0,1},{1,0},{2,3},{3,2},{4,5},{5,4},{6,7},{7,6},{8,9},{9,8},{10,11... | collective-permute-start | bytes 2752520 | tf_op jit(solution)/shard_map/ppermute | solution.py:61
  28.1 23.6 %collective-permute-start.19 = (bf16[896,512]{1,0:T(8,128)(2,1)}, bf16[896,512]{1,0:T(8,128)(2,1)}, u32[]{:S(2)}, u32[]{:S(2)}) collective-permute-start(bf16[896,512]{1,0:T(8,128)(2,1)} %get-tuple-element.32), channel_id=1, source_target_pairs={{0,2},{1,3},{2,0},{3,1},{4,6},{5,7},{6,4},{7,5},{8,10},{9,11},{10,... | collective-permute-start | bytes 2752520 | tf_op jit(solution)/shard_map/ppermute | solution.py:61
  30.0 40.7 %collective-permute-start.20 = (bf16[896,512]{1,0:T(8,128)(2,1)}, bf16[896,512]{1,0:T(8,128)(2,1)}, u32[]{:S(2)}, u32[]{:S(2)}) collective-permute-start(bf16[896,512]{1,0:T(8,128)(2,1)} %get-tuple-element.33), channel_id=1, source_target_pairs={{0,3},{1,2},{2,1},{3,0},{4,7},{5,6},{6,5},{7,4},{8,11},{9,10},{10,... | collective-permute-start | bytes 2752520 | tf_op jit(solution)/shard_map/ppermute | solution.py:61
  30.1 42.5 %collective-permute-start.4 = (bf16[128,3584]{1,0:T(8,128)(2,1)S(1)}, bf16[128,3584]{1,0:T(8,128)(2,1)S(1)}, u32[]{:S(2)}, u32[]{:S(2)}) collective-permute-start(bf16[128,3584]{1,0:T(8,128)(2,1)S(1)} %collective-permute-done.2.refs_4_.refs_6_.refs_5_.refs_3_), channel_id=1, source_target_pairs={{0,8},{4,12},{8,16},{12,20},{16,24},{20,28},{24,0},{28,4},{1,9},{5... | collective-permute-start | bytes 2752520 | tf_op jit(solution)/shard_map/ppermute | solution.py:66
  36.5 36.1 %copy-start.6 = (bf16[896,512]{1,0:T(8,128)(2,1)}, bf16[896,512]{1,0:T(8,128)(2,1)S(1)}, u32[]{:S(2)}) copy-start(bf16[896,512]{1,0:T(8,128)(2,1)S(1)} %collective-permute-done.18.refs_1_) | copy-start | bytes 2752516
  36.5 38.2 %collective-permute-start.24 = (bf16[896,512]{1,0:T(8,128)(2,1)}, bf16[896,512]{1,0:T(8,128)(2,1)}, u32[]{:S(2)}, u32[]{:S(2)}) collective-permute-start(bf16[896,512]{1,0:T(8,128)(2,1)} %get-tuple-element.36), channel_id=1, source_target_pairs={{0,1},{1,0},{2,3},{3,2},{4,5},{5,4},{6,7},{7,6},{8,9},{9,8},{10,11... | collective-permute-start | bytes 2752520 | tf_op jit(solution)/shard_map/ppermute | solution.py:61
  51.8 39.3 %collective-permute-start.25 = (bf16[896,512]{1,0:T(8,128)(2,1)}, bf16[896,512]{1,0:T(8,128)(2,1)}, u32[]{:S(2)}, u32[]{:S(2)}) collective-permute-start(bf16[896,512]{1,0:T(8,128)(2,1)} %get-tuple-element.37), channel_id=1, source_target_pairs={{0,2},{1,3},{2,0},{3,1},{4,6},{5,7},{6,4},{7,5},{8,10},{9,11},{10,... | collective-permute-start | bytes 2752520 | tf_op jit(solution)/shard_map/ppermute | solution.py:61
  70.7 39.0 %collective-permute-start.26 = (bf16[896,512]{1,0:T(8,128)(2,1)}, bf16[896,512]{1,0:T(8,128)(2,1)}, u32[]{:S(2)}, u32[]{:S(2)}) collective-permute-start(bf16[896,512]{1,0:T(8,128)(2,1)} %get-tuple-element.38), channel_id=1, source_target_pairs={{0,3},{1,2},{2,1},{3,0},{4,7},{5,6},{6,5},{7,4},{8,11},{9,10},{10,... | collective-permute-start | bytes 2752520 | tf_op jit(solution)/shard_map/ppermute | solution.py:61
  72.6 54.0 %copy-start.1 = (bf16[128,3584]{1,0:T(8,128)(2,1)}, bf16[128,3584]{1,0:T(8,128)(2,1)S(1)}, u32[]{:S(2)}) copy-start(bf16[128,3584]{1,0:T(8,128)(2,1)S(1)} %collective-permute-done.4.refs_6_.refs_8_.refs_7_.refs_5_) | copy-start | bytes 2752516
  72.6 38.9 %collective-permute-start.6 = (bf16[128,3584]{1,0:T(8,128)(2,1)S(1)}, bf16[128,3584]{1,0:T(8,128)(2,1)S(1)}, u32[]{:S(2)}, u32[]{:S(2)}) collective-permute-start(bf16[128,3584]{1,0:T(8,128)(2,1)S(1)} %collective-permute-done.4.refs_6_.refs_8_.refs_7_.refs_5_), channel_id=1, source_target_pairs={{0,8},{4,12},{8,16},{12,20},{16,24},{20,28},{24,0},{28,4},{1,9},{5... | collective-permute-start | bytes 2752520 | tf_op jit(solution)/shard_map/ppermute | solution.py:66
  74.4 43.4 %copy-start.17 = (s32[16]{0:T(128)}, s32[16]{0:T(128)S(1)}, u32[]{:S(2)}) copy-start(s32[16]{0:T(128)S(1)} %concatenate.34.place_ref) | copy-start | bytes 196
  74.6 51.9 %collective-permute-start.3 = (bf16[128,3584]{1,0:T(8,128)(2,1)S(1)}, bf16[128,3584]{1,0:T(8,128)(2,1)}, u32[]{:S(2)}, u32[]{:S(2)}) collective-permute-start(bf16[128,3584]{1,0:T(8,128)(2,1)S(1)} %collective-permute-done.2.refs_4_.refs_6_.refs_5_.refs_3_), channel_id=1, source_target_pairs={{0,4},{4,0},{8,12},{12,8},{16,20},{20,16},{24,28},{28,24},{1,5},{5... | collective-permute-start | bytes 2752520 | tf_op jit(solution)/shard_map/ppermute | solution.py:61
  91.1 35.6 %collective-permute-start.10 = (bf16[128,3584]{1,0:T(8,128)(2,1)S(1)}, bf16[128,3584]{1,0:T(8,128)(2,1)}, u32[]{:S(2)}, u32[]{:S(2)}) collective-permute-start(bf16[128,3584]{1,0:T(8,128)(2,1)S(1)} %collective-permute-done.2.refs_4_.refs_6_.refs_5_.refs_3_), channel_id=1, source_target_pairs={{0,1},{1,0},{2,3},{3,2},{4,5},{5,4},{6,7},{7,6},{8,9},{9,8},{10,11... | collective-permute-start | bytes 2752520 | tf_op jit(solution)/shard_map/ppermute | solution.py:61
  109.7 22.7 %collective-permute-start.5 = (bf16[128,3584]{1,0:T(8,128)(2,1)S(1)}, bf16[128,3584]{1,0:T(8,128)(2,1)}, u32[]{:S(2)}, u32[]{:S(2)}) collective-permute-start(bf16[128,3584]{1,0:T(8,128)(2,1)S(1)} %collective-permute-done.4.refs_6_.refs_8_.refs_7_.refs_5_), channel_id=1, source_target_pairs={{0,4},{4,0},{8,12},{12,8},{16,20},{20,16},{24,28},{28,24},{1,5},{5... | collective-permute-start | bytes 2752520 | tf_op jit(solution)/shard_map/ppermute | solution.py:61
  111.5 24.9 %copy-start.2 = (bf16[128,3584]{1,0:T(8,128)(2,1)}, bf16[128,3584]{1,0:T(8,128)(2,1)S(1)}, u32[]{:S(2)}) copy-start(bf16[128,3584]{1,0:T(8,128)(2,1)S(1)} %collective-permute-done.6.refs_8_.refs_10_.refs_9_.refs_7_) | copy-start | bytes 2752516
  111.5 24.3 %collective-permute-start.8 = (bf16[128,3584]{1,0:T(8,128)(2,1)S(1)}, bf16[128,3584]{1,0:T(8,128)(2,1)}, u32[]{:S(2)}, u32[]{:S(2)}) collective-permute-start(bf16[128,3584]{1,0:T(8,128)(2,1)S(1)} %collective-permute-done.6.refs_8_.refs_10_.refs_9_.refs_7_), channel_id=1, source_target_pairs={{0,8},{4,12},{8,16},{12,20},{16,24},{20,28},{24,0},{28,4},{1,9},{5... | collective-permute-start | bytes 2752520 | tf_op jit(solution)/shard_map/ppermute | solution.py:66
  121.9 14.3 %copy-start.16 = (s32[1024]{0:T(1024)S(1)}, s32[1024]{0:T(1024)}, u32[]{:S(2)}) copy-start(s32[1024]{0:T(1024)} %param.8) | copy-start | bytes 12292
  126.4 65.2 %copy-start.19 = (f32[16]{0:T(128)}, f32[16]{0:T(128)S(1)}, u32[]{:S(2)}) copy-start(f32[16]{0:T(128)S(1)} %maximum_minimum_fusion) | copy-start | bytes 196
  126.6 9.7 %collective-permute-start.12 = (bf16[128,3584]{1,0:T(8,128)(2,1)S(1)}, bf16[128,3584]{1,0:T(8,128)(2,1)S(1)}, u32[]{:S(2)}, u32[]{:S(2)}) collective-permute-start(bf16[128,3584]{1,0:T(8,128)(2,1)S(1)} %collective-permute-done.4.refs_6_.refs_8_.refs_7_.refs_5_), channel_id=1, source_target_pairs={{0,1},{1,0},{2,3},{3,2},{4,5},{5,4},{6,7},{7,6},{8,9},{9,8},{10,11... | collective-permute-start | bytes 2752520 | tf_op jit(solution)/shard_map/ppermute | solution.py:61
  126.6 9.8 %collective-permute-start.11 = (bf16[128,3584]{1,0:T(8,128)(2,1)}, bf16[128,3584]{1,0:T(8,128)(2,1)S(1)}, u32[]{:S(2)}, u32[]{:S(2)}) collective-permute-start(bf16[128,3584]{1,0:T(8,128)(2,1)} %collective-permute-done.3.refs_5_.refs_7_.refs_6_.refs_4_), channel_id=1, source_target_pairs={{0,1},{1,0},{2,3},{3,2},{4,5},{5,4},{6,7},{7,6},{8,9},{9,8},{10,11... | collective-permute-start | bytes 2752520 | tf_op jit(solution)/shard_map/ppermute | solution.py:61
  132.4 23.3 %collective-permute-start.7 = (bf16[128,3584]{1,0:T(8,128)(2,1)S(1)}, bf16[128,3584]{1,0:T(8,128)(2,1)}, u32[]{:S(2)}, u32[]{:S(2)}) collective-permute-start(bf16[128,3584]{1,0:T(8,128)(2,1)S(1)} %collective-permute-done.6.refs_8_.refs_10_.refs_9_.refs_7_), channel_id=1, source_target_pairs={{0,4},{4,0},{8,12},{12,8},{16,20},{20,16},{24,28},{28,24},{1,5},{5... | collective-permute-start | bytes 2752520 | tf_op jit(solution)/shard_map/ppermute | solution.py:61
  135.7 38.2 %collective-permute-start.9 = (bf16[128,3584]{1,0:T(8,128)(2,1)}, bf16[128,3584]{1,0:T(8,128)(2,1)}, u32[]{:S(2)}, u32[]{:S(2)}) collective-permute-start(bf16[128,3584]{1,0:T(8,128)(2,1)} %collective-permute-done.8.refs_10_.refs_12_.refs_11_.refs_9_), channel_id=1, source_target_pairs={{0,4},{4,0},{8,12},{12,8},{16,20},{20,16},{24,28},{28,24},{1,5},{5... | collective-permute-start | bytes 2752520 | tf_op jit(solution)/shard_map/ppermute | solution.py:61
  136.3 19.4 %copy-start.3 = (bf16[128,3584]{1,0:T(8,128)(2,1)}, bf16[128,3584]{1,0:T(8,128)(2,1)S(1)}, u32[]{:S(2)}) copy-start(bf16[128,3584]{1,0:T(8,128)(2,1)S(1)} %collective-permute-done.12.refs_14_.refs_16_.refs_15_.refs_13_) | copy-start | bytes 2752516
  136.3 71.4 %collective-permute-start.14 = (bf16[128,3584]{1,0:T(8,128)(2,1)S(1)}, bf16[128,3584]{1,0:T(8,128)(2,1)S(1)}, u32[]{:S(2)}, u32[]{:S(2)}) collective-permute-start(bf16[128,3584]{1,0:T(8,128)(2,1)S(1)} %collective-permute-done.6.refs_8_.refs_10_.refs_9_.refs_7_), channel_id=1, source_target_pairs={{0,1},{1,0},{2,3},{3,2},{4,5},{5,4},{6,7},{7,6},{8,9},{9,8},{10,11... | collective-permute-start | bytes 2752520 | tf_op jit(solution)/shard_map/ppermute | solution.py:61
  136.4 55.3 %copy-start.4 = (bf16[128,3584]{1,0:T(8,128)(2,1)}, bf16[128,3584]{1,0:T(8,128)(2,1)S(1)}, u32[]{:S(2)}) copy-start(bf16[128,3584]{1,0:T(8,128)(2,1)S(1)} %collective-permute-done.11.refs_13_.refs_15_.refs_14_.refs_12_) | copy-start | bytes 2752516
  136.4 71.4 %collective-permute-start.13 = (bf16[128,3584]{1,0:T(8,128)(2,1)}, bf16[128,3584]{1,0:T(8,128)(2,1)}, u32[]{:S(2)}, u32[]{:S(2)}) collective-permute-start(bf16[128,3584]{1,0:T(8,128)(2,1)} %collective-permute-done.5.refs_7_.refs_9_.refs_8_.refs_6_), channel_id=1, source_target_pairs={{0,1},{1,0},{2,3},{3,2},{4,5},{5,4},{6,7},{7,6},{8,9},{9,8},{10,11... | collective-permute-start | bytes 2752520 | tf_op jit(solution)/shard_map/ppermute | solution.py:61
  155.7 53.9 %collective-permute-start.16 = (bf16[128,3584]{1,0:T(8,128)(2,1)}, bf16[128,3584]{1,0:T(8,128)(2,1)}, u32[]{:S(2)}, u32[]{:S(2)}) collective-permute-start(bf16[128,3584]{1,0:T(8,128)(2,1)} %collective-permute-done.8.refs_10_.refs_12_.refs_11_.refs_9_), channel_id=1, source_target_pairs={{0,1},{1,0},{2,3},{3,2},{4,5},{5,4},{6,7},{7,6},{8,9},{9,8},{10,11... | collective-permute-start | bytes 2752520 | tf_op jit(solution)/shard_map/ppermute | solution.py:61
  174.0 35.8 %collective-permute-start.15 = (bf16[128,3584]{1,0:T(8,128)(2,1)}, bf16[128,3584]{1,0:T(8,128)(2,1)}, u32[]{:S(2)}, u32[]{:S(2)}) collective-permute-start(bf16[128,3584]{1,0:T(8,128)(2,1)} %collective-permute-done.7.refs_9_.refs_11_.refs_10_.refs_8_), channel_id=1, source_target_pairs={{0,1},{1,0},{2,3},{3,2},{4,5},{5,4},{6,7},{7,6},{8,9},{9,8},{10,11... | collective-permute-start | bytes 2752520 | tf_op jit(solution)/shard_map/ppermute | solution.py:61
  174.0 36.1 %collective-permute-start.17 = (bf16[128,3584]{1,0:T(8,128)(2,1)}, bf16[128,3584]{1,0:T(8,128)(2,1)}, u32[]{:S(2)}, u32[]{:S(2)}) collective-permute-start(bf16[128,3584]{1,0:T(8,128)(2,1)} %collective-permute-done.9.refs_11_.refs_13_.refs_12_.refs_10_), channel_id=1, source_target_pairs={{0,1},{1,0},{2,3},{3,2},{4,5},{5,4},{6,7},{7,6},{8,9},{9,8},{10,11... | collective-permute-start | bytes 2752520 | tf_op jit(solution)/shard_map/ppermute | solution.py:61
  192.2 15.6 %copy-start.20 = (bf16[896,512]{1,0:T(8,128)(2,1)S(1)}, bf16[896,512]{1,0:T(8,128)(2,1)}, u32[]{:S(2)}) copy-start(bf16[896,512]{1,0:T(8,128)(2,1)} %get-tuple-element.43) | copy-start | bytes 2752516
  207.8 37.5 %collective-permute-start.27 = (bf16[896,512]{1,0:T(8,128)(2,1)}, bf16[896,512]{1,0:T(8,128)(2,1)S(1)}, u32[]{:S(2)}, u32[]{:S(2)}) collective-permute-start(bf16[896,512]{1,0:T(8,128)(2,1)} %get-tuple-element.42), channel_id=1, source_target_pairs={{0,1},{1,0},{2,3},{3,2},{4,5},{5,4},{6,7},{7,6},{8,9},{9,8},{10,11... | collective-permute-start | bytes 2752520 | tf_op jit(solution)/shard_map/ppermute | solution.py:61
  207.9 37.5 %collective-permute-start.28 = (bf16[896,512]{1,0:T(8,128)(2,1)S(1)}, bf16[896,512]{1,0:T(8,128)(2,1)}, u32[]{:S(2)}, u32[]{:S(2)}) collective-permute-start(bf16[896,512]{1,0:T(8,128)(2,1)S(1)} %copy-done.20), channel_id=1, source_target_pairs={{0,2},{1,3},{2,0},{3,1},{4,6},{5,7},{6,4},{7,5},{8,10},{9,11},{10,... | collective-permute-start | bytes 2752520 | tf_op jit(solution)/shard_map/ppermute | solution.py:61
  209.7 40.5 %collective-permute-start.29 = (bf16[896,512]{1,0:T(8,128)(2,1)}, bf16[896,512]{1,0:T(8,128)(2,1)}, u32[]{:S(2)}, u32[]{:S(2)}) collective-permute-start(bf16[896,512]{1,0:T(8,128)(2,1)} %get-tuple-element.44), channel_id=1, source_target_pairs={{0,3},{1,2},{2,1},{3,0},{4,7},{5,6},{6,5},{7,4},{8,11},{9,10},{10,... | collective-permute-start | bytes 2752520 | tf_op jit(solution)/shard_map/ppermute | solution.py:61
  209.8 69.2 %collective-permute-start.30 = (bf16[896,512]{1,0:T(8,128)(2,1)}, bf16[896,512]{1,0:T(8,128)(2,1)}, u32[]{:S(2)}, u32[]{:S(2)}) collective-permute-start(bf16[896,512]{1,0:T(8,128)(2,1)} %get-tuple-element.46), channel_id=1, source_target_pairs={{0,1},{1,0},{2,3},{3,2},{4,5},{5,4},{6,7},{7,6},{8,9},{9,8},{10,11... | collective-permute-start | bytes 2752520 | tf_op jit(solution)/shard_map/ppermute | solution.py:61
  210.1 69.5 %collective-permute-start.31 = (bf16[896,512]{1,0:T(8,128)(2,1)}, bf16[896,512]{1,0:T(8,128)(2,1)}, u32[]{:S(2)}, u32[]{:S(2)}) collective-permute-start(bf16[896,512]{1,0:T(8,128)(2,1)} %get-tuple-element.47), channel_id=1, source_target_pairs={{0,2},{1,3},{2,0},{3,1},{4,6},{5,7},{6,4},{7,5},{8,10},{9,11},{10,... | collective-permute-start | bytes 2752520 | tf_op jit(solution)/shard_map/ppermute | solution.py:61
  245.3 44.2 %collective-permute-start.32 = (bf16[896,512]{1,0:T(8,128)(2,1)}, bf16[896,512]{1,0:T(8,128)(2,1)}, u32[]{:S(2)}, u32[]{:S(2)}) collective-permute-start(bf16[896,512]{1,0:T(8,128)(2,1)} %get-tuple-element.48), channel_id=1, source_target_pairs={{0,3},{1,2},{2,1},{3,0},{4,7},{5,6},{6,5},{7,4},{8,11},{9,10},{10,... | collective-permute-start | bytes 2752520 | tf_op jit(solution)/shard_map/ppermute | solution.py:61
  245.4 70.1 %collective-permute-start.33 = (bf16[896,512]{1,0:T(8,128)(2,1)}, bf16[896,512]{1,0:T(8,128)(2,1)S(1)}, u32[]{:S(2)}, u32[]{:S(2)}) collective-permute-start(bf16[896,512]{1,0:T(8,128)(2,1)} %get-tuple-element.50), channel_id=1, source_target_pairs={{0,1},{1,0},{2,3},{3,2},{4,5},{5,4},{6,7},{7,6},{8,9},{9,8},{10,11... | collective-permute-start | bytes 2752520 | tf_op jit(solution)/shard_map/ppermute | solution.py:61
  250.2 65.3 %collective-permute-start.34 = (bf16[896,512]{1,0:T(8,128)(2,1)}, bf16[896,512]{1,0:T(8,128)(2,1)S(1)}, u32[]{:S(2)}, u32[]{:S(2)}) collective-permute-start(bf16[896,512]{1,0:T(8,128)(2,1)} %get-tuple-element.51), channel_id=1, source_target_pairs={{0,2},{1,3},{2,0},{3,1},{4,6},{5,7},{6,4},{7,5},{8,10},{9,11},{10,... | collective-permute-start | bytes 2752520 | tf_op jit(solution)/shard_map/ppermute | solution.py:61
  278.9 35.0 %copy-start.10 = (f32[3,16,128]{2,1,0:T(8,128)S(1)}, f32[3,16,128]{2,1,0:T(8,128)}, u32[]{:S(2)}) copy-start(f32[3,16,128]{2,1,0:T(8,128)} %chunk.8) | copy-start | bytes 73732
  278.9 35.0 %copy-start.11 = (f32[3,16,128]{2,1,0:T(8,128)S(1)}, f32[3,16,128]{2,1,0:T(8,128)}, u32[]{:S(2)}) copy-start(f32[3,16,128]{2,1,0:T(8,128)} %chunk.9) | copy-start | bytes 73732
  279.0 35.0 %copy-start.12 = (f32[3,16,128]{2,1,0:T(8,128)S(1)}, f32[3,16,128]{2,1,0:T(8,128)}, u32[]{:S(2)}) copy-start(f32[3,16,128]{2,1,0:T(8,128)} %chunk.10) | copy-start | bytes 73732
  279.0 35.0 %copy-start.13 = (f32[3,16,128]{2,1,0:T(8,128)S(1)}, f32[3,16,128]{2,1,0:T(8,128)}, u32[]{:S(2)}) copy-start(f32[3,16,128]{2,1,0:T(8,128)} %chunk.11) | copy-start | bytes 73732
  279.0 35.0 %copy-start.15 = (f32[3,32,128]{2,1,0:T(8,128)S(1)}, f32[3,32,128]{2,1,0:T(8,128)}, u32[]{:S(2)}) copy-start(f32[3,32,128]{2,1,0:T(8,128)} %chunk.12) | copy-start | bytes 147460
  279.0 57.5 %collective-permute-start = (bf16[896,512]{1,0:T(8,128)(2,1)}, bf16[896,512]{1,0:T(8,128)(2,1)S(1)}, u32[]{:S(2)}, u32[]{:S(2)}) collective-permute-start(bf16[896,512]{1,0:T(8,128)(2,1)} %get-tuple-element.30), channel_id=1, source_target_pairs={{0,3},{1,2},{2,1},{3,0},{4,7},{5,6},{6,5},{7,4},{8,11},{9,10},{10,... | collective-permute-start | bytes 2752520 | tf_op jit(solution)/shard_map/ppermute | solution.py:61
  350.6 2.4 collective-permute-start.35
  351.2 3.9 %collective-permute-start.36 = (f32[3,8,128]{2,1,0:T(8,128)}, f32[3,8,128]{2,1,0:T(8,128)S(1)}, u32[]{:S(2)}, u32[]{:S(2)}) collective-permute-start(f32[3,8,128]{2,1,0:T(8,128)} %get-tuple-element.54), channel_id=1, source_target_pairs={{0,2},{1,3},{2,0},{3,1},{4,6},{5,7},{6,4},{7,5},{8,10},{9,11},{10,... | collective-permute-start | bytes 36872 | tf_op jit(solution)/shard_map/ppermute | solution.py:61
  353.0 3.4 collective-permute-start.37
  357.1 7.6 %collective-permute-start.38 = (f32[3,8,128]{2,1,0:T(8,128)S(1)}, f32[3,8,128]{2,1,0:T(8,128)S(1)}, u32[]{:S(2)}, u32[]{:S(2)}) collective-permute-start(f32[3,8,128]{2,1,0:T(8,128)S(1)} %pad_maximum_fusion.3), channel_id=1, source_target_pairs={{0,4},{4,0},{8,12},{12,8},{16,20},{20,16},{24,28},{28,24},{1,5},{5... | collective-permute-start | bytes 36872 | tf_op jit(solution)/shard_map/ppermute | solution.py:61
  358.7 9.6 %collective-permute-start.39 = (f32[3,8,128]{2,1,0:T(8,128)S(1)}, f32[3,8,128]{2,1,0:T(8,128)S(1)}, u32[]{:S(2)}, u32[]{:S(2)}) collective-permute-start(f32[3,8,128]{2,1,0:T(8,128)S(1)} %pad_maximum_fusion.3), channel_id=1, source_target_pairs={{0,8},{4,12},{8,0},{12,4},{16,24},{20,28},{24,16},{28,20},{1,9},{5... | collective-permute-start | bytes 36872 | tf_op jit(solution)/shard_map/ppermute | solution.py:61
  360.4 8.4 %collective-permute-start.40 = (f32[3,8,128]{2,1,0:T(8,128)S(1)}, f32[3,8,128]{2,1,0:T(8,128)S(1)}, u32[]{:S(2)}, u32[]{:S(2)}) collective-permute-start(f32[3,8,128]{2,1,0:T(8,128)S(1)} %pad_maximum_fusion.3), channel_id=1, source_target_pairs={{0,12},{4,8},{8,4},{12,0},{16,28},{20,24},{24,20},{28,16},{1,13},{... | collective-permute-start | bytes 36872 | tf_op jit(solution)/shard_map/ppermute | solution.py:61
  360.8 8.0 %collective-permute-start.41 = (f32[3,8,128]{2,1,0:T(8,128)S(1)}, f32[3,8,128]{2,1,0:T(8,128)S(1)}, u32[]{:S(2)}, u32[]{:S(2)}) collective-permute-start(f32[3,8,128]{2,1,0:T(8,128)S(1)} %pad_maximum_fusion.3), channel_id=1, source_target_pairs={{0,16},{4,20},{8,24},{12,28},{16,0},{20,4},{24,8},{28,12},{1,17},{... | collective-permute-start | bytes 36872 | tf_op jit(solution)/shard_map/ppermute | solution.py:61
  363.4 5.5 %collective-permute-start.42 = (f32[3,8,128]{2,1,0:T(8,128)S(1)}, f32[3,8,128]{2,1,0:T(8,128)S(1)}, u32[]{:S(2)}, u32[]{:S(2)}) collective-permute-start(f32[3,8,128]{2,1,0:T(8,128)S(1)} %pad_maximum_fusion.3), channel_id=1, source_target_pairs={{0,20},{4,16},{8,28},{12,24},{16,4},{20,0},{24,12},{28,8},{1,21},{... | collective-permute-start | bytes 36872 | tf_op jit(solution)/shard_map/ppermute | solution.py:61
  364.7 5.5 %collective-permute-start.43 = (f32[3,8,128]{2,1,0:T(8,128)S(1)}, f32[3,8,128]{2,1,0:T(8,128)S(1)}, u32[]{:S(2)}, u32[]{:S(2)}) collective-permute-start(f32[3,8,128]{2,1,0:T(8,128)S(1)} %pad_maximum_fusion.3), channel_id=1, source_target_pairs={{0,24},{4,28},{8,16},{12,20},{16,8},{20,12},{24,0},{28,4},{1,25},{... | collective-permute-start | bytes 36872 | tf_op jit(solution)/shard_map/ppermute | solution.py:61
  368.3 6.4 %collective-permute-start.44 = (f32[3,8,128]{2,1,0:T(8,128)S(1)}, f32[3,8,128]{2,1,0:T(8,128)S(1)}, u32[]{:S(2)}, u32[]{:S(2)}) collective-permute-start(f32[3,8,128]{2,1,0:T(8,128)S(1)} %pad_maximum_fusion.3), channel_id=1, source_target_pairs={{0,28},{4,24},{8,20},{12,16},{16,12},{20,8},{24,4},{28,0},{1,29},{... | collective-permute-start | bytes 36872 | tf_op jit(solution)/shard_map/ppermute | solution.py:61
  368.6 12.7 %copy-start.18 = (f32[256]{0:T(256)}, f32[256]{0:T(256)S(1)}, u32[]{:S(2)}) copy-start(f32[256]{0:T(256)S(1)} %div.75) | copy-start | bytes 3076
  375.4 4.7 %collective-permute-start.46 = (f32[1]{0:T(128)}, f32[1]{0:T(128)}, u32[]{:S(2)}, u32[]{:S(2)}) collective-permute-start(f32[1]{0:T(128)} %bitcast.39), channel_id=1, source_target_pairs={{0,2},{1,3},{2,0},{3,1},{4,6},{5,7},{6,4},{7,5},{8,10},{9,11},{10,... | collective-permute-start | bytes 20 | tf_op jit(solution)/shard_map/ppermute | solution.py:61
  375.9 4.2 %collective-permute-start.47 = (f32[1]{0:T(128)}, f32[1]{0:T(128)}, u32[]{:S(2)}, u32[]{:S(2)}) collective-permute-start(f32[1]{0:T(128)} %bitcast.39), channel_id=1, source_target_pairs={{0,3},{1,2},{2,1},{3,0},{4,7},{5,6},{6,5},{7,4},{8,11},{9,10},{10,... | collective-permute-start | bytes 20 | tf_op jit(solution)/shard_map/ppermute | solution.py:61
  375.9 3.0 collective-permute-start.45
  (6 other events, 21.7 us)

commit v2 on v1

--- a/solution.py
+++ b/solution.py
@@ -16,7 +16,8 @@
 
 LANES = 128
 WIDTH = 512
-ROWS = 512
+ROWS = 256
+SLOTS = 3
 CUTS = 4
 EARLY = 2
 VMEM_LIMIT = 60 * 1024 * 1024
@@ -132,7 +133,7 @@
         strips += [(ref, row, high) for row in range(0, ref.shape[0], high)]
 
     def copies(which):
-        slot = which % 2
+        slot = which % SLOTS
         found = []
         reached = 0
         start = which * tall
@@ -176,15 +177,16 @@
 
     def finish(acc, tile):
         lane = lax.broadcasted_iota(jnp.int32, (LANES, LANES), 1)
+        position = lane.astype(jnp.float32)
         for part in range(ROWS // LANES):
             row = place_ref[tile * (ROWS // LANES) + part]
             logits = acc[part * LANES : (part + 1) * LANES, :]
-            ids = ids_ref[pl.ds(pl.multiple_of(row * LANES, LANES), LANES), :]
+            ids = jnp.broadcast_to(ids_ref[pl.ds(row, 1), :], (LANES, LANES)).T
             largest = jnp.max(logits, axis=1, keepdims=True)
             total = jnp.sum(jnp.exp(logits - largest), axis=1, keepdims=True)
             picked = jnp.zeros((LANES, LANES), jnp.float32)
             for block in range(width // LANES):
-                hit = ids == lane + (offset + block * LANES)
+                hit = ids == position + float(offset + block * LANES)
                 picked += jnp.where(hit, logits[:, block * LANES : (block + 1) * LANES], 0.0)
             chosen = jnp.sum(picked, axis=1, keepdims=True)
             packed = jnp.where(lane == 0, largest, jnp.where(lane == 1, total, chosen)).T
@@ -199,10 +201,11 @@
 
     @pl.when(step == 0)
     def _():
-        for copy in copies(0):
-            copy.start()
         for index in range(len(distances)):
             piece_copy(index).start()
+        for ahead in range(min(SLOTS - 1, steps)):
+            for copy in copies(ahead):
+                copy.start()
         if second is not None:
             second[...] = jnp.zeros_like(second)
         for index in range(len(distances)):
@@ -212,13 +215,13 @@
 
         @pl.when(step == which)
         def _():
-            if which + 1 < steps:
-                for copy in copies(which + 1):
+            if which + SLOTS - 1 < steps:
+                for copy in copies(which + SLOTS - 1):
                     copy.start()
             for copy in copies(which):
                 copy.wait()
 
-    slot = lax.rem(step, 2)
+    slot = lax.rem(step, SLOTS)
     if not cfg["finish"]:
         outs[0][0:ROWS, :] = product(slot, 0)
         outs[0][ROWS:tall, :] = product(slot, ROWS)
@@ -262,9 +265,9 @@
     most = max(1, tall // min(part.shape[0] for part in tokens))
     scratch = [
         pltpu.VMEM((inner, width), tokens[0].dtype),
-        pltpu.VMEM((2, tall, inner), tokens[0].dtype),
+        pltpu.VMEM((SLOTS, tall, inner), tokens[0].dtype),
         pltpu.SemaphoreType.DMA((len(distances),)),
-        pltpu.SemaphoreType.DMA((2, most * len(distances))),
+        pltpu.SemaphoreType.DMA((SLOTS, most * len(distances))),
     ]
     if partial is not None:
         operands.append(partial)
@@ -287,7 +290,7 @@
         out_shape = [jax.ShapeDtypeStruct((count, width), jnp.float32)]
         out_specs = [pl.BlockSpec((tall, width), lambda i, *_: (i, 0))]
     if partial is not None:
-        scratch += [pltpu.VMEM((2, tall, width), jnp.float32), pltpu.SemaphoreType.DMA((2,))]
+        scratch += [pltpu.VMEM((SLOTS, tall, width), jnp.float32), pltpu.SemaphoreType.DMA((SLOTS,))]
     cfg = dict(
         distances=distances,
         offset=offset,
@@ -358,7 +361,7 @@
     partner = swap(latent_vectors, "prompt", 1)
     ids_all = [sampled_ids] + [swap(sampled_ids, "prompt", d) for d in range(1, prompts)]
     local = jnp.concatenate(ids_all) - (shard * columns + me * quarter)
-    ids = jnp.broadcast_to(local[:, None], (each * prompts, LANES))
+    ids = local.astype(jnp.float32).reshape(-1, LANES)
 
     cut = [
         cut_blocks(mine, unembedding_table, prompts, chunk * WIDTH, WIDTH)
@@ -389,7 +392,7 @@
     place = jnp.concatenate([near, far + 2 * each // LANES])
 
     close, distant = [latent_vectors, partner], remote + remote_pair
-    halves = ((near, close, ids[: 2 * each]), (far, distant, ids[2 * each :]))
+    halves = ((near, close, ids[: 2 * each // LANES]), (far, distant, ids[2 * each // LANES :]))
     both = (place, close + distant, ids)
     early = min(EARLY, chunks - 1)
     jobs = [(chunk, half) for half in (0, 1) for chunk in range(early)]
@@ -433,12 +436,13 @@
 
 def over_vocab(stats):
     size = lax.axis_size("vocab")
-    if size <= 8:
-        return merge(all_pairs(stats, "vocab"))
-    distance = 1
-    while distance < size:
-        stats = merge([stats, swap(stats, "vocab", distance)])
-        distance *= 2
+    base = 1
+    while base < size:
+        radix = 2 if base == 1 else min(4, size // base)
+        stats = merge(
+            [stats] + [swap(stats, "vocab", base * digit) for digit in range(1, radix)]
+        )
+        base *= radix
     return stats
 
 

time: 384 us -> 374 us (0.974)
  waiting for transfers between devices: 144 us -> 152 us
  Pallas kernels: 165 us -> 159 us
  starting transfers between devices: 45.2 us -> 40.1 us
  local copies, waits for them, and re-layouts: 11.1 us -> 6.15 us
    ppermute x45 -> x42, waiting for transfers between devices: 142 us -> 150 us  [swap(): return lax.ppermute(value, axis, [(i, i ^ distance) for i in range(size)])]
    pallas_call x8, Pallas kernels: 144 us -> 138 us  [chunk_call(): pl.pallas_call(functools.partial(chunk_kernel, cfg), grid_spec=pltpu.Pref...]
    broadcast_in_dim x3 -> x0, local copies, waits for them, and re-layouts: 5.5 us -> none  [exchange_stats(): ids = jnp.broadcast_to(local[:, None], (each * prompts, LANES))]
    ppermute x45 -> x42, starting transfers between devices: 40.2 us -> 35.1 us  [swap(): return lax.ppermute(value, axis, [(i, i ^ distance) for i in range(size)])]
  transfers between devices with their start and end apart: 48 -> 45, of which waited for: 16 -> 16; matrix products, arithmetic and copies ran while one was open for 5% -> 3% of each run, Pallas kernels for 40% -> 40%
where the time goes in v2:
time: 374 us; the launch traced here: 373 us
  Pallas kernels  159 us (43%)
  waiting for transfers between devices  152 us (41%)
  starting transfers between devices  40.1 us (11%)
  other arithmetic  11.1 us (3%)
  local copies, waits for them, and re-layouts  6.15 us (2%)
  between operations  4.74 us (1%)
    ppermute x42, waiting for transfers between devices, swap(): return lax.ppermute(value, axis, [(i, i ^ distance) for i in range(size)])  150 us
    pallas_call x8, Pallas kernels, chunk_call(): pl.pallas_call(functools.partial(chunk_kernel, cfg), grid_spec=pltpu.Pref...  138 us
    ppermute x42, starting transfers between devices, swap(): return lax.ppermute(value, axis, [(i, i ^ distance) for i in range(size)])  35.1 us
    pallas_call x5, Pallas kernels, cut_blocks(): pl.pallas_call(cut_kernel, grid_spec=pltpu.PrefetchScalarGridSpec(num_sca...  20.8 us
  transfers between devices with their start and end apart: 45, of which 16 were waited for; matrix products, arithmetic and copies ran while one was open for 3% of the time, Pallas kernels for 40%

profile of v2, /device:TPU:0, one launch (start us, length us, event | category | flops | bytes accessed | tf_op | source)
XLA Modules:
  0.0 372.7 jit_solution(13809240664713472385)
XLA Ops:
  1.3 2.9 collective-permute-start.22
  4.2 1.2 constant_dynamic-slice_fusion
  5.4 1.5 collective-permute-start.2
  6.9 0.7 broadcast_subtract_fusion
  7.6 0.8 select_reduce_fusion.22
  8.4 0.7 select_reduce_fusion.20
  9.1 0.7 divide_exponential_fusion.3
  10.0 0.7 fusion.51
  10.9 0.7 multiply_multiply_fusion.2
  11.7 4.2 %cut.6 = (bf16[896,512]{1,0:T(8,128)(2,1)}, bf16[896,512]{1,0:T(8,128)(2,1)}, bf16[896,512]{1,0:T(8,128)(2,1)}) custom-call(s32[1]{0:T(128)} %bitcast.me_ref, bf16[896,10240]{1,0:T(8,128)(2,1)} %refs_0_.23, bf16[896,10240]{1,0:T(8,128)(2,1)} %refs_0_.23, bf16[896,10240]{1,0:T(8,128)(2,1)} %refs_0_.23), custom_call_target="tpu_custom_call" | custom-call | flops 458752 | bytes 5505024 | tf_op jit(solution)/shard_map/cut/pallas_call | solution.py:91
  16.0 12.2 %collective-permute-done.2.refs_4_.refs_6_.refs_5_.refs_3_ = bf16[128,3584]{1,0:T(8,128)(2,1)S(1)} collective-permute-done((bf16[128,3584]{1,0:T(8,128)(2,1)S(1)}, bf16[128,3584]{1,0:T(8,128)(2,1)S(1)}, u32[]{:S(2)}, u32[]{:S(2)}) %collective-permute-start.2) | collective-permute-done | bytes 917536 | tf_op jit(solution)/shard_map/ppermute | solution.py:62
  28.1 1.8 collective-permute-start.19
  30.1 1.8 collective-permute-start.4
  31.9 4.2 %cut.7 = (bf16[896,512]{1,0:T(8,128)(2,1)}, bf16[896,512]{1,0:T(8,128)(2,1)}, bf16[896,512]{1,0:T(8,128)(2,1)}) custom-call(s32[1]{0:T(128)} %bitcast.me_ref, bf16[896,10240]{1,0:T(8,128)(2,1)} %refs_0_.23, bf16[896,10240]{1,0:T(8,128)(2,1)} %refs_0_.23, bf16[896,10240]{1,0:T(8,128)(2,1)} %refs_0_.23), custom_call_target="tpu_custom_call" | custom-call | flops 458752 | bytes 5505024 | tf_op jit(solution)/shard_map/cut/pallas_call | solution.py:91
  36.6 15.1 %collective-permute-done.19.refs_2_ = bf16[896,512]{1,0:T(8,128)(2,1)} collective-permute-done((bf16[896,512]{1,0:T(8,128)(2,1)}, bf16[896,512]{1,0:T(8,128)(2,1)}, u32[]{:S(2)}, u32[]{:S(2)}) %collective-permute-start.19) | collective-permute-done | bytes 917536 | tf_op jit(solution)/shard_map/ppermute | solution.py:62
  51.8 1.7 collective-permute-start.25
  53.5 17.2 %collective-permute-done.20.refs_3_ = bf16[896,512]{1,0:T(8,128)(2,1)} collective-permute-done((bf16[896,512]{1,0:T(8,128)(2,1)}, bf16[896,512]{1,0:T(8,128)(2,1)}, u32[]{:S(2)}, u32[]{:S(2)}) %collective-permute-start.20) | collective-permute-done | bytes 917536 | tf_op jit(solution)/shard_map/ppermute | solution.py:62
  70.7 1.9 collective-permute-start.26
  72.6 1.6 collective-permute-start.6
  74.6 1.6 collective-permute-start.3
  76.2 14.9 %collective-permute-done.25.refs_2_ = bf16[896,512]{1,0:T(8,128)(2,1)} collective-permute-done((bf16[896,512]{1,0:T(8,128)(2,1)}, bf16[896,512]{1,0:T(8,128)(2,1)}, u32[]{:S(2)}, u32[]{:S(2)}) %collective-permute-start.25) | collective-permute-done | bytes 917536 | tf_op jit(solution)/shard_map/ppermute | solution.py:62
  91.1 18.6 %collective-permute-done.26.refs_3_ = bf16[896,512]{1,0:T(8,128)(2,1)} collective-permute-done((bf16[896,512]{1,0:T(8,128)(2,1)}, bf16[896,512]{1,0:T(8,128)(2,1)}, u32[]{:S(2)}, u32[]{:S(2)}) %collective-permute-start.26) | collective-permute-done | bytes 917536 | tf_op jit(solution)/shard_map/ppermute | solution.py:62
  109.7 1.8 collective-permute-start.5
  111.5 1.6 collective-permute-start.8
  114.1 18.3 %collective-permute-done.5.refs_7_.refs_9_.refs_8_.refs_6_ = bf16[128,3584]{1,0:T(8,128)(2,1)} collective-permute-done((bf16[128,3584]{1,0:T(8,128)(2,1)S(1)}, bf16[128,3584]{1,0:T(8,128)(2,1)}, u32[]{:S(2)}, u32[]{:S(2)}) %collective-permute-start.5) | collective-permute-done | bytes 917536 | tf_op jit(solution)/shard_map/ppermute | solution.py:62
  132.4 1.7 collective-permute-start.7
  134.2 1.6 collective-permute-done.8.refs_10_.refs_12_.refs_11_.refs_9_
  136.3 4.1 %cut.8 = (bf16[896,512]{1,0:T(8,128)(2,1)}, bf16[896,512]{1,0:T(8,128)(2,1)}, bf16[896,512]{1,0:T(8,128)(2,1)}) custom-call(s32[1]{0:T(128)} %bitcast.me_ref, bf16[896,10240]{1,0:T(8,128)(2,1)} %refs_0_.23, bf16[896,10240]{1,0:T(8,128)(2,1)} %refs_0_.23, bf16[896,10240]{1,0:T(8,128)(2,1)} %refs_0_.23), custom_call_target="tpu_custom_call" | custom-call | flops 458752 | bytes 5505024 | tf_op jit(solution)/shard_map/cut/pallas_call | solution.py:91
  140.4 4.1 %cut.9 = (bf16[896,512]{1,0:T(8,128)(2,1)}, bf16[896,512]{1,0:T(8,128)(2,1)}, bf16[896,512]{1,0:T(8,128)(2,1)}) custom-call(s32[1]{0:T(128)} %bitcast.me_ref, bf16[896,10240]{1,0:T(8,128)(2,1)} %refs_0_.23, bf16[896,10240]{1,0:T(8,128)(2,1)} %refs_0_.23, bf16[896,10240]{1,0:T(8,128)(2,1)} %refs_0_.23), custom_call_target="tpu_custom_call" | custom-call | flops 458752 | bytes 5505024 | tf_op jit(solution)/shard_map/cut/pallas_call | solution.py:91
  144.5 4.2 %cut.5 = (bf16[896,512]{1,0:T(8,128)(2,1)}, bf16[896,512]{1,0:T(8,128)(2,1)}, bf16[896,512]{1,0:T(8,128)(2,1)}) custom-call(s32[1]{0:T(128)} %bitcast.me_ref, bf16[896,10240]{1,0:T(8,128)(2,1)} %refs_0_.23, bf16[896,10240]{1,0:T(8,128)(2,1)} %refs_0_.23, bf16[896,10240]{1,0:T(8,128)(2,1)} %refs_0_.23), custom_call_target="tpu_custom_call" | custom-call | flops 458752 | bytes 5505024 | tf_op jit(solution)/shard_map/cut/pallas_call | solution.py:91
  150.7 5.1 %collective-permute-done.7.refs_9_.refs_11_.refs_10_.refs_8_ = bf16[128,3584]{1,0:T(8,128)(2,1)} collective-permute-done((bf16[128,3584]{1,0:T(8,128)(2,1)S(1)}, bf16[128,3584]{1,0:T(8,128)(2,1)}, u32[]{:S(2)}, u32[]{:S(2)}) %collective-permute-start.7) | collective-permute-done | bytes 917536 | tf_op jit(solution)/shard_map/ppermute | solution.py:62
  155.7 18.2 %collective-permute-done.9.refs_11_.refs_13_.refs_12_.refs_10_ = bf16[128,3584]{1,0:T(8,128)(2,1)} collective-permute-done((bf16[128,3584]{1,0:T(8,128)(2,1)}, bf16[128,3584]{1,0:T(8,128)(2,1)}, u32[]{:S(2)}, u32[]{:S(2)}) %collective-permute-start.9) | collective-permute-done | bytes 917536 | tf_op jit(solution)/shard_map/ppermute | solution.py:62
  175.0 13.9 %chunk.8 = f32[3,16,128]{2,1,0:T(8,128)} custom-call(s32[1]{0:T(128)} %bitcast.me_ref, s32[16]{0:T(128)} %iota.12.place_ref, bf16[896,10240]{1,0:T(8,128)(2,1)} %refs_0_.23, bf16[896,512]{1,0:T(8,128)(2,1)} %copy-done.5, bf16[896,512]{1,0:T(8,128)(2,1)} %collective-permute-done.19.refs_2_, bf16[896,512]{1,0:T(8,128)(2,1)} %collective-permute-done.20.refs_3_, ...), custom_call_target="tpu_custom_call" | custom-call | flops 7516192768 | bytes 18350080 | tf_op jit(solution)/shard_map/chunk/pallas_call | solution.py:305
  189.5 14.1 %chunk.9 = f32[3,16,128]{2,1,0:T(8,128)} custom-call(s32[1]{0:T(128)} %bitcast.me_ref, s32[16]{0:T(128)} %iota.13.place_ref, bf16[896,10240]{1,0:T(8,128)(2,1)} %refs_0_.23, bf16[896,512]{1,0:T(8,128)(2,1)} %collective-permute-done.24.refs_1_, bf16[896,512]{1,0:T(8,128)(2,1)} %collective-permute-done.25.refs_2_, ...), custom_call_target="tpu_custom_call" | custom-call | flops 7516192768 | bytes 18350080 | tf_op jit(solution)/shard_map/chunk/pallas_call | solution.py:305
  203.7 1.8 collective-permute-start.28
  205.9 1.7 collective-permute-start.31
  207.6 15.4 %chunk.10 = f32[3,16,128]{2,1,0:T(8,128)} custom-call(s32[1]{0:T(128)} %bitcast.me_ref, s32[16]{0:T(128)} %copy-done.16, bf16[896,10240]{1,0:T(8,128)(2,1)} %refs_0_.23, bf16[896,512]{1,0:T(8,128)(2,1)} %copy-done.5, bf16[896,512]{1,0:T(8,128)(2,1)} %collective-permute-done.19.refs_2_, bf16[896,512]{1,0:T(8,128)(2,1)} %collective-permute-done.20.refs_3_, ...), custom_call_target="tpu_custom_call" | custom-call | flops 7516192768 | bytes 18350080 | tf_op jit(solution)/shard_map/chunk/pallas_call | solution.py:305
  223.0 15.4 %chunk.11 = f32[3,16,128]{2,1,0:T(8,128)} custom-call(s32[1]{0:T(128)} %bitcast.me_ref, s32[16]{0:T(128)} %copy-done.16, bf16[896,10240]{1,0:T(8,128)(2,1)} %refs_0_.23, bf16[896,512]{1,0:T(8,128)(2,1)} %collective-permute-done.24.refs_1_, bf16[896,512]{1,0:T(8,128)(2,1)} %collective-permute-done.25.refs_2_, ...), custom_call_target="tpu_custom_call" | custom-call | flops 7516192768 | bytes 18350080 | tf_op jit(solution)/shard_map/chunk/pallas_call | solution.py:305
  239.0 7.0 %collective-permute-done.29.refs_3_ = bf16[896,512]{1,0:T(8,128)(2,1)} collective-permute-done((bf16[896,512]{1,0:T(8,128)(2,1)}, bf16[896,512]{1,0:T(8,128)(2,1)}, u32[]{:S(2)}, u32[]{:S(2)}) %collective-permute-start.29) | collective-permute-done | bytes 917536 | tf_op jit(solution)/shard_map/ppermute | solution.py:62
  246.0 1.4 collective-permute-start.34
  247.3 24.0 %chunk.12 = f32[3,32,128]{2,1,0:T(8,128)} custom-call(s32[1]{0:T(128)} %bitcast.me_ref, s32[32]{0:T(128)} %pad_add_fusion.place_ref, bf16[896,10240]{1,0:T(8,128)(2,1)} %refs_0_.23, bf16[896,512]{1,0:T(8,128)(2,1)} %copy-done.23, bf16[896,512]{1,0:T(8,128)(2,1)} %collective-permute-done.28.refs_2_, bf16[896,512]{1,0:T(8,128)(2,1)} %collective-permute-done.29.refs_3_, ...), custom_call_target="tpu_custom_call" | custom-call | flops 15032385536 | bytes 33030144 | tf_op jit(solution)/shard_map/chunk/pallas_call | solution.py:305
  271.4 0.8 collective-permute-start
  272.2 13.1 %collective-permute-done.32.refs_3_ = bf16[896,512]{1,0:T(8,128)(2,1)} collective-permute-done((bf16[896,512]{1,0:T(8,128)(2,1)}, bf16[896,512]{1,0:T(8,128)(2,1)}, u32[]{:S(2)}, u32[]{:S(2)}) %collective-permute-start.32) | collective-permute-done | bytes 917536 | tf_op jit(solution)/shard_map/ppermute | solution.py:62
  285.3 24.2 %chunk.13 = f32[3,32,128]{2,1,0:T(8,128)} custom-call(s32[1]{0:T(128)} %bitcast.me_ref, s32[32]{0:T(128)} %pad_add_fusion.place_ref, bf16[896,10240]{1,0:T(8,128)(2,1)} %refs_0_.23, bf16[896,512]{1,0:T(8,128)(2,1)} %collective-permute-done.30.refs_1_, bf16[896,512]{1,0:T(8,128)(2,1)} %collective-permute-done.31.refs_2_, ...), custom_call_target="tpu_custom_call" | custom-call | flops 15032385536 | bytes 33030144 | tf_op jit(solution)/shard_map/chunk/pallas_call | solution.py:305
  309.5 0.8 fusion.3
  311.0 0.9 copy-done.6
  311.9 1.0 copy-done.7
  312.8 19.9 %chunk.14.refs_19_ = f32[4096,512]{1,0:T(8,128)} custom-call(s32[1]{0:T(128)} %bitcast.me_ref, s32[32]{0:T(128)} %pad_add_fusion.place_ref, bf16[896,10240]{1,0:T(8,128)(2,1)} %refs_0_.23, bf16[896,512]{1,0:T(8,128)(2,1)} %copy-done.6, bf16[896,512]{1,0:T(8,128)(2,1)} %copy-done.7, bf16[1024,3584]{1,0:T(8,128)(2,1)} %refs_1_.11, ...), custom_call_target="tpu_custom_call" | custom-call | flops 11274289152 | bytes 24772608 | tf_op jit(solution)/shard_map/chunk/pallas_call | solution.py:305
  332.8 0.9 copy-done.8
  333.7 11.3 %chunk.15 = (f32[3,8,128]{2,1,0:T(8,128)}, f32[3,8,128]{2,1,0:T(8,128)}, f32[3,8,128]{2,1,0:T(8,128)}, f32[3,8,128]{2,1,0:T(8,128)}) custom-call(s32[1]{0:T(128)} %bitcast.me_ref, s32[32]{0:T(128)} %pad_add_fusion.place_ref, bf16[896,512]{1,0:T(8,128)(2,1)} %copy-done.8, bf16[1024,3584]{1,0:T(8,128)(2,1)} %refs_1_.11, ...), custom_call_target="tpu_custom_call" | custom-call | flops 3758096384 | bytes 8257536 | tf_op jit(solution)/shard_map/chunk/pallas_call | solution.py:305
  345.0 0.7 collective-permute-start.35
  345.7 1.7 collective-permute-start.36
  347.4 2.2 collective-permute-done.36
  349.6 1.2 collective-permute-done.37
  350.8 0.7 add_add_fusion
  351.5 1.6 collective-permute-start.38
  353.2 2.1 collective-permute-done.38
  355.3 1.6 collective-permute-start.39
  357.0 2.6 collective-permute-start.40
  360.1 1.5 collective-permute-done.40
  361.6 3.5 collective-permute-done.41
  365.0 0.6 multiply_reduce_fusion
  366.2 1.6 collective-permute-start.42
  367.8 1.3 fusion.18
  (147 shorter events, 10.3 us)
Async XLA Ops:
  0.6 173.3 %collective-permute-start.1 = (bf16[1024,3584]{1,0:T(8,128)(2,1)}, bf16[1024,3584]{1,0:T(8,128)(2,1)}, u32[]{:S(2)}, u32[]{:S(2)}) collective-permute-start(bf16[1024,3584]{1,0:T(8,128)(2,1)} %refs_1_.11), channel_id=1, source_target_pairs={{0,1},{1,0},{2,3},{3,2},{4,5},{5,4},{6,7},{7,6},{8,9},{9,8},{10,11... | collective-permute-start | bytes 22020104 | tf_op jit(solution)/shard_map/ppermute | solution.py:62
  1.2 27.0 %collective-permute-start.21 = (s32[1024]{0:T(1024)}, s32[1024]{0:T(1024)S(1)}, u32[]{:S(2)}, u32[]{:S(2)}) collective-permute-start(s32[1024]{0:T(1024)} %param.8), channel_id=1, source_target_pairs={{0,1},{1,0},{2,3},{3,2},{4,5},{5,4},{6,7},{7,6},{8,9},{9,8},{10,11... | collective-permute-start | bytes 12296 | tf_op jit(solution)/shard_map/ppermute | solution.py:62
  1.3 28.7 %collective-permute-start.22 = (s32[1024]{0:T(1024)}, s32[1024]{0:T(1024)S(1)}, u32[]{:S(2)}, u32[]{:S(2)}) collective-permute-start(s32[1024]{0:T(1024)} %param.8), channel_id=1, source_target_pairs={{0,2},{1,3},{2,0},{3,1},{4,6},{5,7},{6,4},{7,5},{8,10},{9,11},{10,... | collective-permute-start | bytes 12296 | tf_op jit(solution)/shard_map/ppermute | solution.py:62
  4.2 25.9 %collective-permute-start.23 = (s32[1024]{0:T(1024)}, s32[1024]{0:T(1024)S(1)}, u32[]{:S(2)}, u32[]{:S(2)}) collective-permute-start(s32[1024]{0:T(1024)} %param.8), channel_id=1, source_target_pairs={{0,3},{1,2},{2,1},{3,0},{4,7},{5,6},{6,5},{7,4},{8,11},{9,10},{10,... | collective-permute-start | bytes 12296 | tf_op jit(solution)/shard_map/ppermute | solution.py:62
  5.4 22.7 %collective-permute-start.2 = (bf16[128,3584]{1,0:T(8,128)(2,1)S(1)}, bf16[128,3584]{1,0:T(8,128)(2,1)S(1)}, u32[]{:S(2)}, u32[]{:S(2)}) collective-permute-start(bf16[128,3584]{1,0:T(8,128)(2,1)S(1)} %constant_dynamic-slice_fusion), channel_id=1, source_target_pairs={{0,2},{1,3},{2,0},{3,1},{4,6},{5,7},{6,4},{7,5},{8,10},{9,11},{10,... | collective-permute-start | bytes 2752520 | tf_op jit(solution)/shard_map/ppermute | solution.py:62
  11.7 20.1 %copy-start.20 = (f32[16]{0:T(128)S(1)}, f32[16]{0:T(128)}, u32[]{:S(2)}) copy-start(f32[16]{0:T(128)} %param.11) | copy-start | bytes 196
  28.1 62.9 %copy-start = (bf16[128,3584]{1,0:T(8,128)(2,1)}, bf16[128,3584]{1,0:T(8,128)(2,1)S(1)}, u32[]{:S(2)}) copy-start(bf16[128,3584]{1,0:T(8,128)(2,1)S(1)} %collective-permute-done.2.refs_4_.refs_6_.refs_5_.refs_3_) | copy-start | bytes 2752516
  28.1 8.3 %collective-permute-start.18 = (bf16[896,512]{1,0:T(8,128)(2,1)}, bf16[896,512]{1,0:T(8,128)(2,1)S(1)}, u32[]{:S(2)}, u32[]{:S(2)}) collective-permute-start(bf16[896,512]{1,0:T(8,128)(2,1)} %get-tuple-element.31), channel_id=1, source_target_pairs={{0,1},{1,0},{2,3},{3,2},{4,5},{5,4},{6,7},{7,6},{8,9},{9,8},{10,11... | collective-permute-start | bytes 2752520 | tf_op jit(solution)/shard_map/ppermute | solution.py:62
  28.1 23.6 %collective-permute-start.19 = (bf16[896,512]{1,0:T(8,128)(2,1)}, bf16[896,512]{1,0:T(8,128)(2,1)}, u32[]{:S(2)}, u32[]{:S(2)}) collective-permute-start(bf16[896,512]{1,0:T(8,128)(2,1)} %get-tuple-element.32), channel_id=1, source_target_pairs={{0,2},{1,3},{2,0},{3,1},{4,6},{5,7},{6,4},{7,5},{8,10},{9,11},{10,... | collective-permute-start | bytes 2752520 | tf_op jit(solution)/shard_map/ppermute | solution.py:62
  30.0 40.7 %collective-permute-start.20 = (bf16[896,512]{1,0:T(8,128)(2,1)}, bf16[896,512]{1,0:T(8,128)(2,1)}, u32[]{:S(2)}, u32[]{:S(2)}) collective-permute-start(bf16[896,512]{1,0:T(8,128)(2,1)} %get-tuple-element.33), channel_id=1, source_target_pairs={{0,3},{1,2},{2,1},{3,0},{4,7},{5,6},{6,5},{7,4},{8,11},{9,10},{10,... | collective-permute-start | bytes 2752520 | tf_op jit(solution)/shard_map/ppermute | solution.py:62
  30.1 42.5 %collective-permute-start.4 = (bf16[128,3584]{1,0:T(8,128)(2,1)S(1)}, bf16[128,3584]{1,0:T(8,128)(2,1)S(1)}, u32[]{:S(2)}, u32[]{:S(2)}) collective-permute-start(bf16[128,3584]{1,0:T(8,128)(2,1)S(1)} %collective-permute-done.2.refs_4_.refs_6_.refs_5_.refs_3_), channel_id=1, source_target_pairs={{0,8},{4,12},{8,16},{12,20},{16,24},{20,28},{24,0},{28,4},{1,9},{5... | collective-permute-start | bytes 2752520 | tf_op jit(solution)/shard_map/ppermute | solution.py:67
  36.5 36.1 %copy-start.5 = (bf16[896,512]{1,0:T(8,128)(2,1)}, bf16[896,512]{1,0:T(8,128)(2,1)S(1)}, u32[]{:S(2)}) copy-start(bf16[896,512]{1,0:T(8,128)(2,1)S(1)} %collective-permute-done.18.refs_1_) | copy-start | bytes 2752516
  36.5 38.1 %collective-permute-start.24 = (bf16[896,512]{1,0:T(8,128)(2,1)}, bf16[896,512]{1,0:T(8,128)(2,1)}, u32[]{:S(2)}, u32[]{:S(2)}) collective-permute-start(bf16[896,512]{1,0:T(8,128)(2,1)} %get-tuple-element.36), channel_id=1, source_target_pairs={{0,1},{1,0},{2,3},{3,2},{4,5},{5,4},{6,7},{7,6},{8,9},{9,8},{10,11... | collective-permute-start | bytes 2752520 | tf_op jit(solution)/shard_map/ppermute | solution.py:62
  51.8 39.3 %collective-permute-start.25 = (bf16[896,512]{1,0:T(8,128)(2,1)}, bf16[896,512]{1,0:T(8,128)(2,1)}, u32[]{:S(2)}, u32[]{:S(2)}) collective-permute-start(bf16[896,512]{1,0:T(8,128)(2,1)} %get-tuple-element.37), channel_id=1, source_target_pairs={{0,2},{1,3},{2,0},{3,1},{4,6},{5,7},{6,4},{7,5},{8,10},{9,11},{10,... | collective-permute-start | bytes 2752520 | tf_op jit(solution)/shard_map/ppermute | solution.py:62
  70.7 39.0 %collective-permute-start.26 = (bf16[896,512]{1,0:T(8,128)(2,1)}, bf16[896,512]{1,0:T(8,128)(2,1)}, u32[]{:S(2)}, u32[]{:S(2)}) collective-permute-start(bf16[896,512]{1,0:T(8,128)(2,1)} %get-tuple-element.38), channel_id=1, source_target_pairs={{0,3},{1,2},{2,1},{3,0},{4,7},{5,6},{6,5},{7,4},{8,11},{9,10},{10,... | collective-permute-start | bytes 2752520 | tf_op jit(solution)/shard_map/ppermute | solution.py:62
  72.6 67.8 %copy-start.1 = (bf16[128,3584]{1,0:T(8,128)(2,1)}, bf16[128,3584]{1,0:T(8,128)(2,1)S(1)}, u32[]{:S(2)}) copy-start(bf16[128,3584]{1,0:T(8,128)(2,1)S(1)} %collective-permute-done.4.refs_6_.refs_8_.refs_7_.refs_5_) | copy-start | bytes 2752516
  72.6 38.9 %collective-permute-start.6 = (bf16[128,3584]{1,0:T(8,128)(2,1)S(1)}, bf16[128,3584]{1,0:T(8,128)(2,1)S(1)}, u32[]{:S(2)}, u32[]{:S(2)}) collective-permute-start(bf16[128,3584]{1,0:T(8,128)(2,1)S(1)} %collective-permute-done.4.refs_6_.refs_8_.refs_7_.refs_5_), channel_id=1, source_target_pairs={{0,8},{4,12},{8,16},{12,20},{16,24},{20,28},{24,0},{28,4},{1,9},{5... | collective-permute-start | bytes 2752520 | tf_op jit(solution)/shard_map/ppermute | solution.py:67
  74.6 38.9 %collective-permute-start.3 = (bf16[128,3584]{1,0:T(8,128)(2,1)S(1)}, bf16[128,3584]{1,0:T(8,128)(2,1)}, u32[]{:S(2)}, u32[]{:S(2)}) collective-permute-start(bf16[128,3584]{1,0:T(8,128)(2,1)S(1)} %collective-permute-done.2.refs_4_.refs_6_.refs_5_.refs_3_), channel_id=1, source_target_pairs={{0,4},{4,0},{8,12},{12,8},{16,20},{20,16},{24,28},{28,24},{1,5},{5... | collective-permute-start | bytes 2752520 | tf_op jit(solution)/shard_map/ppermute | solution.py:62
  91.1 22.6 %collective-permute-start.10 = (bf16[128,3584]{1,0:T(8,128)(2,1)S(1)}, bf16[128,3584]{1,0:T(8,128)(2,1)}, u32[]{:S(2)}, u32[]{:S(2)}) collective-permute-start(bf16[128,3584]{1,0:T(8,128)(2,1)S(1)} %collective-permute-done.2.refs_4_.refs_6_.refs_5_.refs_3_), channel_id=1, source_target_pairs={{0,1},{1,0},{2,3},{3,2},{4,5},{5,4},{6,7},{7,6},{8,9},{9,8},{10,11... | collective-permute-start | bytes 2752520 | tf_op jit(solution)/shard_map/ppermute | solution.py:62
  109.7 22.7 %collective-permute-start.5 = (bf16[128,3584]{1,0:T(8,128)(2,1)S(1)}, bf16[128,3584]{1,0:T(8,128)(2,1)}, u32[]{:S(2)}, u32[]{:S(2)}) collective-permute-start(bf16[128,3584]{1,0:T(8,128)(2,1)S(1)} %collective-permute-done.4.refs_6_.refs_8_.refs_7_.refs_5_), channel_id=1, source_target_pairs={{0,4},{4,0},{8,12},{12,8},{16,20},{20,16},{24,28},{28,24},{1,5},{5... | collective-permute-start | bytes 2752520 | tf_op jit(solution)/shard_map/ppermute | solution.py:62
  111.5 38.7 %copy-start.2 = (bf16[128,3584]{1,0:T(8,128)(2,1)}, bf16[128,3584]{1,0:T(8,128)(2,1)S(1)}, u32[]{:S(2)}) copy-start(bf16[128,3584]{1,0:T(8,128)(2,1)S(1)} %collective-permute-done.6.refs_8_.refs_10_.refs_9_.refs_7_) | copy-start | bytes 2752516
  111.5 24.3 %collective-permute-start.8 = (bf16[128,3584]{1,0:T(8,128)(2,1)S(1)}, bf16[128,3584]{1,0:T(8,128)(2,1)}, u32[]{:S(2)}, u32[]{:S(2)}) collective-permute-start(bf16[128,3584]{1,0:T(8,128)(2,1)S(1)} %collective-permute-done.6.refs_8_.refs_10_.refs_9_.refs_7_), channel_id=1, source_target_pairs={{0,8},{4,12},{8,16},{12,20},{16,24},{20,28},{24,0},{28,4},{1,9},{5... | collective-permute-start | bytes 2752520 | tf_op jit(solution)/shard_map/ppermute | solution.py:67
  113.1 27.3 %copy-start.16 = (s32[16]{0:T(128)}, s32[16]{0:T(128)S(1)}, u32[]{:S(2)}) copy-start(s32[16]{0:T(128)S(1)} %concatenate.27.place_ref) | copy-start | bytes 196
  113.6 36.6 %collective-permute-start.12 = (bf16[128,3584]{1,0:T(8,128)(2,1)S(1)}, bf16[128,3584]{1,0:T(8,128)(2,1)}, u32[]{:S(2)}, u32[]{:S(2)}) collective-permute-start(bf16[128,3584]{1,0:T(8,128)(2,1)S(1)} %collective-permute-done.4.refs_6_.refs_8_.refs_7_.refs_5_), channel_id=1, source_target_pairs={{0,1},{1,0},{2,3},{3,2},{4,5},{5,4},{6,7},{7,6},{8,9},{9,8},{10,11... | collective-permute-start | bytes 2752520 | tf_op jit(solution)/shard_map/ppermute | solution.py:62
  113.7 36.5 %collective-permute-start.11 = (bf16[128,3584]{1,0:T(8,128)(2,1)}, bf16[128,3584]{1,0:T(8,128)(2,1)S(1)}, u32[]{:S(2)}, u32[]{:S(2)}) collective-permute-start(bf16[128,3584]{1,0:T(8,128)(2,1)} %collective-permute-done.3.refs_5_.refs_7_.refs_6_.refs_4_), channel_id=1, source_target_pairs={{0,1},{1,0},{2,3},{3,2},{4,5},{5,4},{6,7},{7,6},{8,9},{9,8},{10,11... | collective-permute-start | bytes 2752520 | tf_op jit(solution)/shard_map/ppermute | solution.py:62
  132.4 23.3 %collective-permute-start.7 = (bf16[128,3584]{1,0:T(8,128)(2,1)S(1)}, bf16[128,3584]{1,0:T(8,128)(2,1)}, u32[]{:S(2)}, u32[]{:S(2)}) collective-permute-start(bf16[128,3584]{1,0:T(8,128)(2,1)S(1)} %collective-permute-done.6.refs_8_.refs_10_.refs_9_.refs_7_), channel_id=1, source_target_pairs={{0,4},{4,0},{8,12},{12,8},{16,20},{20,16},{24,28},{28,24},{1,5},{5... | collective-permute-start | bytes 2752520 | tf_op jit(solution)/shard_map/ppermute | solution.py:62
  135.7 38.2 %collective-permute-start.9 = (bf16[128,3584]{1,0:T(8,128)(2,1)}, bf16[128,3584]{1,0:T(8,128)(2,1)}, u32[]{:S(2)}, u32[]{:S(2)}) collective-permute-start(bf16[128,3584]{1,0:T(8,128)(2,1)} %collective-permute-done.8.refs_10_.refs_12_.refs_11_.refs_9_), channel_id=1, source_target_pairs={{0,4},{4,0},{8,12},{12,8},{16,20},{20,16},{24,28},{28,24},{1,5},{5... | collective-permute-start | bytes 2752520 | tf_op jit(solution)/shard_map/ppermute | solution.py:62
  144.5 5.0 %copy-start.18 = (s32[1024]{0:T(1024)S(1)}, s32[1024]{0:T(1024)}, u32[]{:S(2)}) copy-start(s32[1024]{0:T(1024)} %param.8) | copy-start | bytes 12292
  149.4 39.5 %copy-start.19 = (f32[16]{0:T(128)}, f32[16]{0:T(128)S(1)}, u32[]{:S(2)}) copy-start(f32[16]{0:T(128)S(1)} %maximum_minimum_fusion) | copy-start | bytes 196
  149.5 39.4 %copy-start.9 = (f32[32,128]{1,0:T(8,128)}, f32[32,128]{1,0:T(8,128)S(1)}, u32[]{:S(2)}) copy-start(f32[32,128]{1,0:T(8,128)S(1)} %fusion.11.refs_22_.refs_20_) | copy-start | bytes 49156
  150.2 53.4 %collective-permute-start.14 = (bf16[128,3584]{1,0:T(8,128)(2,1)S(1)}, bf16[128,3584]{1,0:T(8,128)(2,1)S(1)}, u32[]{:S(2)}, u32[]{:S(2)}) collective-permute-start(bf16[128,3584]{1,0:T(8,128)(2,1)S(1)} %collective-permute-done.6.refs_8_.refs_10_.refs_9_.refs_7_), channel_id=1, source_target_pairs={{0,1},{1,0},{2,3},{3,2},{4,5},{5,4},{6,7},{7,6},{8,9},{9,8},{10,11... | collective-permute-start | bytes 2752520 | tf_op jit(solution)/shard_map/ppermute | solution.py:62
  150.2 38.8 %copy-start.3 = (bf16[128,3584]{1,0:T(8,128)(2,1)}, bf16[128,3584]{1,0:T(8,128)(2,1)S(1)}, u32[]{:S(2)}) copy-start(bf16[128,3584]{1,0:T(8,128)(2,1)S(1)} %collective-permute-done.11.refs_13_.refs_15_.refs_14_.refs_12_) | copy-start | bytes 2752516
  150.2 53.5 %collective-permute-start.13 = (bf16[128,3584]{1,0:T(8,128)(2,1)}, bf16[128,3584]{1,0:T(8,128)(2,1)}, u32[]{:S(2)}, u32[]{:S(2)}) collective-permute-start(bf16[128,3584]{1,0:T(8,128)(2,1)} %collective-permute-done.5.refs_7_.refs_9_.refs_8_.refs_6_), channel_id=1, source_target_pairs={{0,1},{1,0},{2,3},{3,2},{4,5},{5,4},{6,7},{7,6},{8,9},{9,8},{10,11... | collective-permute-start | bytes 2752520 | tf_op jit(solution)/shard_map/ppermute | solution.py:62
  155.7 49.7 %collective-permute-start.16 = (bf16[128,3584]{1,0:T(8,128)(2,1)}, bf16[128,3584]{1,0:T(8,128)(2,1)}, u32[]{:S(2)}, u32[]{:S(2)}) collective-permute-start(bf16[128,3584]{1,0:T(8,128)(2,1)} %collective-permute-done.8.refs_10_.refs_12_.refs_11_.refs_9_), channel_id=1, source_target_pairs={{0,1},{1,0},{2,3},{3,2},{4,5},{5,4},{6,7},{7,6},{8,9},{9,8},{10,11... | collective-permute-start | bytes 2752520 | tf_op jit(solution)/shard_map/ppermute | solution.py:62
  174.0 31.6 %collective-permute-start.15 = (bf16[128,3584]{1,0:T(8,128)(2,1)}, bf16[128,3584]{1,0:T(8,128)(2,1)}, u32[]{:S(2)}, u32[]{:S(2)}) collective-permute-start(bf16[128,3584]{1,0:T(8,128)(2,1)} %collective-permute-done.7.refs_9_.refs_11_.refs_10_.refs_8_), channel_id=1, source_target_pairs={{0,1},{1,0},{2,3},{3,2},{4,5},{5,4},{6,7},{7,6},{8,9},{9,8},{10,11... | collective-permute-start | bytes 2752520 | tf_op jit(solution)/shard_map/ppermute | solution.py:62
  174.0 31.9 %collective-permute-start.17 = (bf16[128,3584]{1,0:T(8,128)(2,1)}, bf16[128,3584]{1,0:T(8,128)(2,1)}, u32[]{:S(2)}, u32[]{:S(2)}) collective-permute-start(bf16[128,3584]{1,0:T(8,128)(2,1)} %collective-permute-done.9.refs_11_.refs_13_.refs_12_.refs_10_), channel_id=1, source_target_pairs={{0,1},{1,0},{2,3},{3,2},{4,5},{5,4},{6,7},{7,6},{8,9},{9,8},{10,11... | collective-permute-start | bytes 2752520 | tf_op jit(solution)/shard_map/ppermute | solution.py:62
  189.5 14.2 %copy-start.22 = (bf16[896,512]{1,0:T(8,128)(2,1)S(1)}, bf16[896,512]{1,0:T(8,128)(2,1)}, u32[]{:S(2)}) copy-start(bf16[896,512]{1,0:T(8,128)(2,1)} %get-tuple-element.43) | copy-start | bytes 2752516
  203.6 34.9 %collective-permute-start.27 = (bf16[896,512]{1,0:T(8,128)(2,1)}, bf16[896,512]{1,0:T(8,128)(2,1)S(1)}, u32[]{:S(2)}, u32[]{:S(2)}) collective-permute-start(bf16[896,512]{1,0:T(8,128)(2,1)} %get-tuple-element.42), channel_id=1, source_target_pairs={{0,1},{1,0},{2,3},{3,2},{4,5},{5,4},{6,7},{7,6},{8,9},{9,8},{10,11... | collective-permute-start | bytes 2752520 | tf_op jit(solution)/shard_map/ppermute | solution.py:62
  203.7 34.8 %collective-permute-start.28 = (bf16[896,512]{1,0:T(8,128)(2,1)S(1)}, bf16[896,512]{1,0:T(8,128)(2,1)}, u32[]{:S(2)}, u32[]{:S(2)}) collective-permute-start(bf16[896,512]{1,0:T(8,128)(2,1)S(1)} %copy-done.22), channel_id=1, source_target_pairs={{0,2},{1,3},{2,0},{3,1},{4,6},{5,7},{6,4},{7,5},{8,10},{9,11},{10,... | collective-permute-start | bytes 2752520 | tf_op jit(solution)/shard_map/ppermute | solution.py:62
  205.5 40.5 %collective-permute-start.29 = (bf16[896,512]{1,0:T(8,128)(2,1)}, bf16[896,512]{1,0:T(8,128)(2,1)}, u32[]{:S(2)}, u32[]{:S(2)}) collective-permute-start(bf16[896,512]{1,0:T(8,128)(2,1)} %get-tuple-element.44), channel_id=1, source_target_pairs={{0,3},{1,2},{2,1},{3,0},{4,7},{5,6},{6,5},{7,4},{8,11},{9,10},{10,... | collective-permute-start | bytes 2752520 | tf_op jit(solution)/shard_map/ppermute | solution.py:62
  205.6 65.8 %collective-permute-start.30 = (bf16[896,512]{1,0:T(8,128)(2,1)}, bf16[896,512]{1,0:T(8,128)(2,1)}, u32[]{:S(2)}, u32[]{:S(2)}) collective-permute-start(bf16[896,512]{1,0:T(8,128)(2,1)} %get-tuple-element.46), channel_id=1, source_target_pairs={{0,1},{1,0},{2,3},{3,2},{4,5},{5,4},{6,7},{7,6},{8,9},{9,8},{10,11... | collective-permute-start | bytes 2752520 | tf_op jit(solution)/shard_map/ppermute | solution.py:62
  205.9 66.3 %collective-permute-start.31 = (bf16[896,512]{1,0:T(8,128)(2,1)}, bf16[896,512]{1,0:T(8,128)(2,1)}, u32[]{:S(2)}, u32[]{:S(2)}) collective-permute-start(bf16[896,512]{1,0:T(8,128)(2,1)} %get-tuple-element.47), channel_id=1, source_target_pairs={{0,2},{1,3},{2,0},{3,1},{4,6},{5,7},{6,4},{7,5},{8,10},{9,11},{10,... | collective-permute-start | bytes 2752520 | tf_op jit(solution)/shard_map/ppermute | solution.py:62
  238.4 8.9 %copy-start.23 = (bf16[896,512]{1,0:T(8,128)(2,1)}, bf16[896,512]{1,0:T(8,128)(2,1)S(1)}, u32[]{:S(2)}) copy-start(bf16[896,512]{1,0:T(8,128)(2,1)S(1)} %collective-permute-done.27.refs_1_) | copy-start | bytes 2752516
  238.5 46.8 %collective-permute-start.32 = (bf16[896,512]{1,0:T(8,128)(2,1)}, bf16[896,512]{1,0:T(8,128)(2,1)}, u32[]{:S(2)}, u32[]{:S(2)}) collective-permute-start(bf16[896,512]{1,0:T(8,128)(2,1)} %get-tuple-element.48), channel_id=1, source_target_pairs={{0,3},{1,2},{2,1},{3,0},{4,7},{5,6},{6,5},{7,4},{8,11},{9,10},{10,... | collective-permute-start | bytes 2752520 | tf_op jit(solution)/shard_map/ppermute | solution.py:62
  238.5 72.4 %collective-permute-start.33 = (bf16[896,512]{1,0:T(8,128)(2,1)}, bf16[896,512]{1,0:T(8,128)(2,1)S(1)}, u32[]{:S(2)}, u32[]{:S(2)}) collective-permute-start(bf16[896,512]{1,0:T(8,128)(2,1)} %get-tuple-element.50), channel_id=1, source_target_pairs={{0,1},{1,0},{2,3},{3,2},{4,5},{5,4},{6,7},{7,6},{8,9},{9,8},{10,11... | collective-permute-start | bytes 2752520 | tf_op jit(solution)/shard_map/ppermute | solution.py:62
  246.0 25.4 %copy-start.21 = (bf16[896,512]{1,0:T(8,128)(2,1)S(1)}, bf16[896,512]{1,0:T(8,128)(2,1)}, u32[]{:S(2)}) copy-start(bf16[896,512]{1,0:T(8,128)(2,1)} %get-tuple-element.30) | copy-start | bytes 2752516
  246.0 65.0 %collective-permute-start.34 = (bf16[896,512]{1,0:T(8,128)(2,1)}, bf16[896,512]{1,0:T(8,128)(2,1)S(1)}, u32[]{:S(2)}, u32[]{:S(2)}) collective-permute-start(bf16[896,512]{1,0:T(8,128)(2,1)} %get-tuple-element.51), channel_id=1, source_target_pairs={{0,2},{1,3},{2,0},{3,1},{4,6},{5,7},{6,4},{7,5},{8,10},{9,11},{10,... | collective-permute-start | bytes 2752520 | tf_op jit(solution)/shard_map/ppermute | solution.py:62
  271.4 38.1 %copy-start.10 = (f32[3,16,128]{2,1,0:T(8,128)S(1)}, f32[3,16,128]{2,1,0:T(8,128)}, u32[]{:S(2)}) copy-start(f32[3,16,128]{2,1,0:T(8,128)} %chunk.8) | copy-start | bytes 73732
  271.4 38.1 %copy-start.11 = (f32[3,16,128]{2,1,0:T(8,128)S(1)}, f32[3,16,128]{2,1,0:T(8,128)}, u32[]{:S(2)}) copy-start(f32[3,16,128]{2,1,0:T(8,128)} %chunk.9) | copy-start | bytes 73732
  271.4 38.1 %copy-start.12 = (f32[3,16,128]{2,1,0:T(8,128)S(1)}, f32[3,16,128]{2,1,0:T(8,128)}, u32[]{:S(2)}) copy-start(f32[3,16,128]{2,1,0:T(8,128)} %chunk.10) | copy-start | bytes 73732
  271.4 38.1 %copy-start.13 = (f32[3,16,128]{2,1,0:T(8,128)S(1)}, f32[3,16,128]{2,1,0:T(8,128)}, u32[]{:S(2)}) copy-start(f32[3,16,128]{2,1,0:T(8,128)} %chunk.11) | copy-start | bytes 73732
  271.4 38.1 %copy-start.15 = (f32[3,32,128]{2,1,0:T(8,128)S(1)}, f32[3,32,128]{2,1,0:T(8,128)}, u32[]{:S(2)}) copy-start(f32[3,32,128]{2,1,0:T(8,128)} %chunk.12) | copy-start | bytes 147460
  271.4 61.4 %collective-permute-start = (bf16[896,512]{1,0:T(8,128)(2,1)S(1)}, bf16[896,512]{1,0:T(8,128)(2,1)S(1)}, u32[]{:S(2)}, u32[]{:S(2)}) collective-permute-start(bf16[896,512]{1,0:T(8,128)(2,1)S(1)} %copy-done.21), channel_id=1, source_target_pairs={{0,3},{1,2},{2,1},{3,0},{4,7},{5,6},{6,5},{7,4},{8,11},{9,10},{10,... | collective-permute-start | bytes 2752520 | tf_op jit(solution)/shard_map/ppermute | solution.py:62
  345.0 2.4 collective-permute-start.35
  345.7 3.9 %collective-permute-start.36 = (f32[3,8,128]{2,1,0:T(8,128)}, f32[3,8,128]{2,1,0:T(8,128)S(1)}, u32[]{:S(2)}, u32[]{:S(2)}) collective-permute-start(f32[3,8,128]{2,1,0:T(8,128)} %get-tuple-element.54), channel_id=1, source_target_pairs={{0,2},{1,3},{2,0},{3,1},{4,6},{5,7},{6,4},{7,5},{8,10},{9,11},{10,... | collective-permute-start | bytes 36872 | tf_op jit(solution)/shard_map/ppermute | solution.py:62
  347.4 3.4 collective-permute-start.37
  351.5 3.8 %collective-permute-start.38 = (f32[3,8,128]{2,1,0:T(8,128)S(1)}, f32[3,8,128]{2,1,0:T(8,128)S(1)}, u32[]{:S(2)}, u32[]{:S(2)}) collective-permute-start(f32[3,8,128]{2,1,0:T(8,128)S(1)} %pad_maximum_fusion.3), channel_id=1, source_target_pairs={{0,4},{4,0},{8,12},{12,8},{16,20},{20,16},{24,28},{28,24},{1,5},{5... | collective-permute-start | bytes 36872 | tf_op jit(solution)/shard_map/ppermute | solution.py:62
  355.3 4.8 %collective-permute-start.39 = (f32[3,8,128]{2,1,0:T(8,128)S(1)}, f32[3,8,128]{2,1,0:T(8,128)S(1)}, u32[]{:S(2)}, u32[]{:S(2)}) collective-permute-start(f32[3,8,128]{2,1,0:T(8,128)S(1)} %pad_maximum_fusion.4), channel_id=1, source_target_pairs={{0,8},{4,12},{8,0},{12,4},{16,24},{20,28},{24,16},{28,20},{1,9},{5... | collective-permute-start | bytes 36872 | tf_op jit(solution)/shard_map/ppermute | solution.py:62
  357.0 4.6 %collective-permute-start.40 = (f32[3,8,128]{2,1,0:T(8,128)S(1)}, f32[3,8,128]{2,1,0:T(8,128)S(1)}, u32[]{:S(2)}, u32[]{:S(2)}) collective-permute-start(f32[3,8,128]{2,1,0:T(8,128)S(1)} %pad_maximum_fusion.4), channel_id=1, source_target_pairs={{0,16},{4,20},{8,24},{12,28},{16,0},{20,4},{24,8},{28,12},{1,17},{... | collective-permute-start | bytes 36872 | tf_op jit(solution)/shard_map/ppermute | solution.py:62
  359.5 5.5 %collective-permute-start.41 = (f32[3,8,128]{2,1,0:T(8,128)S(1)}, f32[3,8,128]{2,1,0:T(8,128)S(1)}, u32[]{:S(2)}, u32[]{:S(2)}) collective-permute-start(f32[3,8,128]{2,1,0:T(8,128)S(1)} %pad_maximum_fusion.4), channel_id=1, source_target_pairs={{0,24},{4,28},{8,16},{12,20},{16,8},{20,12},{24,0},{28,4},{1,25},{... | collective-permute-start | bytes 36872 | tf_op jit(solution)/shard_map/ppermute | solution.py:62
  359.9 11.7 %copy-start.17 = (f32[256]{0:T(256)}, f32[256]{0:T(256)S(1)}, u32[]{:S(2)}) copy-start(f32[256]{0:T(256)S(1)} %div.75) | copy-start | bytes 3076
  365.7 4.7 %collective-permute-start.43 = (f32[1]{0:T(128)}, f32[1]{0:T(128)}, u32[]{:S(2)}, u32[]{:S(2)}) collective-permute-start(f32[1]{0:T(128)} %bitcast.31), channel_id=1, source_target_pairs={{0,2},{1,3},{2,0},{3,1},{4,6},{5,7},{6,4},{7,5},{8,10},{9,11},{10,... | collective-permute-start | bytes 20 | tf_op jit(solution)/shard_map/ppermute | solution.py:62
  366.2 4.2 %collective-permute-start.44 = (f32[1]{0:T(128)}, f32[1]{0:T(128)}, u32[]{:S(2)}, u32[]{:S(2)}) collective-permute-start(f32[1]{0:T(128)} %bitcast.31), channel_id=1, source_target_pairs={{0,3},{1,2},{2,1},{3,0},{4,7},{5,6},{6,5},{7,4},{8,11},{9,10},{10,... | collective-permute-start | bytes 20 | tf_op jit(solution)/shard_map/ppermute | solution.py:62
  366.2 2.9 collective-permute-start.42
  (5 other events, 11.3 us)

commit v3 on v2

--- a/solution.py
+++ b/solution.py
@@ -15,6 +15,7 @@
 
 
 LANES = 128
+LOWEST = -3.0e38
 WIDTH = 512
 ROWS = 256
 SLOTS = 3
@@ -153,16 +154,20 @@
                         )
             reached += high
         made = [
-            pltpu.make_async_copy(source, target, token_sem.at[slot, index])
-            for index, (source, target) in enumerate(found)
+            pltpu.make_async_copy(source, target, token_sem.at[slot]) for source, target in found
         ]
         if partial_ref is not None:
-            made.append(
-                pltpu.make_async_copy(
-                    partial_ref.at[pl.ds(start, tall), :], before.at[slot], before_sem.at[slot]
-                )
-            )
+            made.append(before_copy(which))
         return made
+
+    def before_copy(which):
+        slot = which % SLOTS
+        return pltpu.make_async_copy(
+            partial_ref.at[pl.ds(which * tall, tall), :], before.at[slot], before_sem.at[slot]
+        )
+
+    def landed(ref, sem):
+        pltpu.make_async_copy(ref, ref, sem).wait()
 
     def piece_copy(index):
         distance = distances[index]
@@ -173,7 +178,7 @@
         if distance == 0:
             column = pl.multiple_of(me * quarter + offset, LANES)
             source = source.at[:, pl.ds(column, width)]
-        return pltpu.make_async_copy(source, target, piece_sem.at[index])
+        return pltpu.make_async_copy(source, target, piece_sem.at[0])
 
     def finish(acc, tile):
         lane = lax.broadcasted_iota(jnp.int32, (LANES, LANES), 1)
@@ -208,8 +213,12 @@
                 copy.start()
         if second is not None:
             second[...] = jnp.zeros_like(second)
-        for index in range(len(distances)):
-            piece_copy(index).wait()
+            if prior_ref is None:
+                neutral = jnp.zeros(stats_ref.shape[1:], jnp.float32)
+                stats_ref[0] = neutral + LOWEST
+                stats_ref[1] = neutral
+                stats_ref[2] = neutral
+        landed(weights, piece_sem.at[0])
 
     for which in range(steps):
 
@@ -218,8 +227,9 @@
             if which + SLOTS - 1 < steps:
                 for copy in copies(which + SLOTS - 1):
                     copy.start()
-            for copy in copies(which):
-                copy.wait()
+            landed(held.at[which % SLOTS], token_sem.at[which % SLOTS])
+            if partial_ref is not None:
+                before_copy(which).wait()
 
     slot = lax.rem(step, SLOTS)
     if not cfg["finish"]:
@@ -262,12 +272,11 @@
     whole = lambda shape: pl.BlockSpec(shape, lambda i, *_: (0,) * len(shape))
     operands = [*pieces, *tokens]
     in_specs = [anywhere] * len(operands)
-    most = max(1, tall // min(part.shape[0] for part in tokens))
     scratch = [
         pltpu.VMEM((inner, width), tokens[0].dtype),
         pltpu.VMEM((SLOTS, tall, inner), tokens[0].dtype),
-        pltpu.SemaphoreType.DMA((len(distances),)),
-        pltpu.SemaphoreType.DMA((SLOTS, most * len(distances))),
+        pltpu.SemaphoreType.DMA((1,)),
+        pltpu.SemaphoreType.DMA((SLOTS,)),
     ]
     if partial is not None:
         operands.append(partial)
@@ -284,8 +293,8 @@
         out_shape = [jax.ShapeDtypeStruct(shape, jnp.float32)] * parts
         out_specs = [whole(shape)] * parts
     elif finish:
-        out_shape = [jax.ShapeDtypeStruct((3, rows, LANES), jnp.float32)]
-        out_specs = [whole((3, rows, LANES))]
+        out_shape = [jax.ShapeDtypeStruct((3, *ids.shape), jnp.float32)]
+        out_specs = [whole((3, *ids.shape))]
     else:
         out_shape = [jax.ShapeDtypeStruct((count, width), jnp.float32)]
         out_specs = [pl.BlockSpec((tall, width), lambda i, *_: (i, 0))]
@@ -381,40 +390,55 @@
     remote_pair = [swap(part, "prompt", 1) for part in remote]
 
     rows = strip // LANES
-    order = []
-    for hop in range(vocabs // 2):
-        for other in (0, 1):
-            origin = lax.rem((shard ^ other) - 2 * hop + vocabs, vocabs)
-            order += [origin * rows + part for part in range(rows)]
-    order = jnp.stack(order).astype(jnp.int32)
-    near = jnp.arange(2 * each // LANES, dtype=jnp.int32)
-    far = jnp.concatenate([order, order + each // LANES])
-    place = jnp.concatenate([near, far + 2 * each // LANES])
-
-    close, distant = [latent_vectors, partner], remote + remote_pair
-    halves = ((near, close, ids[: 2 * each // LANES]), (far, distant, ids[2 * each // LANES :]))
-    both = (place, close + distant, ids)
+    base = each // LANES
+
+    def origins(hops):
+        found = []
+        for hop in hops:
+            for other in (0, 1):
+                origin = lax.rem((shard ^ other) - 2 * hop + vocabs, vocabs)
+                found += [origin * rows + part for part in range(rows)]
+        found = jnp.stack(found).astype(jnp.int32)
+        return jnp.concatenate([found + half * base, found + (half + 1) * base])
+
+    hops = vocabs // 2
+    split = max(1, hops // 2)
+    near = jnp.arange(2 * base, dtype=jnp.int32)
+    soon = remote[: 2 * split] + remote_pair[: 2 * split]
+    late = remote[2 * split :] + remote_pair[2 * split :]
+    first = (jnp.concatenate([near, origins(range(split))]), [latent_vectors, partner] + soon)
+    second = (origins(range(split, hops)), late)
+    both = (jnp.concatenate([first[0], second[0]]), first[1] + second[1])
+
     early = min(EARLY, chunks - 1)
-    jobs = [(chunk, half) for half in (0, 1) for chunk in range(early)]
-    jobs += [(chunk, None) for chunk in range(early, chunks - 1)]
-    done = {}
     gate = mine
-    for chunk, half in jobs:
-        where, tokens, part = both if half is None else halves[half]
-        done[chunk, half] = chunk_call(
-            gate, where, pieces[chunk], spans, tokens, quarter, chunk * WIDTH, WIDTH, ids=part
+    stats = []
+    partial = None
+    last = (chunks - 1) * WIDTH
+
+    def head(distances, gate, partial):
+        where, tokens = both
+        return chunk_call(
+            gate, where, [pieces[-1][d] for d in distances], distances, tokens, quarter, last, WIDTH,
+            partial=partial,
         )[0]
-        gate = after(mine, done[chunk, half])
-    prior = [jnp.concatenate([done[chunk, 0], done[chunk, 1]], axis=1) for chunk in range(early)]
-    prior = merge(prior + [done[chunk, None] for chunk in range(early, chunks - 1)])
-    offset = (chunks - 1) * WIDTH
-    partial = chunk_call(
-        gate, place, pieces[-1][: prompts - 1], spans[: prompts - 1], close + distant, quarter,
-        offset, WIDTH,
-    )[0]
+
+    jobs = [(chunk, group) for group in (first, second) for chunk in range(early)]
+    jobs += [(chunk, both) for chunk in range(early, chunks - 1)]
+    for index, (chunk, (where, tokens)) in enumerate(jobs):
+        if index == len(jobs) - 1:
+            partial = head(spans[:half], gate, None)
+            gate = after(mine, partial)
+        found = chunk_call(
+            gate, where, pieces[chunk], spans, tokens, quarter, chunk * WIDTH, WIDTH, ids=ids
+        )[0]
+        stats.append(found)
+        gate = after(mine, found)
+    for distance in spans[half:-1]:
+        partial = head([distance], gate, partial)
     blocks = chunk_call(
-        mine, place, pieces[-1][prompts - 1 :], spans[prompts - 1 :], close + distant, quarter,
-        offset, WIDTH, ids=ids, partial=partial, prior=prior, parts=prompts,
+        mine, both[0], pieces[-1][-1:], spans[-1:], both[1], quarter, last, WIDTH, ids=ids,
+        partial=partial, prior=merge(stats), parts=prompts,
     )
     return merge([block if d == 0 else swap(block, "prompt", d) for d, block in enumerate(blocks)])
 

time: 374 us -> 334 us (0.89)
  waiting for transfers between devices: 152 us -> 114 us
    ppermute x42, waiting for transfers between devices: 150 us -> 103 us  [swap(): return lax.ppermute(value, axis, [(i, i ^ distance) for i in range(size)])]
    ppermute x3, waiting for transfers between devices: 1.59 us -> 10.6 us  [shift(): lax.ppermute(value, axis, [(i, (i + distance) % size) for i in range(size)])]
    pallas_call x8 -> x9, Pallas kernels: 138 us -> 141 us  [chunk_call(): pl.pallas_call(functools.partial(chunk_kernel, cfg), grid_spec=pltpu.Pref...]
  transfers between devices with their start and end apart: 45 -> 45, of which waited for: 16 -> 18; matrix products, arithmetic and copies ran while one was open for 3% -> 3% of each run, Pallas kernels for 40% -> 45%
where the time goes in v3:
time: 334 us; the launch traced here: 333 us
  Pallas kernels  162 us (49%)
  waiting for transfers between devices  114 us (34%)
  starting transfers between devices  38.1 us (11%)
  other arithmetic  8.31 us (2%)
  local copies, waits for them, and re-layouts  6.16 us (2%)
  between operations  4.85 us (1%)
    pallas_call x9, Pallas kernels, chunk_call(): pl.pallas_call(functools.partial(chunk_kernel, cfg), grid_spec=pltpu.Pref...  141 us
    ppermute x42, waiting for transfers between devices, swap(): return lax.ppermute(value, axis, [(i, i ^ distance) for i in range(size)])  103 us
    ppermute x42, starting transfers between devices, swap(): return lax.ppermute(value, axis, [(i, i ^ distance) for i in range(size)])  34.7 us
    pallas_call x5, Pallas kernels, cut_blocks(): pl.pallas_call(cut_kernel, grid_spec=pltpu.PrefetchScalarGridSpec(num_sca...  20.8 us
    ppermute x3, waiting for transfers between devices, shift(): lax.ppermute(value, axis, [(i, (i + distance) % size) for i in range(size)])  10.6 us
  transfers between devices with their start and end apart: 45, of which 18 were waited for; matrix products, arithmetic and copies ran while one was open for 3% of the time, Pallas kernels for 45%

profile of v3, /device:TPU:0, one launch (start us, length us, event | category | flops | bytes accessed | tf_op | source)
XLA Modules:
  0.0 332.7 jit_solution(6779967562258932020)
XLA Ops:
  1.2 2.2 constant_dynamic-slice_fusion
  3.4 2.5 collective-permute-start.2
  5.9 4.2 %cut.6 = (bf16[896,512]{1,0:T(8,128)(2,1)}, bf16[896,512]{1,0:T(8,128)(2,1)}, bf16[896,512]{1,0:T(8,128)(2,1)}) custom-call(s32[1]{0:T(128)} %bitcast.me_ref, bf16[896,10240]{1,0:T(8,128)(2,1)} %refs_0_.23, bf16[896,10240]{1,0:T(8,128)(2,1)} %refs_0_.23, bf16[896,10240]{1,0:T(8,128)(2,1)} %refs_0_.23), custom_call_target="tpu_custom_call" | custom-call | flops 458752 | bytes 5505024 | tf_op jit(solution)/shard_map/cut/pallas_call | solution.py:92
  11.9 2.1 collective-permute-done.21
  14.0 2.8 collective-permute-start.22
  16.9 10.4 %collective-permute-done.2.refs_6_.refs_4_.refs_3_ = bf16[128,3584]{1,0:T(8,128)(2,1)S(1)} collective-permute-done((bf16[128,3584]{1,0:T(8,128)(2,1)}, bf16[128,3584]{1,0:T(8,128)(2,1)S(1)}, u32[]{:S(2)}, u32[]{:S(2)}) %collective-permute-start.2) | collective-permute-done | bytes 917536 | tf_op jit(solution)/shard_map/ppermute | solution.py:63
  27.3 0.8 collective-permute-start.23
  28.1 4.1 %cut.7 = (bf16[896,512]{1,0:T(8,128)(2,1)}, bf16[896,512]{1,0:T(8,128)(2,1)}, bf16[896,512]{1,0:T(8,128)(2,1)}) custom-call(s32[1]{0:T(128)} %bitcast.me_ref, bf16[896,10240]{1,0:T(8,128)(2,1)} %refs_0_.23, bf16[896,10240]{1,0:T(8,128)(2,1)} %refs_0_.23, bf16[896,10240]{1,0:T(8,128)(2,1)} %refs_0_.23), custom_call_target="tpu_custom_call" | custom-call | flops 458752 | bytes 5505024 | tf_op jit(solution)/shard_map/cut/pallas_call | solution.py:92
  32.3 14.6 %collective-permute-done.22 = s32[1024]{0:T(1024)S(1)} collective-permute-done((s32[1024]{0:T(1024)S(1)}, s32[1024]{0:T(1024)S(1)}, u32[]{:S(2)}, u32[]{:S(2)}) %collective-permute-start.22) | collective-permute-done | bytes 4128 | tf_op jit(solution)/shard_map/ppermute | solution.py:63
  46.9 0.9 collective-permute-start.20
  47.8 0.9 collective-permute-start.24
  49.0 0.7 copy-done.8
  49.7 1.6 collective-permute-start.4
  51.6 17.8 %collective-permute-done.20.refs_3_ = bf16[896,512]{1,0:T(8,128)(2,1)S(1)} collective-permute-done((bf16[896,512]{1,0:T(8,128)(2,1)}, bf16[896,512]{1,0:T(8,128)(2,1)S(1)}, u32[]{:S(2)}, u32[]{:S(2)}) %collective-permute-start.20) | collective-permute-done | bytes 917536 | tf_op jit(solution)/shard_map/ppermute | solution.py:63
  69.4 2.0 collective-permute-start.3
  71.6 2.3 collective-permute-done.4.refs_8_.refs_6_.refs_5_
  73.8 1.5 collective-permute-start.5
  75.4 14.0 %collective-permute-done.25.refs_2_ = bf16[896,512]{1,0:T(8,128)(2,1)S(1)} collective-permute-done((bf16[896,512]{1,0:T(8,128)(2,1)}, bf16[896,512]{1,0:T(8,128)(2,1)S(1)}, u32[]{:S(2)}, u32[]{:S(2)}) %collective-permute-start.25) | collective-permute-done | bytes 917536 | tf_op jit(solution)/shard_map/ppermute | solution.py:63
  89.4 1.8 collective-permute-start.10
  93.2 19.0 %collective-permute-done.5.refs_9_.refs_7_.refs_6_ = bf16[128,3584]{1,0:T(8,128)(2,1)} collective-permute-done((bf16[128,3584]{1,0:T(8,128)(2,1)S(1)}, bf16[128,3584]{1,0:T(8,128)(2,1)}, u32[]{:S(2)}, u32[]{:S(2)}) %collective-permute-start.5) | collective-permute-done | bytes 917536 | tf_op jit(solution)/shard_map/ppermute | solution.py:63
  112.2 1.8 collective-permute-done.10.refs_4_.refs_14_.refs_12_.refs_11_
  114.0 0.6 pad_add_fusion.2.place_ref
  114.6 4.1 %cut.8 = (bf16[896,512]{1,0:T(8,128)(2,1)}, bf16[896,512]{1,0:T(8,128)(2,1)}, bf16[896,512]{1,0:T(8,128)(2,1)}) custom-call(s32[1]{0:T(128)} %bitcast.me_ref, bf16[896,10240]{1,0:T(8,128)(2,1)} %refs_0_.23, bf16[896,10240]{1,0:T(8,128)(2,1)} %refs_0_.23, bf16[896,10240]{1,0:T(8,128)(2,1)} %refs_0_.23), custom_call_target="tpu_custom_call" | custom-call | flops 458752 | bytes 5505024 | tf_op jit(solution)/shard_map/cut/pallas_call | solution.py:92
  118.7 4.2 %cut.5 = (bf16[896,512]{1,0:T(8,128)(2,1)}, bf16[896,512]{1,0:T(8,128)(2,1)}, bf16[896,512]{1,0:T(8,128)(2,1)}) custom-call(s32[1]{0:T(128)} %bitcast.me_ref, bf16[896,10240]{1,0:T(8,128)(2,1)} %refs_0_.23, bf16[896,10240]{1,0:T(8,128)(2,1)} %refs_0_.23, bf16[896,10240]{1,0:T(8,128)(2,1)} %refs_0_.23), custom_call_target="tpu_custom_call" | custom-call | flops 458752 | bytes 5505024 | tf_op jit(solution)/shard_map/cut/pallas_call | solution.py:92
  122.9 4.2 %cut.9 = (bf16[896,512]{1,0:T(8,128)(2,1)}, bf16[896,512]{1,0:T(8,128)(2,1)}, bf16[896,512]{1,0:T(8,128)(2,1)}) custom-call(s32[1]{0:T(128)} %bitcast.me_ref, bf16[896,10240]{1,0:T(8,128)(2,1)} %refs_0_.23, bf16[896,10240]{1,0:T(8,128)(2,1)} %refs_0_.23, bf16[896,10240]{1,0:T(8,128)(2,1)} %refs_0_.23), custom_call_target="tpu_custom_call" | custom-call | flops 458752 | bytes 5505024 | tf_op jit(solution)/shard_map/cut/pallas_call | solution.py:92
  128.0 0.6 fusion.7.refs_14_.refs_12_.refs_22_.refs_20_
  129.2 1.5 collective-permute-start.11
  131.2 6.6 %collective-permute-done.12.refs_6_.refs_16_.refs_14_.refs_13_ = bf16[128,3584]{1,0:T(8,128)(2,1)} collective-permute-done((bf16[128,3584]{1,0:T(8,128)(2,1)}, bf16[128,3584]{1,0:T(8,128)(2,1)}, u32[]{:S(2)}, u32[]{:S(2)}) %collective-permute-start.12) | collective-permute-done | bytes 917536 | tf_op jit(solution)/shard_map/ppermute | solution.py:68
  137.8 1.3 collective-permute-start.13
  139.1 18.1 %chunk.9 = f32[3,32,128]{2,1,0:T(8,128)} custom-call(s32[1]{0:T(128)} %bitcast.me_ref, s32[24]{0:T(128)} %pad_add_fusion.2.place_ref, bf16[896,10240]{1,0:T(8,128)(2,1)} %refs_0_.23, bf16[896,512]{1,0:T(8,128)(2,1)} %copy-done.8, bf16[896,512]{1,0:T(8,128)(2,1)} %copy-done.9, bf16[896,512]{1,0:T(8,128)(2,1)} %copy-done.10, bf16[1024,3584]{1,0:T(8,128)(2,1)} %refs_1_.13, ...), custom_call_target="tpu_custom_call" | custom-call | flops 11274289152 | bytes 25690112 | tf_op jit(solution)/shard_map/chunk/pallas_call | solution.py:314
  157.8 1.6 collective-permute-start.28
  159.4 12.8 %collective-permute-done.13.refs_7_.refs_17_.refs_15_.refs_14_ = bf16[128,3584]{1,0:T(8,128)(2,1)} collective-permute-done((bf16[128,3584]{1,0:T(8,128)(2,1)}, bf16[128,3584]{1,0:T(8,128)(2,1)}, u32[]{:S(2)}, u32[]{:S(2)}) %collective-permute-start.13) | collective-permute-done | bytes 917536 | tf_op jit(solution)/shard_map/ppermute | solution.py:63
  172.7 18.1 %chunk.10 = f32[3,32,128]{2,1,0:T(8,128)} custom-call(s32[1]{0:T(128)} %bitcast.me_ref, s32[24]{0:T(128)} %pad_add_fusion.2.place_ref, bf16[896,10240]{1,0:T(8,128)(2,1)} %refs_0_.23, bf16[896,512]{1,0:T(8,128)(2,1)} %copy-done.11, bf16[896,512]{1,0:T(8,128)(2,1)} %copy-done.12, bf16[896,512]{1,0:T(8,128)(2,1)} %collective-permute-done.26.refs_3_, ...), custom_call_target="tpu_custom_call" | custom-call | flops 11274289152 | bytes 25690112 | tf_op jit(solution)/shard_map/chunk/pallas_call | solution.py:314
  191.9 10.5 %chunk.11 = f32[3,32,128]{2,1,0:T(8,128)} custom-call(s32[1]{0:T(128)} %bitcast.me_ref, s32[8]{0:T(128)} %pad_add_fusion.3.place_ref, bf16[896,10240]{1,0:T(8,128)(2,1)} %refs_0_.23, bf16[896,512]{1,0:T(8,128)(2,1)} %copy-done.8, bf16[896,512]{1,0:T(8,128)(2,1)} %copy-done.9, bf16[896,512]{1,0:T(8,128)(2,1)} %copy-done.10, ...), custom_call_target="tpu_custom_call" | custom-call | flops 3758096384 | bytes 11010048 | tf_op jit(solution)/shard_map/chunk/pallas_call | solution.py:314
  202.4 10.5 %chunk.12 = f32[3,32,128]{2,1,0:T(8,128)} custom-call(s32[1]{0:T(128)} %bitcast.me_ref, s32[8]{0:T(128)} %pad_add_fusion.3.place_ref, bf16[896,10240]{1,0:T(8,128)(2,1)} %refs_0_.23, bf16[896,512]{1,0:T(8,128)(2,1)} %copy-done.11, bf16[896,512]{1,0:T(8,128)(2,1)} %copy-done.12, bf16[896,512]{1,0:T(8,128)(2,1)} %collective-permute-done.26.refs_3_, ...), custom_call_target="tpu_custom_call" | custom-call | flops 3758096384 | bytes 11010048 | tf_op jit(solution)/shard_map/chunk/pallas_call | solution.py:314
  213.0 0.8 collective-permute-start.32
  213.8 0.6 collective-permute-start.33
  214.4 0.8 collective-permute-start.34
  215.1 23.5 %chunk.13 = f32[3,32,128]{2,1,0:T(8,128)} custom-call(s32[1]{0:T(128)} %bitcast.me_ref, s32[32]{0:T(128)} %concatenate.22.place_ref, bf16[896,10240]{1,0:T(8,128)(2,1)} %refs_0_.23, bf16[896,512]{1,0:T(8,128)(2,1)} %collective-permute-done.27.refs_1_, bf16[896,512]{1,0:T(8,128)(2,1)} %collective-permute-done.28.refs_2_, ...), custom_call_target="tpu_custom_call" | custom-call | flops 15032385536 | bytes 33030144 | tf_op jit(solution)/shard_map/chunk/pallas_call | solution.py:314
  238.6 1.4 collective-permute-start
  240.1 14.0 %chunk.14.refs_19_ = f32[4096,512]{1,0:T(8,128)} custom-call(s32[1]{0:T(128)} %bitcast.me_ref, s32[32]{0:T(128)} %concatenate.22.place_ref, bf16[896,10240]{1,0:T(8,128)(2,1)} %refs_0_.23, bf16[896,512]{1,0:T(8,128)(2,1)} %copy-done.15, bf16[1024,3584]{1,0:T(8,128)(2,1)} %refs_1_.13, bf16[1024,3584]{1,0:T(8,128)(2,1)} %collective-permute-done.1.refs_5_.refs_3_.refs_2_, ...), custom_call_target="tpu_custom_call" | custom-call | flops 7516192768 | bytes 16515072 | tf_op jit(solution)/shard_map/chunk/pallas_call | solution.py:314
  254.5 23.5 %chunk.15 = f32[3,32,128]{2,1,0:T(8,128)} custom-call(s32[1]{0:T(128)} %bitcast.me_ref, s32[32]{0:T(128)} %concatenate.22.place_ref, bf16[896,10240]{1,0:T(8,128)(2,1)} %refs_0_.23, bf16[896,512]{1,0:T(8,128)(2,1)} %collective-permute-done.31.refs_1_, bf16[896,512]{1,0:T(8,128)(2,1)} %collective-permute-done.32.refs_2_, ...), custom_call_target="tpu_custom_call" | custom-call | flops 15032385536 | bytes 33030144 | tf_op jit(solution)/shard_map/chunk/pallas_call | solution.py:314
  278.0 0.8 fusion.3
  278.8 0.6 pad_maximum_fusion.refs_21_
  279.4 1.0 copy-done.14
  280.4 11.7 %chunk.16.refs_19_ = f32[4096,512]{1,0:T(8,128)} custom-call(s32[1]{0:T(128)} %bitcast.me_ref, s32[32]{0:T(128)} %concatenate.22.place_ref, bf16[896,512]{1,0:T(8,128)(2,1)} %copy-done.14, bf16[1024,3584]{1,0:T(8,128)(2,1)} %refs_1_.13, bf16[1024,3584]{1,0:T(8,128)(2,1)} %collective-permute-done.1.refs_5_.refs_3_.refs_2_, bf16[128,3584]{1,0:T(8,128)(2,1)} %copy-done, ...), custom_call_target="tpu_custom_call" | custom-call | flops 3758096384 | bytes 8257536 | tf_op jit(solution)/shard_map/chunk/pallas_call | solution.py:314
  292.1 1.3 collective-permute-done.refs_0_
  293.5 1.0 copy-done.13
  294.5 10.9 %chunk.17 = (f32[3,8,128]{2,1,0:T(8,128)}, f32[3,8,128]{2,1,0:T(8,128)}, f32[3,8,128]{2,1,0:T(8,128)}, f32[3,8,128]{2,1,0:T(8,128)}) custom-call(s32[1]{0:T(128)} %bitcast.me_ref, s32[32]{0:T(128)} %concatenate.22.place_ref, bf16[896,512]{1,0:T(8,128)(2,1)} %copy-done.13, bf16[1024,3584]{1,0:T(8,128)(2,1)} %refs_1_.13, ...), custom_call_target="tpu_custom_call" | custom-call | flops 3758096384 | bytes 8257536 | tf_op jit(solution)/shard_map/chunk/pallas_call | solution.py:314
  305.4 0.9 collective-permute-start.35
  306.3 0.8 collective-permute-start.36
  307.0 0.7 collective-permute-start.37
  307.7 2.5 collective-permute-done.36
  310.5 0.7 add_add_fusion
  311.2 1.6 collective-permute-start.38
  312.9 2.1 collective-permute-done.38
  315.0 1.6 collective-permute-start.39
  316.6 2.8 collective-permute-start.40
  319.7 1.5 collective-permute-done.40
  321.2 3.7 %collective-permute-done.41 = f32[3,8,128]{2,1,0:T(8,128)S(1)} collective-permute-done((f32[3,8,128]{2,1,0:T(8,128)S(1)}, f32[3,8,128]{2,1,0:T(8,128)S(1)}, u32[]{:S(2)}, u32[]{:S(2)}) %collective-permute-start.41) | collective-permute-done | bytes 12320 | tf_op jit(solution)/shard_map/ppermute | solution.py:63
  324.9 0.6 multiply_reduce_fusion
  325.5 1.1 collective-permute-start.43
  326.6 1.0 collective-permute-start.42
  327.6 1.3 fusion.14
  (157 shorter events, 10.3 us)
Async XLA Ops:
  0.6 138.5 %collective-permute-start.1 = (bf16[1024,3584]{1,0:T(8,128)(2,1)}, bf16[1024,3584]{1,0:T(8,128)(2,1)}, u32[]{:S(2)}, u32[]{:S(2)}) collective-permute-start(bf16[1024,3584]{1,0:T(8,128)(2,1)} %refs_1_.13), channel_id=1, source_target_pairs={{0,1},{1,0},{2,3},{3,2},{4,5},{5,4},{6,7},{7,6},{8,9},{9,8},{10,11... | collective-permute-start | bytes 22020104 | tf_op jit(solution)/shard_map/ppermute | solution.py:63
  3.4 23.9 %collective-permute-start.2 = (bf16[128,3584]{1,0:T(8,128)(2,1)}, bf16[128,3584]{1,0:T(8,128)(2,1)S(1)}, u32[]{:S(2)}, u32[]{:S(2)}) collective-permute-start(bf16[128,3584]{1,0:T(8,128)(2,1)} %constant_dynamic-slice_fusion), channel_id=1, source_target_pairs={{0,2},{1,3},{2,0},{3,1},{4,6},{5,7},{6,4},{7,5},{8,10},{9,11},{10,... | collective-permute-start | bytes 2752520 | tf_op jit(solution)/shard_map/ppermute | solution.py:63
  5.9 4.9 %copy-start.27 = (f32[16]{0:T(128)S(1)}, f32[16]{0:T(128)}, u32[]{:S(2)}) copy-start(f32[16]{0:T(128)} %param.11) | copy-start | bytes 196
  10.1 38.6 %collective-permute-start.18 = (bf16[896,512]{1,0:T(8,128)(2,1)}, bf16[896,512]{1,0:T(8,128)(2,1)S(1)}, u32[]{:S(2)}, u32[]{:S(2)}) collective-permute-start(bf16[896,512]{1,0:T(8,128)(2,1)} %get-tuple-element.32), channel_id=1, source_target_pairs={{0,1},{1,0},{2,3},{3,2},{4,5},{5,4},{6,7},{7,6},{8,9},{9,8},{10,11... | collective-permute-start | bytes 2752520 | tf_op jit(solution)/shard_map/ppermute | solution.py:63
  10.3 39.4 %collective-permute-start.19 = (bf16[896,512]{1,0:T(8,128)(2,1)}, bf16[896,512]{1,0:T(8,128)(2,1)S(1)}, u32[]{:S(2)}, u32[]{:S(2)}) collective-permute-start(bf16[896,512]{1,0:T(8,128)(2,1)} %get-tuple-element.33), channel_id=1, source_target_pairs={{0,2},{1,3},{2,0},{3,1},{4,6},{5,7},{6,4},{7,5},{8,10},{9,11},{10,... | collective-permute-start | bytes 2752520 | tf_op jit(solution)/shard_map/ppermute | solution.py:63
  10.6 3.4 %collective-permute-start.21 = (s32[1024]{0:T(1024)S(1)}, s32[1024]{0:T(1024)S(1)}, u32[]{:S(2)}, u32[]{:S(2)}) collective-permute-start(s32[1024]{0:T(1024)S(1)} %copy-done.25), channel_id=1, source_target_pairs={{0,1},{1,0},{2,3},{3,2},{4,5},{5,4},{6,7},{7,6},{8,9},{9,8},{10,11... | collective-permute-start | bytes 12296 | tf_op jit(solution)/shard_map/ppermute | solution.py:63
  10.8 40.8 %copy-start.22 = (f32[256]{0:T(256)}, f32[256]{0:T(256)S(1)}, u32[]{:S(2)}) copy-start(f32[256]{0:T(256)S(1)} %get-tuple-element.69) | copy-start | bytes 3076
  14.0 32.9 %collective-permute-start.22 = (s32[1024]{0:T(1024)S(1)}, s32[1024]{0:T(1024)S(1)}, u32[]{:S(2)}, u32[]{:S(2)}) collective-permute-start(s32[1024]{0:T(1024)S(1)} %copy-done.25), channel_id=1, source_target_pairs={{0,2},{1,3},{2,0},{3,1},{4,6},{5,7},{6,4},{7,5},{8,10},{9,11},{10,... | collective-permute-start | bytes 12296 | tf_op jit(solution)/shard_map/ppermute | solution.py:63
  27.3 44.2 %copy-start = (bf16[128,3584]{1,0:T(8,128)(2,1)}, bf16[128,3584]{1,0:T(8,128)(2,1)S(1)}, u32[]{:S(2)}) copy-start(bf16[128,3584]{1,0:T(8,128)(2,1)S(1)} %collective-permute-done.2.refs_6_.refs_4_.refs_3_) | copy-start | bytes 2752516
  27.3 20.5 %collective-permute-start.23 = (s32[1024]{0:T(1024)S(1)}, s32[1024]{0:T(1024)S(1)}, u32[]{:S(2)}, u32[]{:S(2)}) collective-permute-start(s32[1024]{0:T(1024)S(1)} %copy-done.25), channel_id=1, source_target_pairs={{0,3},{1,2},{2,1},{3,0},{4,7},{5,6},{6,5},{7,4},{8,11},{9,10},{10,... | collective-permute-start | bytes 12296 | tf_op jit(solution)/shard_map/ppermute | solution.py:63
  46.9 22.6 %collective-permute-start.20 = (bf16[896,512]{1,0:T(8,128)(2,1)}, bf16[896,512]{1,0:T(8,128)(2,1)S(1)}, u32[]{:S(2)}, u32[]{:S(2)}) collective-permute-start(bf16[896,512]{1,0:T(8,128)(2,1)} %get-tuple-element.34), channel_id=1, source_target_pairs={{0,3},{1,2},{2,1},{3,0},{4,7},{5,6},{6,5},{7,4},{8,11},{9,10},{10,... | collective-permute-start | bytes 2752520 | tf_op jit(solution)/shard_map/ppermute | solution.py:63
  47.8 23.7 %collective-permute-start.24 = (bf16[896,512]{1,0:T(8,128)(2,1)}, bf16[896,512]{1,0:T(8,128)(2,1)S(1)}, u32[]{:S(2)}, u32[]{:S(2)}) collective-permute-start(bf16[896,512]{1,0:T(8,128)(2,1)} %get-tuple-element.37), channel_id=1, source_target_pairs={{0,1},{1,0},{2,3},{3,2},{4,5},{5,4},{6,7},{7,6},{8,9},{9,8},{10,11... | collective-permute-start | bytes 2752520 | tf_op jit(solution)/shard_map/ppermute | solution.py:63
  48.7 40.7 %collective-permute-start.25 = (bf16[896,512]{1,0:T(8,128)(2,1)}, bf16[896,512]{1,0:T(8,128)(2,1)S(1)}, u32[]{:S(2)}, u32[]{:S(2)}) collective-permute-start(bf16[896,512]{1,0:T(8,128)(2,1)} %get-tuple-element.38), channel_id=1, source_target_pairs={{0,2},{1,3},{2,0},{3,1},{4,6},{5,7},{6,4},{7,5},{8,10},{9,11},{10,... | collective-permute-start | bytes 2752520 | tf_op jit(solution)/shard_map/ppermute | solution.py:63
  49.7 24.1 %collective-permute-start.4 = (bf16[128,3584]{1,0:T(8,128)(2,1)S(1)}, bf16[128,3584]{1,0:T(8,128)(2,1)S(1)}, u32[]{:S(2)}, u32[]{:S(2)}) collective-permute-start(bf16[128,3584]{1,0:T(8,128)(2,1)S(1)} %collective-permute-done.2.refs_6_.refs_4_.refs_3_), channel_id=1, source_target_pairs={{0,8},{4,12},{8,16},{12,20},{16,24},{20,28},{24,0},{28,4},{1,9},{5... | collective-permute-start | bytes 2752520 | tf_op jit(solution)/shard_map/ppermute | solution.py:68
  69.4 23.2 %collective-permute-start.3 = (bf16[128,3584]{1,0:T(8,128)(2,1)S(1)}, bf16[128,3584]{1,0:T(8,128)(2,1)S(1)}, u32[]{:S(2)}, u32[]{:S(2)}) collective-permute-start(bf16[128,3584]{1,0:T(8,128)(2,1)S(1)} %collective-permute-done.2.refs_6_.refs_4_.refs_3_), channel_id=1, source_target_pairs={{0,4},{4,0},{8,12},{12,8},{16,20},{20,16},{24,28},{28,24},{1,5},{5... | collective-permute-start | bytes 2752520 | tf_op jit(solution)/shard_map/ppermute | solution.py:63
  71.5 42.5 %copy-start.11 = (bf16[896,512]{1,0:T(8,128)(2,1)}, bf16[896,512]{1,0:T(8,128)(2,1)S(1)}, u32[]{:S(2)}) copy-start(bf16[896,512]{1,0:T(8,128)(2,1)S(1)} %collective-permute-done.24.refs_1_) | copy-start | bytes 2752516
  71.5 21.2 %collective-permute-start.6 = (bf16[128,3584]{1,0:T(8,128)(2,1)S(1)}, bf16[128,3584]{1,0:T(8,128)(2,1)S(1)}, u32[]{:S(2)}, u32[]{:S(2)}) collective-permute-start(bf16[128,3584]{1,0:T(8,128)(2,1)S(1)} %collective-permute-done.2.refs_6_.refs_4_.refs_3_), channel_id=1, source_target_pairs={{0,1},{1,0},{2,3},{3,2},{4,5},{5,4},{6,7},{7,6},{8,9},{9,8},{10,11... | collective-permute-start | bytes 2752520 | tf_op jit(solution)/shard_map/ppermute | solution.py:63
  73.8 44.9 %copy-start.1 = (bf16[128,3584]{1,0:T(8,128)(2,1)}, bf16[128,3584]{1,0:T(8,128)(2,1)S(1)}, u32[]{:S(2)}) copy-start(bf16[128,3584]{1,0:T(8,128)(2,1)S(1)} %collective-permute-done.4.refs_8_.refs_6_.refs_5_) | copy-start | bytes 2752516
  73.8 38.3 %collective-permute-start.5 = (bf16[128,3584]{1,0:T(8,128)(2,1)S(1)}, bf16[128,3584]{1,0:T(8,128)(2,1)}, u32[]{:S(2)}, u32[]{:S(2)}) collective-permute-start(bf16[128,3584]{1,0:T(8,128)(2,1)S(1)} %collective-permute-done.4.refs_8_.refs_6_.refs_5_), channel_id=1, source_target_pairs={{0,4},{4,0},{8,12},{12,8},{16,20},{20,16},{24,28},{28,24},{1,5},{5... | collective-permute-start | bytes 2752520 | tf_op jit(solution)/shard_map/ppermute | solution.py:63
  89.4 24.6 %copy-start.12 = (bf16[896,512]{1,0:T(8,128)(2,1)}, bf16[896,512]{1,0:T(8,128)(2,1)S(1)}, u32[]{:S(2)}) copy-start(bf16[896,512]{1,0:T(8,128)(2,1)S(1)} %collective-permute-done.25.refs_2_) | copy-start | bytes 2752516
  89.4 24.5 %collective-permute-start.10 = (bf16[128,3584]{1,0:T(8,128)(2,1)S(1)}, bf16[128,3584]{1,0:T(8,128)(2,1)}, u32[]{:S(2)}, u32[]{:S(2)}) collective-permute-start(bf16[128,3584]{1,0:T(8,128)(2,1)S(1)} %collective-permute-done.4.refs_8_.refs_6_.refs_5_), channel_id=1, source_target_pairs={{0,8},{4,12},{8,16},{12,20},{16,24},{20,28},{24,0},{28,4},{1,9},{5... | collective-permute-start | bytes 2752520 | tf_op jit(solution)/shard_map/ppermute | solution.py:68
  92.7 26.0 %copy-start.2 = (bf16[128,3584]{1,0:T(8,128)(2,1)}, bf16[128,3584]{1,0:T(8,128)(2,1)S(1)}, u32[]{:S(2)}) copy-start(bf16[128,3584]{1,0:T(8,128)(2,1)S(1)} %collective-permute-done.3.refs_7_.refs_5_.refs_4_) | copy-start | bytes 2752516
  92.7 35.9 %collective-permute-start.8 = (bf16[128,3584]{1,0:T(8,128)(2,1)S(1)}, bf16[128,3584]{1,0:T(8,128)(2,1)}, u32[]{:S(2)}, u32[]{:S(2)}) collective-permute-start(bf16[128,3584]{1,0:T(8,128)(2,1)S(1)} %collective-permute-done.4.refs_8_.refs_6_.refs_5_), channel_id=1, source_target_pairs={{0,1},{1,0},{2,3},{3,2},{4,5},{5,4},{6,7},{7,6},{8,9},{9,8},{10,11... | collective-permute-start | bytes 2752520 | tf_op jit(solution)/shard_map/ppermute | solution.py:63
  92.7 21.3 %copy-start.3 = (bf16[128,3584]{1,0:T(8,128)(2,1)}, bf16[128,3584]{1,0:T(8,128)(2,1)S(1)}, u32[]{:S(2)}) copy-start(bf16[128,3584]{1,0:T(8,128)(2,1)S(1)} %collective-permute-done.6.refs_10_.refs_8_.refs_7_) | copy-start | bytes 2752516
  92.7 36.5 %collective-permute-start.7 = (bf16[128,3584]{1,0:T(8,128)(2,1)S(1)}, bf16[128,3584]{1,0:T(8,128)(2,1)S(1)}, u32[]{:S(2)}, u32[]{:S(2)}) collective-permute-start(bf16[128,3584]{1,0:T(8,128)(2,1)S(1)} %collective-permute-done.3.refs_7_.refs_5_.refs_4_), channel_id=1, source_target_pairs={{0,1},{1,0},{2,3},{3,2},{4,5},{5,4},{6,7},{7,6},{8,9},{9,8},{10,11... | collective-permute-start | bytes 2752520 | tf_op jit(solution)/shard_map/ppermute | solution.py:63
  112.2 18.5 %collective-permute-start.9 = (bf16[128,3584]{1,0:T(8,128)(2,1)}, bf16[128,3584]{1,0:T(8,128)(2,1)}, u32[]{:S(2)}, u32[]{:S(2)}) collective-permute-start(bf16[128,3584]{1,0:T(8,128)(2,1)} %collective-permute-done.5.refs_9_.refs_7_.refs_6_), channel_id=1, source_target_pairs={{0,1},{1,0},{2,3},{3,2},{4,5},{5,4},{6,7},{7,6},{8,9},{9,8},{10,11... | collective-permute-start | bytes 2752520 | tf_op jit(solution)/shard_map/ppermute | solution.py:63
  113.9 23.9 %collective-permute-start.12 = (bf16[128,3584]{1,0:T(8,128)(2,1)}, bf16[128,3584]{1,0:T(8,128)(2,1)}, u32[]{:S(2)}, u32[]{:S(2)}) collective-permute-start(bf16[128,3584]{1,0:T(8,128)(2,1)} %collective-permute-done.10.refs_4_.refs_14_.refs_12_.refs_11_), channel_id=1, source_target_pairs={{0,8},{4,12},{8,16},{12,20},{16,24},{20,28},{24,0},{28,4},{1,9},{5... | collective-permute-start | bytes 2752520 | tf_op jit(solution)/shard_map/ppermute | solution.py:68
  127.9 29.3 %copy-start.26 = (f32[16]{0:T(128)}, f32[16]{0:T(128)S(1)}, u32[]{:S(2)}) copy-start(f32[16]{0:T(128)S(1)} %maximum_minimum_fusion) | copy-start | bytes 196
  128.6 28.6 %collective-permute-start.26 = (bf16[896,512]{1,0:T(8,128)(2,1)}, bf16[896,512]{1,0:T(8,128)(2,1)}, u32[]{:S(2)}, u32[]{:S(2)}) collective-permute-start(bf16[896,512]{1,0:T(8,128)(2,1)} %get-tuple-element.39), channel_id=1, source_target_pairs={{0,3},{1,2},{2,1},{3,0},{4,7},{5,6},{6,5},{7,4},{8,11},{9,10},{10,... | collective-permute-start | bytes 2752520 | tf_op jit(solution)/shard_map/ppermute | solution.py:63
  129.2 9.9 %copy-start.4 = (bf16[128,3584]{1,0:T(8,128)(2,1)}, bf16[128,3584]{1,0:T(8,128)(2,1)S(1)}, u32[]{:S(2)}) copy-start(bf16[128,3584]{1,0:T(8,128)(2,1)S(1)} %collective-permute-done.7.refs_11_.refs_9_.refs_8_) | copy-start | bytes 2752516
  129.2 28.6 %collective-permute-start.11 = (bf16[128,3584]{1,0:T(8,128)(2,1)}, bf16[128,3584]{1,0:T(8,128)(2,1)S(1)}, u32[]{:S(2)}, u32[]{:S(2)}) collective-permute-start(bf16[128,3584]{1,0:T(8,128)(2,1)} %collective-permute-done.10.refs_4_.refs_14_.refs_12_.refs_11_), channel_id=1, source_target_pairs={{0,4},{4,0},{8,12},{12,8},{16,20},{20,16},{24,28},{28,24},{1,5},{5... | collective-permute-start | bytes 2752520 | tf_op jit(solution)/shard_map/ppermute | solution.py:63
  130.7 28.7 %collective-permute-start.14 = (bf16[128,3584]{1,0:T(8,128)(2,1)}, bf16[128,3584]{1,0:T(8,128)(2,1)S(1)}, u32[]{:S(2)}, u32[]{:S(2)}) collective-permute-start(bf16[128,3584]{1,0:T(8,128)(2,1)} %collective-permute-done.10.refs_4_.refs_14_.refs_12_.refs_11_), channel_id=1, source_target_pairs={{0,1},{1,0},{2,3},{3,2},{4,5},{5,4},{6,7},{7,6},{8,9},{9,8},{10,11... | collective-permute-start | bytes 2752520 | tf_op jit(solution)/shard_map/ppermute | solution.py:63
  137.8 34.4 %collective-permute-start.13 = (bf16[128,3584]{1,0:T(8,128)(2,1)}, bf16[128,3584]{1,0:T(8,128)(2,1)}, u32[]{:S(2)}, u32[]{:S(2)}) collective-permute-start(bf16[128,3584]{1,0:T(8,128)(2,1)} %collective-permute-done.12.refs_6_.refs_16_.refs_14_.refs_13_), channel_id=1, source_target_pairs={{0,4},{4,0},{8,12},{12,8},{16,20},{20,16},{24,28},{28,24},{1,5},{5... | collective-permute-start | bytes 2752520 | tf_op jit(solution)/shard_map/ppermute | solution.py:63
  139.1 33.1 %collective-permute-start.16 = (bf16[128,3584]{1,0:T(8,128)(2,1)}, bf16[128,3584]{1,0:T(8,128)(2,1)}, u32[]{:S(2)}, u32[]{:S(2)}) collective-permute-start(bf16[128,3584]{1,0:T(8,128)(2,1)} %collective-permute-done.12.refs_6_.refs_16_.refs_14_.refs_13_), channel_id=1, source_target_pairs={{0,1},{1,0},{2,3},{3,2},{4,5},{5,4},{6,7},{7,6},{8,9},{9,8},{10,11... | collective-permute-start | bytes 2752520 | tf_op jit(solution)/shard_map/ppermute | solution.py:63
  157.2 55.7 %collective-permute-start.27 = (bf16[896,512]{1,0:T(8,128)(2,1)}, bf16[896,512]{1,0:T(8,128)(2,1)}, u32[]{:S(2)}, u32[]{:S(2)}) collective-permute-start(bf16[896,512]{1,0:T(8,128)(2,1)} %get-tuple-element.43), channel_id=1, source_target_pairs={{0,1},{1,0},{2,3},{3,2},{4,5},{5,4},{6,7},{7,6},{8,9},{9,8},{10,11... | collective-permute-start | bytes 2752520 | tf_op jit(solution)/shard_map/ppermute | solution.py:63
  157.8 33.1 %copy-start.5 = (bf16[128,3584]{1,0:T(8,128)(2,1)}, bf16[128,3584]{1,0:T(8,128)(2,1)S(1)}, u32[]{:S(2)}) copy-start(bf16[128,3584]{1,0:T(8,128)(2,1)S(1)} %collective-permute-done.11.refs_5_.refs_15_.refs_13_.refs_12_) | copy-start | bytes 2752516
  157.8 56.0 %collective-permute-start.28 = (bf16[896,512]{1,0:T(8,128)(2,1)}, bf16[896,512]{1,0:T(8,128)(2,1)}, u32[]{:S(2)}, u32[]{:S(2)}) collective-permute-start(bf16[896,512]{1,0:T(8,128)(2,1)} %get-tuple-element.44), channel_id=1, source_target_pairs={{0,2},{1,3},{2,0},{3,1},{4,6},{5,7},{6,4},{7,5},{8,10},{9,11},{10,... | collective-permute-start | bytes 2752520 | tf_op jit(solution)/shard_map/ppermute | solution.py:63
  159.4 31.5 %copy-start.6 = (bf16[128,3584]{1,0:T(8,128)(2,1)}, bf16[128,3584]{1,0:T(8,128)(2,1)S(1)}, u32[]{:S(2)}) copy-start(bf16[128,3584]{1,0:T(8,128)(2,1)S(1)} %collective-permute-done.14.refs_8_.refs_18_.refs_16_.refs_15_) | copy-start | bytes 2752516
  159.4 55.0 %collective-permute-start.29 = (bf16[896,512]{1,0:T(8,128)(2,1)}, bf16[896,512]{1,0:T(8,128)(2,1)}, u32[]{:S(2)}, u32[]{:S(2)}) collective-permute-start(bf16[896,512]{1,0:T(8,128)(2,1)} %get-tuple-element.45), channel_id=1, source_target_pairs={{0,3},{1,2},{2,1},{3,0},{4,7},{5,6},{6,5},{7,4},{8,11},{9,10},{10,... | collective-permute-start | bytes 2752520 | tf_op jit(solution)/shard_map/ppermute | solution.py:63
  172.2 18.7 %collective-permute-start.15 = (bf16[128,3584]{1,0:T(8,128)(2,1)S(1)}, bf16[128,3584]{1,0:T(8,128)(2,1)S(1)}, u32[]{:S(2)}, u32[]{:S(2)}) collective-permute-start(bf16[128,3584]{1,0:T(8,128)(2,1)S(1)} %collective-permute-done.11.refs_5_.refs_15_.refs_13_.refs_12_), channel_id=1, source_target_pairs={{0,1},{1,0},{2,3},{3,2},{4,5},{5,4},{6,7},{7,6},{8,9},{9,8},{10,11... | collective-permute-start | bytes 2752520 | tf_op jit(solution)/shard_map/ppermute | solution.py:63
  172.2 18.8 %collective-permute-start.17 = (bf16[128,3584]{1,0:T(8,128)(2,1)}, bf16[128,3584]{1,0:T(8,128)(2,1)}, u32[]{:S(2)}, u32[]{:S(2)}) collective-permute-start(bf16[128,3584]{1,0:T(8,128)(2,1)} %collective-permute-done.13.refs_7_.refs_17_.refs_15_.refs_14_), channel_id=1, source_target_pairs={{0,1},{1,0},{2,3},{3,2},{4,5},{5,4},{6,7},{7,6},{8,9},{9,8},{10,11... | collective-permute-start | bytes 2752520 | tf_op jit(solution)/shard_map/ppermute | solution.py:63
  190.9 47.7 %collective-permute-start.30 = (bf16[896,512]{1,0:T(8,128)(2,1)}, bf16[896,512]{1,0:T(8,128)(2,1)S(1)}, u32[]{:S(2)}, u32[]{:S(2)}) collective-permute-start(bf16[896,512]{1,0:T(8,128)(2,1)} %get-tuple-element.47), channel_id=1, source_target_pairs={{0,1},{1,0},{2,3},{3,2},{4,5},{5,4},{6,7},{7,6},{8,9},{9,8},{10,11... | collective-permute-start | bytes 2752520 | tf_op jit(solution)/shard_map/ppermute | solution.py:63
  191.0 63.2 %collective-permute-start.31 = (bf16[896,512]{1,0:T(8,128)(2,1)}, bf16[896,512]{1,0:T(8,128)(2,1)}, u32[]{:S(2)}, u32[]{:S(2)}) collective-permute-start(bf16[896,512]{1,0:T(8,128)(2,1)} %get-tuple-element.49), channel_id=1, source_target_pairs={{0,1},{1,0},{2,3},{3,2},{4,5},{5,4},{6,7},{7,6},{8,9},{9,8},{10,11... | collective-permute-start | bytes 2752520 | tf_op jit(solution)/shard_map/ppermute | solution.py:63
  213.0 41.2 %collective-permute-start.32 = (bf16[896,512]{1,0:T(8,128)(2,1)}, bf16[896,512]{1,0:T(8,128)(2,1)}, u32[]{:S(2)}, u32[]{:S(2)}) collective-permute-start(bf16[896,512]{1,0:T(8,128)(2,1)} %get-tuple-element.50), channel_id=1, source_target_pairs={{0,2},{1,3},{2,0},{3,1},{4,6},{5,7},{6,4},{7,5},{8,10},{9,11},{10,... | collective-permute-start | bytes 2752520 | tf_op jit(solution)/shard_map/ppermute | solution.py:63
  213.8 40.7 %collective-permute-start.33 = (bf16[896,512]{1,0:T(8,128)(2,1)}, bf16[896,512]{1,0:T(8,128)(2,1)}, u32[]{:S(2)}, u32[]{:S(2)}) collective-permute-start(bf16[896,512]{1,0:T(8,128)(2,1)} %get-tuple-element.51), channel_id=1, source_target_pairs={{0,3},{1,2},{2,1},{3,0},{4,7},{5,6},{6,5},{7,4},{8,11},{9,10},{10,... | collective-permute-start | bytes 2752520 | tf_op jit(solution)/shard_map/ppermute | solution.py:63
  214.4 65.0 %collective-permute-start.34 = (bf16[896,512]{1,0:T(8,128)(2,1)}, bf16[896,512]{1,0:T(8,128)(2,1)S(1)}, u32[]{:S(2)}, u32[]{:S(2)}) collective-permute-start(bf16[896,512]{1,0:T(8,128)(2,1)} %get-tuple-element.53), channel_id=1, source_target_pairs={{0,2},{1,3},{2,0},{3,1},{4,6},{5,7},{6,4},{7,5},{8,10},{9,11},{10,... | collective-permute-start | bytes 2752520 | tf_op jit(solution)/shard_map/ppermute | solution.py:63
  238.6 54.9 %collective-permute-start = (bf16[896,512]{1,0:T(8,128)(2,1)}, bf16[896,512]{1,0:T(8,128)(2,1)S(1)}, u32[]{:S(2)}, u32[]{:S(2)}) collective-permute-start(bf16[896,512]{1,0:T(8,128)(2,1)} %get-tuple-element.31), channel_id=1, source_target_pairs={{0,3},{1,2},{2,1},{3,0},{4,7},{5,6},{6,5},{7,4},{8,11},{9,10},{10,... | collective-permute-start | bytes 2752520 | tf_op jit(solution)/shard_map/ppermute | solution.py:63
  254.1 23.8 %copy-start.16 = (f32[3,32,128]{2,1,0:T(8,128)S(1)}, f32[3,32,128]{2,1,0:T(8,128)}, u32[]{:S(2)}) copy-start(f32[3,32,128]{2,1,0:T(8,128)} %chunk.9) | copy-start | bytes 147460
  254.1 23.8 %copy-start.17 = (f32[3,32,128]{2,1,0:T(8,128)S(1)}, f32[3,32,128]{2,1,0:T(8,128)}, u32[]{:S(2)}) copy-start(f32[3,32,128]{2,1,0:T(8,128)} %chunk.10) | copy-start | bytes 147460
  254.1 23.8 %copy-start.18 = (f32[3,32,128]{2,1,0:T(8,128)S(1)}, f32[3,32,128]{2,1,0:T(8,128)}, u32[]{:S(2)}) copy-start(f32[3,32,128]{2,1,0:T(8,128)} %chunk.11) | copy-start | bytes 147460
  254.2 23.8 %copy-start.19 = (f32[3,32,128]{2,1,0:T(8,128)S(1)}, f32[3,32,128]{2,1,0:T(8,128)}, u32[]{:S(2)}) copy-start(f32[3,32,128]{2,1,0:T(8,128)} %chunk.12) | copy-start | bytes 147460
  254.2 23.8 %copy-start.21 = (f32[3,32,128]{2,1,0:T(8,128)S(1)}, f32[3,32,128]{2,1,0:T(8,128)}, u32[]{:S(2)}) copy-start(f32[3,32,128]{2,1,0:T(8,128)} %chunk.13) | copy-start | bytes 147460
  292.1 15.6 %copy-start.23 = (f32[256]{0:T(256)S(1)}, f32[256]{0:T(256)}, u32[]{:S(2)}) copy-start(f32[256]{0:T(256)} %copy-done.22) | copy-start | bytes 3076
  305.4 2.3 collective-permute-start.35
  306.3 3.9 %collective-permute-start.36 = (f32[3,8,128]{2,1,0:T(8,128)}, f32[3,8,128]{2,1,0:T(8,128)S(1)}, u32[]{:S(2)}, u32[]{:S(2)}) collective-permute-start(f32[3,8,128]{2,1,0:T(8,128)} %get-tuple-element.56), channel_id=1, source_target_pairs={{0,2},{1,3},{2,0},{3,1},{4,6},{5,7},{6,4},{7,5},{8,10},{9,11},{10,... | collective-permute-start | bytes 36872 | tf_op jit(solution)/shard_map/ppermute | solution.py:63
  307.0 3.4 %collective-permute-start.37 = (f32[3,8,128]{2,1,0:T(8,128)}, f32[3,8,128]{2,1,0:T(8,128)S(1)}, u32[]{:S(2)}, u32[]{:S(2)}) collective-permute-start(f32[3,8,128]{2,1,0:T(8,128)} %get-tuple-element.57), channel_id=1, source_target_pairs={{0,3},{1,2},{2,1},{3,0},{4,7},{5,6},{6,5},{7,4},{8,11},{9,10},{10,... | collective-permute-start | bytes 36872 | tf_op jit(solution)/shard_map/ppermute | solution.py:63
  311.2 3.8 %collective-permute-start.38 = (f32[3,8,128]{2,1,0:T(8,128)S(1)}, f32[3,8,128]{2,1,0:T(8,128)S(1)}, u32[]{:S(2)}, u32[]{:S(2)}) collective-permute-start(f32[3,8,128]{2,1,0:T(8,128)S(1)} %pad_maximum_fusion.1), channel_id=1, source_target_pairs={{0,4},{4,0},{8,12},{12,8},{16,20},{20,16},{24,28},{28,24},{1,5},{5... | collective-permute-start | bytes 36872 | tf_op jit(solution)/shard_map/ppermute | solution.py:63
  315.0 4.8 %collective-permute-start.39 = (f32[3,8,128]{2,1,0:T(8,128)S(1)}, f32[3,8,128]{2,1,0:T(8,128)S(1)}, u32[]{:S(2)}, u32[]{:S(2)}) collective-permute-start(f32[3,8,128]{2,1,0:T(8,128)S(1)} %pad_maximum_fusion.2), channel_id=1, source_target_pairs={{0,8},{4,12},{8,0},{12,4},{16,24},{20,28},{24,16},{28,20},{1,9},{5... | collective-permute-start | bytes 36872 | tf_op jit(solution)/shard_map/ppermute | solution.py:63
  316.6 4.6 %collective-permute-start.40 = (f32[3,8,128]{2,1,0:T(8,128)S(1)}, f32[3,8,128]{2,1,0:T(8,128)S(1)}, u32[]{:S(2)}, u32[]{:S(2)}) collective-permute-start(f32[3,8,128]{2,1,0:T(8,128)S(1)} %pad_maximum_fusion.2), channel_id=1, source_target_pairs={{0,16},{4,20},{8,24},{12,28},{16,0},{20,4},{24,8},{28,12},{1,17},{... | collective-permute-start | bytes 36872 | tf_op jit(solution)/shard_map/ppermute | solution.py:63
  319.4 5.5 %collective-permute-start.41 = (f32[3,8,128]{2,1,0:T(8,128)S(1)}, f32[3,8,128]{2,1,0:T(8,128)S(1)}, u32[]{:S(2)}, u32[]{:S(2)}) collective-permute-start(f32[3,8,128]{2,1,0:T(8,128)S(1)} %pad_maximum_fusion.2), channel_id=1, source_target_pairs={{0,24},{4,28},{8,16},{12,20},{16,8},{20,12},{24,0},{28,4},{1,25},{... | collective-permute-start | bytes 36872 | tf_op jit(solution)/shard_map/ppermute | solution.py:63
  319.5 12.1 %copy-start.24 = (f32[256]{0:T(256)}, f32[256]{0:T(256)S(1)}, u32[]{:S(2)}) copy-start(f32[256]{0:T(256)S(1)} %div.75) | copy-start | bytes 3076
  325.5 4.7 %collective-permute-start.43 = (f32[1]{0:T(128)}, f32[1]{0:T(128)}, u32[]{:S(2)}, u32[]{:S(2)}) collective-permute-start(f32[1]{0:T(128)} %bitcast.31), channel_id=1, source_target_pairs={{0,2},{1,3},{2,0},{3,1},{4,6},{5,7},{6,4},{7,5},{8,10},{9,11},{10,... | collective-permute-start | bytes 20 | tf_op jit(solution)/shard_map/ppermute | solution.py:63
  326.6 3.5 %collective-permute-start.44 = (f32[1]{0:T(128)}, f32[1]{0:T(128)}, u32[]{:S(2)}, u32[]{:S(2)}) collective-permute-start(f32[1]{0:T(128)} %bitcast.31), channel_id=1, source_target_pairs={{0,3},{1,2},{2,1},{3,0},{4,7},{5,6},{6,5},{7,4},{8,11},{9,10},{10,... | collective-permute-start | bytes 20 | tf_op jit(solution)/shard_map/ppermute | solution.py:63
  326.6 2.3 collective-permute-start.42
  (10 other events, 23.6 us)

commit v4 on v3

--- a/solution.py
+++ b/solution.py
@@ -18,7 +18,6 @@
 LOWEST = -3.0e38
 WIDTH = 512
 ROWS = 256
-SLOTS = 3
 CUTS = 4
 EARLY = 2
 VMEM_LIMIT = 60 * 1024 * 1024
@@ -121,7 +120,7 @@
     before, before_sem = take(2) if cfg["partial"] else (None, None)
 
     step = pl.program_id(0)
-    steps = cfg["steps"]
+    steps, slots = cfg["steps"], cfg["slots"]
     me = me_ref[0]
     depth = pieces[-1].shape[0]
     width = weights.shape[1]
@@ -134,7 +133,7 @@
         strips += [(ref, row, high) for row in range(0, ref.shape[0], high)]
 
     def copies(which):
-        slot = which % SLOTS
+        slot = which % slots
         found = []
         reached = 0
         start = which * tall
@@ -161,7 +160,7 @@
         return made
 
     def before_copy(which):
-        slot = which % SLOTS
+        slot = which % slots
         return pltpu.make_async_copy(
             partial_ref.at[pl.ds(which * tall, tall), :], before.at[slot], before_sem.at[slot]
         )
@@ -208,7 +207,7 @@
     def _():
         for index in range(len(distances)):
             piece_copy(index).start()
-        for ahead in range(min(SLOTS - 1, steps)):
+        for ahead in range(min(slots - 1, steps)):
             for copy in copies(ahead):
                 copy.start()
         if second is not None:
@@ -224,14 +223,14 @@
 
         @pl.when(step == which)
         def _():
-            if which + SLOTS - 1 < steps:
-                for copy in copies(which + SLOTS - 1):
+            if which + slots - 1 < steps:
+                for copy in copies(which + slots - 1):
                     copy.start()
-            landed(held.at[which % SLOTS], token_sem.at[which % SLOTS])
+            landed(held.at[which % slots], token_sem.at[which % slots])
             if partial_ref is not None:
                 before_copy(which).wait()
 
-    slot = lax.rem(step, SLOTS)
+    slot = lax.rem(step, slots)
     if not cfg["finish"]:
         outs[0][0:ROWS, :] = product(slot, 0)
         outs[0][ROWS:tall, :] = product(slot, ROWS)
@@ -267,6 +266,7 @@
     finish = ids is not None
     tall = 2 * ROWS
     steps = count // tall
+    slots = 2 if partial is None else 3
     rows = count // LANES
     anywhere = pl.BlockSpec(memory_space=pl.ANY)
     whole = lambda shape: pl.BlockSpec(shape, lambda i, *_: (0,) * len(shape))
@@ -274,9 +274,9 @@
     in_specs = [anywhere] * len(operands)
     scratch = [
         pltpu.VMEM((inner, width), tokens[0].dtype),
-        pltpu.VMEM((SLOTS, tall, inner), tokens[0].dtype),
+        pltpu.VMEM((slots, tall, inner), tokens[0].dtype),
         pltpu.SemaphoreType.DMA((1,)),
-        pltpu.SemaphoreType.DMA((SLOTS,)),
+        pltpu.SemaphoreType.DMA((slots,)),
     ]
     if partial is not None:
         operands.append(partial)
@@ -299,7 +299,7 @@
         out_shape = [jax.ShapeDtypeStruct((count, width), jnp.float32)]
         out_specs = [pl.BlockSpec((tall, width), lambda i, *_: (i, 0))]
     if partial is not None:
-        scratch += [pltpu.VMEM((SLOTS, tall, width), jnp.float32), pltpu.SemaphoreType.DMA((SLOTS,))]
+        scratch += [pltpu.VMEM((slots, tall, width), jnp.float32), pltpu.SemaphoreType.DMA((slots,))]
     cfg = dict(
         distances=distances,
         offset=offset,
@@ -310,6 +310,7 @@
         prior=prior is not None,
         outs=len(out_shape),
         steps=steps,
+        slots=slots,
     )
     return pl.pallas_call(
         functools.partial(chunk_kernel, cfg),
@@ -372,10 +373,9 @@
     local = jnp.concatenate(ids_all) - (shard * columns + me * quarter)
     ids = local.astype(jnp.float32).reshape(-1, LANES)
 
-    cut = [
-        cut_blocks(mine, unembedding_table, prompts, chunk * WIDTH, WIDTH)
-        for chunk in range(chunks)
-    ]
+    cut = []
+    for chunk in range(chunks):
+        cut.append(cut_blocks(mine, unembedding_table, prompts, chunk * WIDTH, WIDTH))
     pieces = []
     for blocks in cut:
         sent = [swap(block, "prompt", d + 1) for d, block in enumerate(blocks)]
@@ -387,7 +387,9 @@
         remote += [ring[-1], swap(ring[-1], "vocab", 1)]
         if hop + 1 < vocabs // 2:
             ring.append(shift(ring[-1], "vocab", 2))
-    remote_pair = [swap(part, "prompt", 1) for part in remote]
+    remote_pair = []
+    for part in remote:
+        remote_pair.append(swap(part, "prompt", 1))
 
     rows = strip // LANES
     base = each // LANES
@@ -462,7 +464,7 @@
     size = lax.axis_size("vocab")
     base = 1
     while base < size:
-        radix = 2 if base == 1 else min(4, size // base)
+        radix = min(4, size // base)
         stats = merge(
             [stats] + [swap(stats, "vocab", base * digit) for digit in range(1, radix)]
         )

time: 334 us -> 332 us (level)
  no operation moved by 1% of the time
where the time goes in v4:
time: 332 us; the launch traced here: 330 us
  Pallas kernels  160 us (48%)
  waiting for transfers between devices  112 us (34%)
  starting transfers between devices  38.5 us (12%)
  other arithmetic  8.41 us (3%)
  local copies, waits for them, and re-layouts  6.11 us (2%)
  between operations  4.85 us (1%)
    pallas_call x9, Pallas kernels, chunk_call(): pl.pallas_call(functools.partial(chunk_kernel, cfg), grid_spec=pltpu.Pref...  139 us
    ppermute x42, waiting for transfers between devices, swap(): return lax.ppermute(value, axis, [(i, i ^ distance) for i in range(size)])  102 us
    ppermute x42, starting transfers between devices, swap(): return lax.ppermute(value, axis, [(i, i ^ distance) for i in range(size)])  35 us
    pallas_call x5, Pallas kernels, cut_blocks(): pl.pallas_call(cut_kernel, grid_spec=pltpu.PrefetchScalarGridSpec(num_sca...  20.8 us
    ppermute x3, waiting for transfers between devices, shift(): lax.ppermute(value, axis, [(i, (i + distance) % size) for i in range(size)])  10.6 us
  transfers between devices with their start and end apart: 45, of which 18 were waited for; matrix products, arithmetic and copies ran while one was open for 3% of the time, Pallas kernels for 45%

profile of v4, /device:TPU:0, one launch (start us, length us, event | category | flops | bytes accessed | tf_op | source)
XLA Modules:
  0.0 329.9 jit_solution(9994371328035000221)
XLA Ops:
  1.2 2.2 constant_dynamic-slice_fusion
  3.3 2.5 collective-permute-start.2
  5.9 4.2 %cut.6 = (bf16[896,512]{1,0:T(8,128)(2,1)}, bf16[896,512]{1,0:T(8,128)(2,1)}, bf16[896,512]{1,0:T(8,128)(2,1)}) custom-call(s32[1]{0:T(128)} %bitcast.me_ref, bf16[896,10240]{1,0:T(8,128)(2,1)} %refs_0_.23, bf16[896,10240]{1,0:T(8,128)(2,1)} %refs_0_.23, bf16[896,10240]{1,0:T(8,128)(2,1)} %refs_0_.23), custom_call_target="tpu_custom_call" | custom-call | flops 458752 | bytes 5505024 | tf_op jit(solution)/shard_map/cut/pallas_call | solution.py:91
  11.9 2.2 collective-permute-done.21
  14.0 2.8 collective-permute-start.22
  16.9 10.4 %collective-permute-done.2.refs_6_.refs_4_.refs_3_ = bf16[128,3584]{1,0:T(8,128)(2,1)S(1)} collective-permute-done((bf16[128,3584]{1,0:T(8,128)(2,1)}, bf16[128,3584]{1,0:T(8,128)(2,1)S(1)}, u32[]{:S(2)}, u32[]{:S(2)}) %collective-permute-start.2) | collective-permute-done | bytes 917536 | tf_op jit(solution)/shard_map/ppermute | solution.py:62
  27.3 0.8 collective-permute-start.23
  28.1 4.1 %cut.7 = (bf16[896,512]{1,0:T(8,128)(2,1)}, bf16[896,512]{1,0:T(8,128)(2,1)}, bf16[896,512]{1,0:T(8,128)(2,1)}) custom-call(s32[1]{0:T(128)} %bitcast.me_ref, bf16[896,10240]{1,0:T(8,128)(2,1)} %refs_0_.23, bf16[896,10240]{1,0:T(8,128)(2,1)} %refs_0_.23, bf16[896,10240]{1,0:T(8,128)(2,1)} %refs_0_.23), custom_call_target="tpu_custom_call" | custom-call | flops 458752 | bytes 5505024 | tf_op jit(solution)/shard_map/cut/pallas_call | solution.py:91
  32.2 14.6 %collective-permute-done.22 = s32[1024]{0:T(1024)S(1)} collective-permute-done((s32[1024]{0:T(1024)S(1)}, s32[1024]{0:T(1024)S(1)}, u32[]{:S(2)}, u32[]{:S(2)}) %collective-permute-start.22) | collective-permute-done | bytes 4128 | tf_op jit(solution)/shard_map/ppermute | solution.py:62
  46.8 0.9 collective-permute-start.20
  47.8 0.9 collective-permute-start.24
  49.0 0.7 copy-done.8
  49.7 1.6 collective-permute-start.4
  51.6 17.8 %collective-permute-done.20.refs_3_ = bf16[896,512]{1,0:T(8,128)(2,1)S(1)} collective-permute-done((bf16[896,512]{1,0:T(8,128)(2,1)}, bf16[896,512]{1,0:T(8,128)(2,1)S(1)}, u32[]{:S(2)}, u32[]{:S(2)}) %collective-permute-start.20) | collective-permute-done | bytes 917536 | tf_op jit(solution)/shard_map/ppermute | solution.py:62
  69.4 2.0 collective-permute-start.3
  71.5 2.3 collective-permute-done.4.refs_8_.refs_6_.refs_5_
  73.8 1.5 collective-permute-start.5
  75.3 14.0 %collective-permute-done.25.refs_2_ = bf16[896,512]{1,0:T(8,128)(2,1)S(1)} collective-permute-done((bf16[896,512]{1,0:T(8,128)(2,1)}, bf16[896,512]{1,0:T(8,128)(2,1)S(1)}, u32[]{:S(2)}, u32[]{:S(2)}) %collective-permute-start.25) | collective-permute-done | bytes 917536 | tf_op jit(solution)/shard_map/ppermute | solution.py:62
  89.4 1.8 collective-permute-start.10
  91.2 0.6 pad_add_fusion.3.place_ref
  93.2 19.0 %collective-permute-done.5.refs_9_.refs_7_.refs_6_ = bf16[128,3584]{1,0:T(8,128)(2,1)} collective-permute-done((bf16[128,3584]{1,0:T(8,128)(2,1)S(1)}, bf16[128,3584]{1,0:T(8,128)(2,1)}, u32[]{:S(2)}, u32[]{:S(2)}) %collective-permute-start.5) | collective-permute-done | bytes 917536 | tf_op jit(solution)/shard_map/ppermute | solution.py:62
  112.1 1.8 collective-permute-done.10.refs_4_.refs_14_.refs_12_.refs_11_
  114.0 0.7 pad_add_fusion.2.place_ref
  114.6 4.1 %cut.8 = (bf16[896,512]{1,0:T(8,128)(2,1)}, bf16[896,512]{1,0:T(8,128)(2,1)}, bf16[896,512]{1,0:T(8,128)(2,1)}) custom-call(s32[1]{0:T(128)} %bitcast.me_ref, bf16[896,10240]{1,0:T(8,128)(2,1)} %refs_0_.23, bf16[896,10240]{1,0:T(8,128)(2,1)} %refs_0_.23, bf16[896,10240]{1,0:T(8,128)(2,1)} %refs_0_.23), custom_call_target="tpu_custom_call" | custom-call | flops 458752 | bytes 5505024 | tf_op jit(solution)/shard_map/cut/pallas_call | solution.py:91
  118.7 4.2 %cut.5 = (bf16[896,512]{1,0:T(8,128)(2,1)}, bf16[896,512]{1,0:T(8,128)(2,1)}, bf16[896,512]{1,0:T(8,128)(2,1)}) custom-call(s32[1]{0:T(128)} %bitcast.me_ref, bf16[896,10240]{1,0:T(8,128)(2,1)} %refs_0_.23, bf16[896,10240]{1,0:T(8,128)(2,1)} %refs_0_.23, bf16[896,10240]{1,0:T(8,128)(2,1)} %refs_0_.23), custom_call_target="tpu_custom_call" | custom-call | flops 458752 | bytes 5505024 | tf_op jit(solution)/shard_map/cut/pallas_call | solution.py:91
  122.9 4.2 %cut.9 = (bf16[896,512]{1,0:T(8,128)(2,1)}, bf16[896,512]{1,0:T(8,128)(2,1)}, bf16[896,512]{1,0:T(8,128)(2,1)}) custom-call(s32[1]{0:T(128)} %bitcast.me_ref, bf16[896,10240]{1,0:T(8,128)(2,1)} %refs_0_.23, bf16[896,10240]{1,0:T(8,128)(2,1)} %refs_0_.23, bf16[896,10240]{1,0:T(8,128)(2,1)} %refs_0_.23), custom_call_target="tpu_custom_call" | custom-call | flops 458752 | bytes 5505024 | tf_op jit(solution)/shard_map/cut/pallas_call | solution.py:91
  128.0 0.6 fusion.7.refs_14_.refs_12_.refs_22_.refs_20_
  129.2 1.5 collective-permute-start.11
  131.2 6.5 %collective-permute-done.12.refs_6_.refs_16_.refs_14_.refs_13_ = bf16[128,3584]{1,0:T(8,128)(2,1)} collective-permute-done((bf16[128,3584]{1,0:T(8,128)(2,1)}, bf16[128,3584]{1,0:T(8,128)(2,1)}, u32[]{:S(2)}, u32[]{:S(2)}) %collective-permute-start.12) | collective-permute-done | bytes 917536 | tf_op jit(solution)/shard_map/ppermute | solution.py:67
  137.8 1.3 collective-permute-start.13
  139.1 18.2 %chunk.9 = f32[3,32,128]{2,1,0:T(8,128)} custom-call(s32[1]{0:T(128)} %bitcast.me_ref, s32[24]{0:T(128)} %pad_add_fusion.2.place_ref, bf16[896,10240]{1,0:T(8,128)(2,1)} %refs_0_.23, bf16[896,512]{1,0:T(8,128)(2,1)} %copy-done.8, bf16[896,512]{1,0:T(8,128)(2,1)} %copy-done.9, bf16[896,512]{1,0:T(8,128)(2,1)} %copy-done.10, bf16[1024,3584]{1,0:T(8,128)(2,1)} %refs_1_.13, ...), custom_call_target="tpu_custom_call" | custom-call | flops 11274289152 | bytes 25690112 | tf_op jit(solution)/shard_map/chunk/pallas_call | solution.py:315
  157.9 1.6 collective-permute-start.28
  159.5 12.8 %collective-permute-done.13.refs_7_.refs_17_.refs_15_.refs_14_ = bf16[128,3584]{1,0:T(8,128)(2,1)} collective-permute-done((bf16[128,3584]{1,0:T(8,128)(2,1)}, bf16[128,3584]{1,0:T(8,128)(2,1)}, u32[]{:S(2)}, u32[]{:S(2)}) %collective-permute-start.13) | collective-permute-done | bytes 917536 | tf_op jit(solution)/shard_map/ppermute | solution.py:62
  172.7 18.2 %chunk.10 = f32[3,32,128]{2,1,0:T(8,128)} custom-call(s32[1]{0:T(128)} %bitcast.me_ref, s32[24]{0:T(128)} %pad_add_fusion.2.place_ref, bf16[896,10240]{1,0:T(8,128)(2,1)} %refs_0_.23, bf16[896,512]{1,0:T(8,128)(2,1)} %copy-done.11, bf16[896,512]{1,0:T(8,128)(2,1)} %copy-done.12, bf16[896,512]{1,0:T(8,128)(2,1)} %collective-permute-done.26.refs_3_, ...), custom_call_target="tpu_custom_call" | custom-call | flops 11274289152 | bytes 25690112 | tf_op jit(solution)/shard_map/chunk/pallas_call | solution.py:315
  191.9 9.7 %chunk.11 = f32[3,32,128]{2,1,0:T(8,128)} custom-call(s32[1]{0:T(128)} %bitcast.me_ref, s32[8]{0:T(128)} %pad_add_fusion.3.place_ref, bf16[896,10240]{1,0:T(8,128)(2,1)} %refs_0_.23, bf16[896,512]{1,0:T(8,128)(2,1)} %copy-done.8, bf16[896,512]{1,0:T(8,128)(2,1)} %copy-done.9, bf16[896,512]{1,0:T(8,128)(2,1)} %copy-done.10, ...), custom_call_target="tpu_custom_call" | custom-call | flops 3758096384 | bytes 11010048 | tf_op jit(solution)/shard_map/chunk/pallas_call | solution.py:315
  201.6 9.7 %chunk.12 = f32[3,32,128]{2,1,0:T(8,128)} custom-call(s32[1]{0:T(128)} %bitcast.me_ref, s32[8]{0:T(128)} %pad_add_fusion.3.place_ref, bf16[896,10240]{1,0:T(8,128)(2,1)} %refs_0_.23, bf16[896,512]{1,0:T(8,128)(2,1)} %copy-done.11, bf16[896,512]{1,0:T(8,128)(2,1)} %copy-done.12, bf16[896,512]{1,0:T(8,128)(2,1)} %collective-permute-done.26.refs_3_, ...), custom_call_target="tpu_custom_call" | custom-call | flops 3758096384 | bytes 11010048 | tf_op jit(solution)/shard_map/chunk/pallas_call | solution.py:315
  211.4 0.8 collective-permute-start.32
  212.8 0.8 collective-permute-start.34
  213.6 22.4 %chunk.13 = f32[3,32,128]{2,1,0:T(8,128)} custom-call(s32[1]{0:T(128)} %bitcast.me_ref, s32[32]{0:T(128)} %concatenate.22.place_ref, bf16[896,10240]{1,0:T(8,128)(2,1)} %refs_0_.23, bf16[896,512]{1,0:T(8,128)(2,1)} %collective-permute-done.27.refs_1_, bf16[896,512]{1,0:T(8,128)(2,1)} %collective-permute-done.28.refs_2_, ...), custom_call_target="tpu_custom_call" | custom-call | flops 15032385536 | bytes 33030144 | tf_op jit(solution)/shard_map/chunk/pallas_call | solution.py:315
  236.0 1.4 collective-permute-start
  237.5 15.4 %chunk.14.refs_19_ = f32[4096,512]{1,0:T(8,128)} custom-call(s32[1]{0:T(128)} %bitcast.me_ref, s32[32]{0:T(128)} %concatenate.22.place_ref, bf16[896,10240]{1,0:T(8,128)(2,1)} %refs_0_.23, bf16[896,512]{1,0:T(8,128)(2,1)} %copy-done.15, bf16[1024,3584]{1,0:T(8,128)(2,1)} %refs_1_.13, bf16[1024,3584]{1,0:T(8,128)(2,1)} %collective-permute-done.1.refs_5_.refs_3_.refs_2_, ...), custom_call_target="tpu_custom_call" | custom-call | flops 7516192768 | bytes 16515072 | tf_op jit(solution)/shard_map/chunk/pallas_call | solution.py:315
  253.0 22.8 %chunk.15 = f32[3,32,128]{2,1,0:T(8,128)} custom-call(s32[1]{0:T(128)} %bitcast.me_ref, s32[32]{0:T(128)} %concatenate.22.place_ref, bf16[896,10240]{1,0:T(8,128)(2,1)} %refs_0_.23, bf16[896,512]{1,0:T(8,128)(2,1)} %collective-permute-done.31.refs_1_, bf16[896,512]{1,0:T(8,128)(2,1)} %collective-permute-done.32.refs_2_, ...), custom_call_target="tpu_custom_call" | custom-call | flops 15032385536 | bytes 33030144 | tf_op jit(solution)/shard_map/chunk/pallas_call | solution.py:315
  275.8 0.8 fusion.3
  276.6 0.6 pad_maximum_fusion.refs_21_
  277.3 1.0 copy-done.14
  278.2 11.7 %chunk.16.refs_19_ = f32[4096,512]{1,0:T(8,128)} custom-call(s32[1]{0:T(128)} %bitcast.me_ref, s32[32]{0:T(128)} %concatenate.22.place_ref, bf16[896,512]{1,0:T(8,128)(2,1)} %copy-done.14, bf16[1024,3584]{1,0:T(8,128)(2,1)} %refs_1_.13, bf16[1024,3584]{1,0:T(8,128)(2,1)} %collective-permute-done.1.refs_5_.refs_3_.refs_2_, bf16[128,3584]{1,0:T(8,128)(2,1)} %copy-done, ...), custom_call_target="tpu_custom_call" | custom-call | flops 3758096384 | bytes 8257536 | tf_op jit(solution)/shard_map/chunk/pallas_call | solution.py:315
  290.0 2.0 collective-permute-done.refs_0_
  291.9 1.0 copy-done.13
  293.0 10.9 %chunk.17 = (f32[3,8,128]{2,1,0:T(8,128)}, f32[3,8,128]{2,1,0:T(8,128)}, f32[3,8,128]{2,1,0:T(8,128)}, f32[3,8,128]{2,1,0:T(8,128)}) custom-call(s32[1]{0:T(128)} %bitcast.me_ref, s32[32]{0:T(128)} %concatenate.22.place_ref, bf16[896,512]{1,0:T(8,128)(2,1)} %copy-done.13, bf16[1024,3584]{1,0:T(8,128)(2,1)} %refs_1_.13, ...), custom_call_target="tpu_custom_call" | custom-call | flops 3758096384 | bytes 8257536 | tf_op jit(solution)/shard_map/chunk/pallas_call | solution.py:315
  303.8 0.9 collective-permute-start.35
  304.7 0.8 collective-permute-start.36
  305.5 0.7 collective-permute-start.37
  306.1 2.5 collective-permute-done.36
  308.9 0.7 add_add_fusion.1
  309.6 1.6 collective-permute-start.38
  311.2 1.6 collective-permute-start.39
  313.4 1.6 collective-permute-done.39
  314.9 2.4 collective-permute-done.40
  317.4 2.8 collective-permute-start.41
  320.6 1.5 collective-permute-done.41
  322.1 0.6 multiply_reduce_fusion
  322.7 1.0 collective-permute-start.43
  323.7 1.1 collective-permute-start.42
  324.8 1.3 fusion.13
  (157 shorter events, 10.4 us)
Async XLA Ops:
  0.6 138.5 %collective-permute-start.1 = (bf16[1024,3584]{1,0:T(8,128)(2,1)}, bf16[1024,3584]{1,0:T(8,128)(2,1)}, u32[]{:S(2)}, u32[]{:S(2)}) collective-permute-start(bf16[1024,3584]{1,0:T(8,128)(2,1)} %refs_1_.13), channel_id=1, source_target_pairs={{0,1},{1,0},{2,3},{3,2},{4,5},{5,4},{6,7},{7,6},{8,9},{9,8},{10,11... | collective-permute-start | bytes 22020104 | tf_op jit(solution)/shard_map/ppermute | solution.py:62
  3.3 23.9 %collective-permute-start.2 = (bf16[128,3584]{1,0:T(8,128)(2,1)}, bf16[128,3584]{1,0:T(8,128)(2,1)S(1)}, u32[]{:S(2)}, u32[]{:S(2)}) collective-permute-start(bf16[128,3584]{1,0:T(8,128)(2,1)} %constant_dynamic-slice_fusion), channel_id=1, source_target_pairs={{0,2},{1,3},{2,0},{3,1},{4,6},{5,7},{6,4},{7,5},{8,10},{9,11},{10,... | collective-permute-start | bytes 2752520 | tf_op jit(solution)/shard_map/ppermute | solution.py:62
  5.9 4.9 %copy-start.27 = (f32[16]{0:T(128)S(1)}, f32[16]{0:T(128)}, u32[]{:S(2)}) copy-start(f32[16]{0:T(128)} %param.11) | copy-start | bytes 196
  10.1 38.6 %collective-permute-start.18 = (bf16[896,512]{1,0:T(8,128)(2,1)}, bf16[896,512]{1,0:T(8,128)(2,1)S(1)}, u32[]{:S(2)}, u32[]{:S(2)}) collective-permute-start(bf16[896,512]{1,0:T(8,128)(2,1)} %get-tuple-element.32), channel_id=1, source_target_pairs={{0,1},{1,0},{2,3},{3,2},{4,5},{5,4},{6,7},{7,6},{8,9},{9,8},{10,11... | collective-permute-start | bytes 2752520 | tf_op jit(solution)/shard_map/ppermute | solution.py:62
  10.3 39.4 %collective-permute-start.19 = (bf16[896,512]{1,0:T(8,128)(2,1)}, bf16[896,512]{1,0:T(8,128)(2,1)S(1)}, u32[]{:S(2)}, u32[]{:S(2)}) collective-permute-start(bf16[896,512]{1,0:T(8,128)(2,1)} %get-tuple-element.33), channel_id=1, source_target_pairs={{0,2},{1,3},{2,0},{3,1},{4,6},{5,7},{6,4},{7,5},{8,10},{9,11},{10,... | collective-permute-start | bytes 2752520 | tf_op jit(solution)/shard_map/ppermute | solution.py:62
  10.6 3.4 %collective-permute-start.21 = (s32[1024]{0:T(1024)S(1)}, s32[1024]{0:T(1024)S(1)}, u32[]{:S(2)}, u32[]{:S(2)}) collective-permute-start(s32[1024]{0:T(1024)S(1)} %copy-done.25), channel_id=1, source_target_pairs={{0,1},{1,0},{2,3},{3,2},{4,5},{5,4},{6,7},{7,6},{8,9},{9,8},{10,11... | collective-permute-start | bytes 12296 | tf_op jit(solution)/shard_map/ppermute | solution.py:62
  10.8 40.8 %copy-start.22 = (f32[256]{0:T(256)}, f32[256]{0:T(256)S(1)}, u32[]{:S(2)}) copy-start(f32[256]{0:T(256)S(1)} %get-tuple-element.67) | copy-start | bytes 3076
  14.0 32.8 %collective-permute-start.22 = (s32[1024]{0:T(1024)S(1)}, s32[1024]{0:T(1024)S(1)}, u32[]{:S(2)}, u32[]{:S(2)}) collective-permute-start(s32[1024]{0:T(1024)S(1)} %copy-done.25), channel_id=1, source_target_pairs={{0,2},{1,3},{2,0},{3,1},{4,6},{5,7},{6,4},{7,5},{8,10},{9,11},{10,... | collective-permute-start | bytes 12296 | tf_op jit(solution)/shard_map/ppermute | solution.py:62
  27.3 44.2 %copy-start = (bf16[128,3584]{1,0:T(8,128)(2,1)}, bf16[128,3584]{1,0:T(8,128)(2,1)S(1)}, u32[]{:S(2)}) copy-start(bf16[128,3584]{1,0:T(8,128)(2,1)S(1)} %collective-permute-done.2.refs_6_.refs_4_.refs_3_) | copy-start | bytes 2752516
  27.3 20.5 %collective-permute-start.23 = (s32[1024]{0:T(1024)S(1)}, s32[1024]{0:T(1024)S(1)}, u32[]{:S(2)}, u32[]{:S(2)}) collective-permute-start(s32[1024]{0:T(1024)S(1)} %copy-done.25), channel_id=1, source_target_pairs={{0,3},{1,2},{2,1},{3,0},{4,7},{5,6},{6,5},{7,4},{8,11},{9,10},{10,... | collective-permute-start | bytes 12296 | tf_op jit(solution)/shard_map/ppermute | solution.py:62
  46.8 22.6 %collective-permute-start.20 = (bf16[896,512]{1,0:T(8,128)(2,1)}, bf16[896,512]{1,0:T(8,128)(2,1)S(1)}, u32[]{:S(2)}, u32[]{:S(2)}) collective-permute-start(bf16[896,512]{1,0:T(8,128)(2,1)} %get-tuple-element.34), channel_id=1, source_target_pairs={{0,3},{1,2},{2,1},{3,0},{4,7},{5,6},{6,5},{7,4},{8,11},{9,10},{10,... | collective-permute-start | bytes 2752520 | tf_op jit(solution)/shard_map/ppermute | solution.py:62
  47.8 23.7 %collective-permute-start.24 = (bf16[896,512]{1,0:T(8,128)(2,1)}, bf16[896,512]{1,0:T(8,128)(2,1)S(1)}, u32[]{:S(2)}, u32[]{:S(2)}) collective-permute-start(bf16[896,512]{1,0:T(8,128)(2,1)} %get-tuple-element.37), channel_id=1, source_target_pairs={{0,1},{1,0},{2,3},{3,2},{4,5},{5,4},{6,7},{7,6},{8,9},{9,8},{10,11... | collective-permute-start | bytes 2752520 | tf_op jit(solution)/shard_map/ppermute | solution.py:62
  48.7 40.7 %collective-permute-start.25 = (bf16[896,512]{1,0:T(8,128)(2,1)}, bf16[896,512]{1,0:T(8,128)(2,1)S(1)}, u32[]{:S(2)}, u32[]{:S(2)}) collective-permute-start(bf16[896,512]{1,0:T(8,128)(2,1)} %get-tuple-element.38), channel_id=1, source_target_pairs={{0,2},{1,3},{2,0},{3,1},{4,6},{5,7},{6,4},{7,5},{8,10},{9,11},{10,... | collective-permute-start | bytes 2752520 | tf_op jit(solution)/shard_map/ppermute | solution.py:62
  49.7 24.1 %collective-permute-start.4 = (bf16[128,3584]{1,0:T(8,128)(2,1)S(1)}, bf16[128,3584]{1,0:T(8,128)(2,1)S(1)}, u32[]{:S(2)}, u32[]{:S(2)}) collective-permute-start(bf16[128,3584]{1,0:T(8,128)(2,1)S(1)} %collective-permute-done.2.refs_6_.refs_4_.refs_3_), channel_id=1, source_target_pairs={{0,8},{4,12},{8,16},{12,20},{16,24},{20,28},{24,0},{28,4},{1,9},{5... | collective-permute-start | bytes 2752520 | tf_op jit(solution)/shard_map/ppermute | solution.py:67
  69.4 23.2 %collective-permute-start.3 = (bf16[128,3584]{1,0:T(8,128)(2,1)S(1)}, bf16[128,3584]{1,0:T(8,128)(2,1)S(1)}, u32[]{:S(2)}, u32[]{:S(2)}) collective-permute-start(bf16[128,3584]{1,0:T(8,128)(2,1)S(1)} %collective-permute-done.2.refs_6_.refs_4_.refs_3_), channel_id=1, source_target_pairs={{0,4},{4,0},{8,12},{12,8},{16,20},{20,16},{24,28},{28,24},{1,5},{5... | collective-permute-start | bytes 2752520 | tf_op jit(solution)/shard_map/ppermute | solution.py:62
  71.4 42.5 %copy-start.11 = (bf16[896,512]{1,0:T(8,128)(2,1)}, bf16[896,512]{1,0:T(8,128)(2,1)S(1)}, u32[]{:S(2)}) copy-start(bf16[896,512]{1,0:T(8,128)(2,1)S(1)} %collective-permute-done.24.refs_1_) | copy-start | bytes 2752516
  71.5 21.2 %collective-permute-start.6 = (bf16[128,3584]{1,0:T(8,128)(2,1)S(1)}, bf16[128,3584]{1,0:T(8,128)(2,1)S(1)}, u32[]{:S(2)}, u32[]{:S(2)}) collective-permute-start(bf16[128,3584]{1,0:T(8,128)(2,1)S(1)} %collective-permute-done.2.refs_6_.refs_4_.refs_3_), channel_id=1, source_target_pairs={{0,1},{1,0},{2,3},{3,2},{4,5},{5,4},{6,7},{7,6},{8,9},{9,8},{10,11... | collective-permute-start | bytes 2752520 | tf_op jit(solution)/shard_map/ppermute | solution.py:62
  73.8 44.9 %copy-start.1 = (bf16[128,3584]{1,0:T(8,128)(2,1)}, bf16[128,3584]{1,0:T(8,128)(2,1)S(1)}, u32[]{:S(2)}) copy-start(bf16[128,3584]{1,0:T(8,128)(2,1)S(1)} %collective-permute-done.4.refs_8_.refs_6_.refs_5_) | copy-start | bytes 2752516
  73.8 38.3 %collective-permute-start.5 = (bf16[128,3584]{1,0:T(8,128)(2,1)S(1)}, bf16[128,3584]{1,0:T(8,128)(2,1)}, u32[]{:S(2)}, u32[]{:S(2)}) collective-permute-start(bf16[128,3584]{1,0:T(8,128)(2,1)S(1)} %collective-permute-done.4.refs_8_.refs_6_.refs_5_), channel_id=1, source_target_pairs={{0,4},{4,0},{8,12},{12,8},{16,20},{20,16},{24,28},{28,24},{1,5},{5... | collective-permute-start | bytes 2752520 | tf_op jit(solution)/shard_map/ppermute | solution.py:62
  89.4 24.6 %copy-start.12 = (bf16[896,512]{1,0:T(8,128)(2,1)}, bf16[896,512]{1,0:T(8,128)(2,1)S(1)}, u32[]{:S(2)}) copy-start(bf16[896,512]{1,0:T(8,128)(2,1)S(1)} %collective-permute-done.25.refs_2_) | copy-start | bytes 2752516
  89.4 24.5 %collective-permute-start.10 = (bf16[128,3584]{1,0:T(8,128)(2,1)S(1)}, bf16[128,3584]{1,0:T(8,128)(2,1)}, u32[]{:S(2)}, u32[]{:S(2)}) collective-permute-start(bf16[128,3584]{1,0:T(8,128)(2,1)S(1)} %collective-permute-done.4.refs_8_.refs_6_.refs_5_), channel_id=1, source_target_pairs={{0,8},{4,12},{8,16},{12,20},{16,24},{20,28},{24,0},{28,4},{1,9},{5... | collective-permute-start | bytes 2752520 | tf_op jit(solution)/shard_map/ppermute | solution.py:67
  92.6 26.1 %copy-start.2 = (bf16[128,3584]{1,0:T(8,128)(2,1)}, bf16[128,3584]{1,0:T(8,128)(2,1)S(1)}, u32[]{:S(2)}) copy-start(bf16[128,3584]{1,0:T(8,128)(2,1)S(1)} %collective-permute-done.3.refs_7_.refs_5_.refs_4_) | copy-start | bytes 2752516
  92.6 36.0 %collective-permute-start.8 = (bf16[128,3584]{1,0:T(8,128)(2,1)S(1)}, bf16[128,3584]{1,0:T(8,128)(2,1)}, u32[]{:S(2)}, u32[]{:S(2)}) collective-permute-start(bf16[128,3584]{1,0:T(8,128)(2,1)S(1)} %collective-permute-done.4.refs_8_.refs_6_.refs_5_), channel_id=1, source_target_pairs={{0,1},{1,0},{2,3},{3,2},{4,5},{5,4},{6,7},{7,6},{8,9},{9,8},{10,11... | collective-permute-start | bytes 2752520 | tf_op jit(solution)/shard_map/ppermute | solution.py:62
  92.6 21.3 %copy-start.3 = (bf16[128,3584]{1,0:T(8,128)(2,1)}, bf16[128,3584]{1,0:T(8,128)(2,1)S(1)}, u32[]{:S(2)}) copy-start(bf16[128,3584]{1,0:T(8,128)(2,1)S(1)} %collective-permute-done.6.refs_10_.refs_8_.refs_7_) | copy-start | bytes 2752516
  92.7 36.5 %collective-permute-start.7 = (bf16[128,3584]{1,0:T(8,128)(2,1)S(1)}, bf16[128,3584]{1,0:T(8,128)(2,1)S(1)}, u32[]{:S(2)}, u32[]{:S(2)}) collective-permute-start(bf16[128,3584]{1,0:T(8,128)(2,1)S(1)} %collective-permute-done.3.refs_7_.refs_5_.refs_4_), channel_id=1, source_target_pairs={{0,1},{1,0},{2,3},{3,2},{4,5},{5,4},{6,7},{7,6},{8,9},{9,8},{10,11... | collective-permute-start | bytes 2752520 | tf_op jit(solution)/shard_map/ppermute | solution.py:62
  112.1 18.6 %collective-permute-start.9 = (bf16[128,3584]{1,0:T(8,128)(2,1)}, bf16[128,3584]{1,0:T(8,128)(2,1)}, u32[]{:S(2)}, u32[]{:S(2)}) collective-permute-start(bf16[128,3584]{1,0:T(8,128)(2,1)} %collective-permute-done.5.refs_9_.refs_7_.refs_6_), channel_id=1, source_target_pairs={{0,1},{1,0},{2,3},{3,2},{4,5},{5,4},{6,7},{7,6},{8,9},{9,8},{10,11... | collective-permute-start | bytes 2752520 | tf_op jit(solution)/shard_map/ppermute | solution.py:62
  113.9 23.9 %collective-permute-start.12 = (bf16[128,3584]{1,0:T(8,128)(2,1)}, bf16[128,3584]{1,0:T(8,128)(2,1)}, u32[]{:S(2)}, u32[]{:S(2)}) collective-permute-start(bf16[128,3584]{1,0:T(8,128)(2,1)} %collective-permute-done.10.refs_4_.refs_14_.refs_12_.refs_11_), channel_id=1, source_target_pairs={{0,8},{4,12},{8,16},{12,20},{16,24},{20,28},{24,0},{28,4},{1,9},{5... | collective-permute-start | bytes 2752520 | tf_op jit(solution)/shard_map/ppermute | solution.py:67
  127.9 29.4 %copy-start.26 = (f32[16]{0:T(128)}, f32[16]{0:T(128)S(1)}, u32[]{:S(2)}) copy-start(f32[16]{0:T(128)S(1)} %maximum_minimum_fusion) | copy-start | bytes 196
  128.6 28.7 %collective-permute-start.26 = (bf16[896,512]{1,0:T(8,128)(2,1)}, bf16[896,512]{1,0:T(8,128)(2,1)}, u32[]{:S(2)}, u32[]{:S(2)}) collective-permute-start(bf16[896,512]{1,0:T(8,128)(2,1)} %get-tuple-element.39), channel_id=1, source_target_pairs={{0,3},{1,2},{2,1},{3,0},{4,7},{5,6},{6,5},{7,4},{8,11},{9,10},{10,... | collective-permute-start | bytes 2752520 | tf_op jit(solution)/shard_map/ppermute | solution.py:62
  129.2 9.9 %copy-start.4 = (bf16[128,3584]{1,0:T(8,128)(2,1)}, bf16[128,3584]{1,0:T(8,128)(2,1)S(1)}, u32[]{:S(2)}) copy-start(bf16[128,3584]{1,0:T(8,128)(2,1)S(1)} %collective-permute-done.7.refs_11_.refs_9_.refs_8_) | copy-start | bytes 2752516
  129.2 28.7 %collective-permute-start.11 = (bf16[128,3584]{1,0:T(8,128)(2,1)}, bf16[128,3584]{1,0:T(8,128)(2,1)S(1)}, u32[]{:S(2)}, u32[]{:S(2)}) collective-permute-start(bf16[128,3584]{1,0:T(8,128)(2,1)} %collective-permute-done.10.refs_4_.refs_14_.refs_12_.refs_11_), channel_id=1, source_target_pairs={{0,4},{4,0},{8,12},{12,8},{16,20},{20,16},{24,28},{28,24},{1,5},{5... | collective-permute-start | bytes 2752520 | tf_op jit(solution)/shard_map/ppermute | solution.py:62
  130.7 28.7 %collective-permute-start.14 = (bf16[128,3584]{1,0:T(8,128)(2,1)}, bf16[128,3584]{1,0:T(8,128)(2,1)S(1)}, u32[]{:S(2)}, u32[]{:S(2)}) collective-permute-start(bf16[128,3584]{1,0:T(8,128)(2,1)} %collective-permute-done.10.refs_4_.refs_14_.refs_12_.refs_11_), channel_id=1, source_target_pairs={{0,1},{1,0},{2,3},{3,2},{4,5},{5,4},{6,7},{7,6},{8,9},{9,8},{10,11... | collective-permute-start | bytes 2752520 | tf_op jit(solution)/shard_map/ppermute | solution.py:62
  137.8 34.5 %collective-permute-start.13 = (bf16[128,3584]{1,0:T(8,128)(2,1)}, bf16[128,3584]{1,0:T(8,128)(2,1)}, u32[]{:S(2)}, u32[]{:S(2)}) collective-permute-start(bf16[128,3584]{1,0:T(8,128)(2,1)} %collective-permute-done.12.refs_6_.refs_16_.refs_14_.refs_13_), channel_id=1, source_target_pairs={{0,4},{4,0},{8,12},{12,8},{16,20},{20,16},{24,28},{28,24},{1,5},{5... | collective-permute-start | bytes 2752520 | tf_op jit(solution)/shard_map/ppermute | solution.py:62
  139.1 33.2 %collective-permute-start.16 = (bf16[128,3584]{1,0:T(8,128)(2,1)}, bf16[128,3584]{1,0:T(8,128)(2,1)}, u32[]{:S(2)}, u32[]{:S(2)}) collective-permute-start(bf16[128,3584]{1,0:T(8,128)(2,1)} %collective-permute-done.12.refs_6_.refs_16_.refs_14_.refs_13_), channel_id=1, source_target_pairs={{0,1},{1,0},{2,3},{3,2},{4,5},{5,4},{6,7},{7,6},{8,9},{9,8},{10,11... | collective-permute-start | bytes 2752520 | tf_op jit(solution)/shard_map/ppermute | solution.py:62
  157.3 54.1 %collective-permute-start.27 = (bf16[896,512]{1,0:T(8,128)(2,1)}, bf16[896,512]{1,0:T(8,128)(2,1)}, u32[]{:S(2)}, u32[]{:S(2)}) collective-permute-start(bf16[896,512]{1,0:T(8,128)(2,1)} %get-tuple-element.43), channel_id=1, source_target_pairs={{0,1},{1,0},{2,3},{3,2},{4,5},{5,4},{6,7},{7,6},{8,9},{9,8},{10,11... | collective-permute-start | bytes 2752520 | tf_op jit(solution)/shard_map/ppermute | solution.py:62
  157.9 33.1 %copy-start.5 = (bf16[128,3584]{1,0:T(8,128)(2,1)}, bf16[128,3584]{1,0:T(8,128)(2,1)S(1)}, u32[]{:S(2)}) copy-start(bf16[128,3584]{1,0:T(8,128)(2,1)S(1)} %collective-permute-done.11.refs_5_.refs_15_.refs_13_.refs_12_) | copy-start | bytes 2752516
  157.9 54.3 %collective-permute-start.28 = (bf16[896,512]{1,0:T(8,128)(2,1)}, bf16[896,512]{1,0:T(8,128)(2,1)}, u32[]{:S(2)}, u32[]{:S(2)}) collective-permute-start(bf16[896,512]{1,0:T(8,128)(2,1)} %get-tuple-element.44), channel_id=1, source_target_pairs={{0,2},{1,3},{2,0},{3,1},{4,6},{5,7},{6,4},{7,5},{8,10},{9,11},{10,... | collective-permute-start | bytes 2752520 | tf_op jit(solution)/shard_map/ppermute | solution.py:62
  159.5 31.5 %copy-start.6 = (bf16[128,3584]{1,0:T(8,128)(2,1)}, bf16[128,3584]{1,0:T(8,128)(2,1)S(1)}, u32[]{:S(2)}) copy-start(bf16[128,3584]{1,0:T(8,128)(2,1)S(1)} %collective-permute-done.14.refs_8_.refs_18_.refs_16_.refs_15_) | copy-start | bytes 2752516
  159.5 53.4 %collective-permute-start.29 = (bf16[896,512]{1,0:T(8,128)(2,1)}, bf16[896,512]{1,0:T(8,128)(2,1)}, u32[]{:S(2)}, u32[]{:S(2)}) collective-permute-start(bf16[896,512]{1,0:T(8,128)(2,1)} %get-tuple-element.45), channel_id=1, source_target_pairs={{0,3},{1,2},{2,1},{3,0},{4,7},{5,6},{6,5},{7,4},{8,11},{9,10},{10,... | collective-permute-start | bytes 2752520 | tf_op jit(solution)/shard_map/ppermute | solution.py:62
  172.2 18.7 %collective-permute-start.15 = (bf16[128,3584]{1,0:T(8,128)(2,1)S(1)}, bf16[128,3584]{1,0:T(8,128)(2,1)S(1)}, u32[]{:S(2)}, u32[]{:S(2)}) collective-permute-start(bf16[128,3584]{1,0:T(8,128)(2,1)S(1)} %collective-permute-done.11.refs_5_.refs_15_.refs_13_.refs_12_), channel_id=1, source_target_pairs={{0,1},{1,0},{2,3},{3,2},{4,5},{5,4},{6,7},{7,6},{8,9},{9,8},{10,11... | collective-permute-start | bytes 2752520 | tf_op jit(solution)/shard_map/ppermute | solution.py:62
  172.2 18.8 %collective-permute-start.17 = (bf16[128,3584]{1,0:T(8,128)(2,1)}, bf16[128,3584]{1,0:T(8,128)(2,1)}, u32[]{:S(2)}, u32[]{:S(2)}) collective-permute-start(bf16[128,3584]{1,0:T(8,128)(2,1)} %collective-permute-done.13.refs_7_.refs_17_.refs_15_.refs_14_), channel_id=1, source_target_pairs={{0,1},{1,0},{2,3},{3,2},{4,5},{5,4},{6,7},{7,6},{8,9},{9,8},{10,11... | collective-permute-start | bytes 2752520 | tf_op jit(solution)/shard_map/ppermute | solution.py:62
  191.0 45.0 %collective-permute-start.30 = (bf16[896,512]{1,0:T(8,128)(2,1)}, bf16[896,512]{1,0:T(8,128)(2,1)S(1)}, u32[]{:S(2)}, u32[]{:S(2)}) collective-permute-start(bf16[896,512]{1,0:T(8,128)(2,1)} %get-tuple-element.47), channel_id=1, source_target_pairs={{0,1},{1,0},{2,3},{3,2},{4,5},{5,4},{6,7},{7,6},{8,9},{9,8},{10,11... | collective-permute-start | bytes 2752520 | tf_op jit(solution)/shard_map/ppermute | solution.py:62
  191.1 61.9 %collective-permute-start.31 = (bf16[896,512]{1,0:T(8,128)(2,1)}, bf16[896,512]{1,0:T(8,128)(2,1)}, u32[]{:S(2)}, u32[]{:S(2)}) collective-permute-start(bf16[896,512]{1,0:T(8,128)(2,1)} %get-tuple-element.49), channel_id=1, source_target_pairs={{0,1},{1,0},{2,3},{3,2},{4,5},{5,4},{6,7},{7,6},{8,9},{9,8},{10,11... | collective-permute-start | bytes 2752520 | tf_op jit(solution)/shard_map/ppermute | solution.py:62
  211.4 41.6 %collective-permute-start.32 = (bf16[896,512]{1,0:T(8,128)(2,1)}, bf16[896,512]{1,0:T(8,128)(2,1)}, u32[]{:S(2)}, u32[]{:S(2)}) collective-permute-start(bf16[896,512]{1,0:T(8,128)(2,1)} %get-tuple-element.50), channel_id=1, source_target_pairs={{0,2},{1,3},{2,0},{3,1},{4,6},{5,7},{6,4},{7,5},{8,10},{9,11},{10,... | collective-permute-start | bytes 2752520 | tf_op jit(solution)/shard_map/ppermute | solution.py:62
  212.2 40.8 %collective-permute-start.33 = (bf16[896,512]{1,0:T(8,128)(2,1)}, bf16[896,512]{1,0:T(8,128)(2,1)}, u32[]{:S(2)}, u32[]{:S(2)}) collective-permute-start(bf16[896,512]{1,0:T(8,128)(2,1)} %get-tuple-element.51), channel_id=1, source_target_pairs={{0,3},{1,2},{2,1},{3,0},{4,7},{5,6},{6,5},{7,4},{8,11},{9,10},{10,... | collective-permute-start | bytes 2752520 | tf_op jit(solution)/shard_map/ppermute | solution.py:62
  212.8 64.4 %collective-permute-start.34 = (bf16[896,512]{1,0:T(8,128)(2,1)}, bf16[896,512]{1,0:T(8,128)(2,1)S(1)}, u32[]{:S(2)}, u32[]{:S(2)}) collective-permute-start(bf16[896,512]{1,0:T(8,128)(2,1)} %get-tuple-element.53), channel_id=1, source_target_pairs={{0,2},{1,3},{2,0},{3,1},{4,6},{5,7},{6,4},{7,5},{8,10},{9,11},{10,... | collective-permute-start | bytes 2752520 | tf_op jit(solution)/shard_map/ppermute | solution.py:62
  236.0 55.9 %collective-permute-start = (bf16[896,512]{1,0:T(8,128)(2,1)}, bf16[896,512]{1,0:T(8,128)(2,1)S(1)}, u32[]{:S(2)}, u32[]{:S(2)}) collective-permute-start(bf16[896,512]{1,0:T(8,128)(2,1)} %get-tuple-element.31), channel_id=1, source_target_pairs={{0,3},{1,2},{2,1},{3,0},{4,7},{5,6},{6,5},{7,4},{8,11},{9,10},{10,... | collective-permute-start | bytes 2752520 | tf_op jit(solution)/shard_map/ppermute | solution.py:62
  252.9 22.9 %copy-start.16 = (f32[3,32,128]{2,1,0:T(8,128)S(1)}, f32[3,32,128]{2,1,0:T(8,128)}, u32[]{:S(2)}) copy-start(f32[3,32,128]{2,1,0:T(8,128)} %chunk.9) | copy-start | bytes 147460
  252.9 22.9 %copy-start.17 = (f32[3,32,128]{2,1,0:T(8,128)S(1)}, f32[3,32,128]{2,1,0:T(8,128)}, u32[]{:S(2)}) copy-start(f32[3,32,128]{2,1,0:T(8,128)} %chunk.10) | copy-start | bytes 147460
  252.9 22.9 %copy-start.18 = (f32[3,32,128]{2,1,0:T(8,128)S(1)}, f32[3,32,128]{2,1,0:T(8,128)}, u32[]{:S(2)}) copy-start(f32[3,32,128]{2,1,0:T(8,128)} %chunk.11) | copy-start | bytes 147460
  252.9 22.9 %copy-start.19 = (f32[3,32,128]{2,1,0:T(8,128)S(1)}, f32[3,32,128]{2,1,0:T(8,128)}, u32[]{:S(2)}) copy-start(f32[3,32,128]{2,1,0:T(8,128)} %chunk.12) | copy-start | bytes 147460
  252.9 22.9 %copy-start.21 = (f32[3,32,128]{2,1,0:T(8,128)S(1)}, f32[3,32,128]{2,1,0:T(8,128)}, u32[]{:S(2)}) copy-start(f32[3,32,128]{2,1,0:T(8,128)} %chunk.13) | copy-start | bytes 147460
  290.0 16.2 %copy-start.23 = (f32[256]{0:T(256)S(1)}, f32[256]{0:T(256)}, u32[]{:S(2)}) copy-start(f32[256]{0:T(256)} %copy-done.22) | copy-start | bytes 3076
  303.8 2.3 collective-permute-start.35
  304.7 3.9 %collective-permute-start.36 = (f32[3,8,128]{2,1,0:T(8,128)}, f32[3,8,128]{2,1,0:T(8,128)S(1)}, u32[]{:S(2)}, u32[]{:S(2)}) collective-permute-start(f32[3,8,128]{2,1,0:T(8,128)} %get-tuple-element.56), channel_id=1, source_target_pairs={{0,2},{1,3},{2,0},{3,1},{4,6},{5,7},{6,4},{7,5},{8,10},{9,11},{10,... | collective-permute-start | bytes 36872 | tf_op jit(solution)/shard_map/ppermute | solution.py:62
  305.5 3.4 %collective-permute-start.37 = (f32[3,8,128]{2,1,0:T(8,128)}, f32[3,8,128]{2,1,0:T(8,128)S(1)}, u32[]{:S(2)}, u32[]{:S(2)}) collective-permute-start(f32[3,8,128]{2,1,0:T(8,128)} %get-tuple-element.57), channel_id=1, source_target_pairs={{0,3},{1,2},{2,1},{3,0},{4,7},{5,6},{6,5},{7,4},{8,11},{9,10},{10,... | collective-permute-start | bytes 36872 | tf_op jit(solution)/shard_map/ppermute | solution.py:62
  309.6 3.8 %collective-permute-start.38 = (f32[3,8,128]{2,1,0:T(8,128)S(1)}, f32[3,8,128]{2,1,0:T(8,128)S(1)}, u32[]{:S(2)}, u32[]{:S(2)}) collective-permute-start(f32[3,8,128]{2,1,0:T(8,128)S(1)} %pad_maximum_fusion.1), channel_id=1, source_target_pairs={{0,4},{4,0},{8,12},{12,8},{16,20},{20,16},{24,28},{28,24},{1,5},{5... | collective-permute-start | bytes 36872 | tf_op jit(solution)/shard_map/ppermute | solution.py:62
  311.2 3.7 %collective-permute-start.39 = (f32[3,8,128]{2,1,0:T(8,128)S(1)}, f32[3,8,128]{2,1,0:T(8,128)S(1)}, u32[]{:S(2)}, u32[]{:S(2)}) collective-permute-start(f32[3,8,128]{2,1,0:T(8,128)S(1)} %pad_maximum_fusion.1), channel_id=1, source_target_pairs={{0,8},{4,12},{8,0},{12,4},{16,24},{20,28},{24,16},{28,20},{1,9},{5... | collective-permute-start | bytes 36872 | tf_op jit(solution)/shard_map/ppermute | solution.py:62
  312.8 4.6 %collective-permute-start.40 = (f32[3,8,128]{2,1,0:T(8,128)S(1)}, f32[3,8,128]{2,1,0:T(8,128)S(1)}, u32[]{:S(2)}, u32[]{:S(2)}) collective-permute-start(f32[3,8,128]{2,1,0:T(8,128)S(1)} %pad_maximum_fusion.1), channel_id=1, source_target_pairs={{0,12},{4,8},{8,4},{12,0},{16,28},{20,24},{24,20},{28,16},{1,13},{... | collective-permute-start | bytes 36872 | tf_op jit(solution)/shard_map/ppermute | solution.py:62
  317.4 4.7 %collective-permute-start.41 = (f32[3,8,128]{2,1,0:T(8,128)S(1)}, f32[3,8,128]{2,1,0:T(8,128)S(1)}, u32[]{:S(2)}, u32[]{:S(2)}) collective-permute-start(f32[3,8,128]{2,1,0:T(8,128)S(1)} %pad_maximum_fusion.2), channel_id=1, source_target_pairs={{0,16},{4,20},{8,24},{12,28},{16,0},{20,4},{24,8},{28,12},{1,17},{... | collective-permute-start | bytes 36872 | tf_op jit(solution)/shard_map/ppermute | solution.py:62
  320.3 8.4 %copy-start.24 = (f32[256]{0:T(256)}, f32[256]{0:T(256)S(1)}, u32[]{:S(2)}) copy-start(f32[256]{0:T(256)S(1)} %div.75) | copy-start | bytes 3076
  322.7 4.8 %collective-permute-start.43 = (f32[1]{0:T(128)}, f32[1]{0:T(128)}, u32[]{:S(2)}, u32[]{:S(2)}) collective-permute-start(f32[1]{0:T(128)} %bitcast.31), channel_id=1, source_target_pairs={{0,2},{1,3},{2,0},{3,1},{4,6},{5,7},{6,4},{7,5},{8,10},{9,11},{10,... | collective-permute-start | bytes 20 | tf_op jit(solution)/shard_map/ppermute | solution.py:62
  323.7 3.8 %collective-permute-start.44 = (f32[1]{0:T(128)}, f32[1]{0:T(128)}, u32[]{:S(2)}, u32[]{:S(2)}) collective-permute-start(f32[1]{0:T(128)} %bitcast.31), channel_id=1, source_target_pairs={{0,3},{1,2},{2,1},{3,0},{4,7},{5,6},{6,5},{7,4},{8,11},{9,10},{10,... | collective-permute-start | bytes 20 | tf_op jit(solution)/shard_map/ppermute | solution.py:62
  323.7 2.4 collective-permute-start.42
  (10 other events, 23.5 us)
